TPU v7x, 8 devices: a whole 2x2x1 slice. The times are simulated.
8 devices in a mesh: data: 1 (over z), seq: 8 (over y, x, core).
Axes of the slice: x: 2, y: 2, z: 1, core: 2. Of those that a mesh axis runs over, the one named last changes fastest.
Arguments:
- x: bfloat16 [4096, 4096], P(('data', 'seq'))
- g: float32 [4096], replicated
- wqkv: bfloat16 [4096, 3, 16, 256], replicated
- wo: bfloat16 [16, 256, 4096], replicated
Outputs:
- output: bfloat16 [4096, 4096], P(('data', 'seq'))
All inputs are finite; a program needn't handle non-finite values.
Results may differ from a plain program's by a relative error of at most 0.00306945.
Values are sent between devices in bfloat16 or wider.
A program may use at most 1 GiB of HBM per device.

v0:
```python
import functools

import jax
import jax.numpy as jnp
from jax import lax
from jax.experimental import pallas as pl
from jax.experimental.pallas import tpu as pltpu
from jax.sharding import PartitionSpec as P


BF = jnp.bfloat16
F32 = jnp.float32
VMEM_LIMIT = 62 << 20
COST = 0.05
GROUPS = ((2, 4), (6, 0))
ME, B_TILE, B_PART, OWN_TILE, OWN_PART, SRC, DEV = 0, 1, 2, 3, 4, 5, 13


def _norm(x_ref, g_ref, xn, base):
    rb = 16

    def body(i, c):
        r = pl.ds(pl.multiple_of(i * rb, rb), rb)
        xf = x_ref[r, :].astype(F32)
        ms = jnp.mean(xf * xf, axis=-1, keepdims=True)
        xn[pl.ds(pl.multiple_of(base + i * rb, rb), rb), :] = (xf * lax.rsqrt(ms + 1e-5) * g_ref[...]).astype(BF)
        return c

    lax.fori_loop(0, x_ref.shape[0] // rb, body, 0, unroll=2)


def _norm_rows(x_ref, g_ref, o_ref):
    _norm(x_ref, g_ref, o_ref, 0)


def _emit_heads(acc, cos, sin, is_v, outs):
    @pl.when(is_v)
    def _():
        for j, o in enumerate(outs):
            o[...] = acc[:, j * 256:(j + 1) * 256].astype(BF)

    @pl.when(jnp.logical_not(is_v))
    def _():
        cs, sn = cos[...], sin[...]
        for j, o in enumerate(outs):
            x1, x2 = acc[:, j * 256:j * 256 + 128], acc[:, j * 256 + 128:(j + 1) * 256]
            o[:, :128] = (x1 * cs - x2 * sn).astype(BF)
            o[:, 128:] = (x2 * cs + x1 * sn).astype(BF)


def _lay(w_ref, wt, at):
    bd, n = w_ref.shape[0], wt.shape[1]
    for p in range(8 * 256 // n):
        @pl.when(at == p)
        def _():
            wt[...] = w_ref[:, 0].reshape(bd, 8 * 256)[:, p * n:(p + 1) * n]


def _qkv_first(ids, x_ref, g_ref, w_ref, cos_ref, sin_ref, s_ref, c_ref, wr_ref, xn, acc):
    c, d = pl.program_id(0), pl.program_id(1)
    bd = w_ref.shape[0]

    @pl.when((c == 0) & (d == 0))
    def _():
        _norm(x_ref, g_ref, xn, 0)

    @pl.when(d == 0)
    def _():
        acc[...] = jnp.zeros_like(acc)

    _lay(w_ref, wr_ref.at[0], ids[B_PART])
    xb = xn[:, pl.ds(pl.multiple_of(d * bd, bd), bd)]
    acc[...] += jnp.dot(xb, wr_ref[0], preferred_element_type=F32)

    @pl.when(d == pl.num_programs(1) - 1)
    def _():
        k = ids[ME] % 2
        for o, kk in ((s_ref, k), (c_ref, 1 - k)):
            pair = acc.at[:, pl.ds(pl.multiple_of(kk * 512, 512), 512)]
            _emit_heads(pair, cos_ref, sin_ref, c == 2, [o.at[0, h] for h in range(2)])


def _qkv_own(ids, x0, x1, x2, x3, w_ref, tab_ref, ptab_ref, o_ref, xs, acc, wt, sem):
    c, d = pl.program_id(0), pl.program_id(1)
    nd = pl.num_programs(1)
    bd, t = w_ref.shape[0], x0.shape[0]

    def copy(b, k):
        cols = pl.ds(pl.multiple_of(k * bd, bd), bd)
        return pltpu.make_async_copy((x0, x1, x2, x3)[b].at[:, cols], xs.at[pl.ds(b * t, t), cols], sem.at[k, b])

    @pl.when((c == 0) & (d == 0))
    def _():
        for k in range(x0.shape[1] // bd):
            for b in range(4):
                copy(b, k).start()

    @pl.when(d == 0)
    def _():
        acc[...] = jnp.zeros_like(acc)

    @pl.when(c == 0)
    def _():
        for b in range(4):
            copy(b, d).wait()

    _lay(w_ref, wt, ids[OWN_PART])
    cols = pl.ds(pl.multiple_of(d * bd, bd), bd)
    for h in range(2):
        for m in range(2):
            r = slice(m * 2 * t, (m + 1) * 2 * t)
            acc[r, h * 256:(h + 1) * 256] += jnp.dot(xs[r, cols], wt[:, h * 256:(h + 1) * 256],
                                                     preferred_element_type=F32)

    @pl.when(d == nd - 1)
    def _():
        for b in range(4):
            r = pl.ds(b * t, t)
            tb = (tab_ref, ptab_ref)[b % 2]
            tr = pl.ds((b // 2) * t, t)
            _emit_heads(acc.at[r], tb.at[0, tr], tb.at[1, tr], c == 2, [o_ref.at[b, 0, h] for h in range(2)])


def _qkv_next(ids, xn, w_ref, cos_ref, sin_ref, s_ref, c_ref, acc):
    c, j = pl.program_id(0), pl.program_id(1)

    acc[...] = jnp.dot(xn[...], w_ref[0], preferred_element_type=F32)
    for n, o_ref in enumerate((s_ref, c_ref)):
        @pl.when(j == n)
        def _():
            _emit_heads(acc, cos_ref, sin_ref, c == 2, [o_ref.at[0, h] for h in range(2)])


def _attend(masks, ids, l_ref, rs0, rs1, rc0, rc1, *refs):
    nq = len(masks)
    outs = refs[:2 * nq]
    qkv, m_s, l_s, acc, sem = refs[2 * nq:]
    src = [l_ref.at[b] for b in range(4)] + [rs0, rs1, rc0, rc1]
    t, dh = rs0.shape[2:]
    me = ids[ME]
    chips = [(me ^ m) // 2 for m in masks]
    last = functools.reduce(jnp.maximum, chips)

    def kv_copy(n, b):
        rows = pl.ds(pl.multiple_of(b * t, t), t)
        return pltpu.make_async_copy(src[n].at[pl.ds(1, 2)], qkv.at[pl.ds(1, 2), :, rows, :], sem.at[0, b])

    def q_copy(n, b):
        rows = pl.ds(pl.multiple_of(b * t, t), t)
        return pltpu.make_async_copy(src[n].at[0], qkv.at[0, :, rows, :], sem.at[1, b])

    for n in range(8):
        b = ids[SRC + n]
        want = functools.reduce(jnp.logical_or, [b // 2 == cc for cc in chips])

        @pl.when(want)
        def _():
            q_copy(n, b).start()

        @pl.when(b // 2 <= last)
        def _():
            kv_copy(n, b).start()

    k2 = (dh ** -0.5) * 1.4426950408889634

    k = me % 2

    def chip_rows(i, carry):
        cc = jnp.where(i == 0, chips[0], chips[1])
        q0 = pl.multiple_of(cc * 2 * t, 2 * t)
        for b in range(2):
            q_copy(0, 2 * cc + b).wait()
        m_s[...] = jnp.full_like(m_s, -jnp.inf)
        l_s[...] = jnp.zeros_like(l_s)
        acc[...] = jnp.zeros_like(acc)

        def kv_wait(j):
            @pl.when(i == 0)
            def _():
                for b in range(2):
                    kv_copy(0, 2 * j + b).wait()

        def tile(base, r0, nr, w, masked):
            rs = slice(r0, r0 + nr)
            ss = []
            for h in range(2):
                s = lax.dot_general(qkv[0, h, pl.ds(q0 + r0, nr), :], qkv[1, h, pl.ds(base, w), :],
                                    (((1,), (1,)), ((), ())), preferred_element_type=F32)
                if masked:
                    row = lax.broadcasted_iota(jnp.int32, (nr, w), 0)
                    col = lax.broadcasted_iota(jnp.int32, (nr, w), 1)
                    s = jnp.where(row >= col, s, -jnp.inf)
                ss.append(s)
            for h in range(2):
                ch = [ss[h][:, q * 128:(q + 1) * 128] for q in range(w // 128)]
                m_old = m_s[h, rs]
                m_new = jnp.maximum(m_old, jnp.max(functools.reduce(jnp.maximum, ch), axis=-1, keepdims=True))
                alpha = jnp.exp2((m_old - m_new) * k2)
                m_s[h, rs] = m_new
                mk = m_new * k2
                ps = [jnp.exp2(v * k2 - mk) for v in ch]
                l_s[h, rs] = l_s[h, rs] * alpha + functools.reduce(jnp.add, ps)
                p = jnp.concatenate([v.astype(BF) for v in ps], axis=1)
                pv = jnp.dot(p, qkv[2, h, pl.ds(base, w), :], preferred_element_type=F32)
                for q in range(dh // 128):
                    sl = slice(q * 128, (q + 1) * 128)
                    acc[h, rs, sl] = acc[h, rs, sl] * alpha + pv[:, sl]

        def body(j, carry):
            kv_wait(j)
            tile(pl.multiple_of(j * 2 * t, 2 * t), 0, 2 * t, 2 * t, False)
            return carry

        lax.fori_loop(0, cc, body, 0)
        kv_wait(cc)
        tile(q0, 0, t, t, True)
        tile(q0, t, t, t, False)
        tile(pl.multiple_of(q0 + t, t), t, t, t, True)

        @pl.when(i == 0)
        def _():
            def drain(j, carry):
                kv_wait(j)
                return carry

            lax.fori_loop(cc + 1, last + 1, drain, 0)

        for o in range(2):
            rs = pl.ds(pl.multiple_of((k if o == 0 else 1 - k) * t, t), t)
            for h in range(2):
                l = jnp.sum(l_s[h, rs, :], axis=-1, keepdims=True)
                v = (acc[h, rs, :] / l).astype(BF)
                for n in range(nq):
                    @pl.when(i == n)
                    def _(n=n):
                        outs[2 * n + o][:, h * dh:(h + 1) * dh] = v
        return carry

    lax.fori_loop(0, nq, chip_rows, 0)


def _out_first(ids, *refs):
    n = (len(refs) - 1) // 2
    o = jnp.concatenate([r[...] for r in refs[:n]], axis=1)
    w = jnp.concatenate([r[...] for r in refs[n:2 * n]], axis=0)
    refs[-1][...] = jnp.dot(o, w, preferred_element_type=F32)


def _out_last(ids, *refs):
    n = (len(refs) - 3) // 2
    o = jnp.concatenate([r[...] for r in refs[:n]], axis=1)
    w = jnp.concatenate([r[...] for r in refs[n:2 * n]], axis=0)
    part, x, out = refs[2 * n], refs[2 * n + 1], refs[-1]
    a = part[...] + jnp.dot(o, w, preferred_element_type=F32)
    out[...] = (x[...].astype(F32) + a).astype(BF)


def _params(**kw):
    return pltpu.CompilerParams(vmem_limit_bytes=VMEM_LIMIT, **kw)


def _cost(flops, nbytes):
    return pl.CostEstimate(flops=int(flops * COST), bytes_accessed=int(nbytes * COST), transcendentals=0)


def solution(mesh):
    rows = P(("data", "seq"), None)

    def local(x, g, wqkv, wo):
        t, d = x.shape
        _, _, hh, dh = wqkv.shape
        me = lax.axis_index("seq").astype(jnp.int32)
        k = me % 2
        kf, yf = 2 << k, 4 >> k

        def send(a, f):
            return lax.ppermute(a, "seq", [(i, f(i)) for i in range(8)])

        def to_a(i):
            return i ^ (2 << (i & 1))

        def to_same(i):
            return i ^ (4 >> (i & 1))

        def to_cross(i):
            return to_same(i) ^ 1

        inv = 10000.0 ** (-jnp.arange(dh // 2, dtype=F32) * 2.0 / dh)

        def tables(b):
            pos = (b[:, None] * t + jnp.arange(t)[None, :]).reshape(-1).astype(F32)
            ang = pos[:, None] * inv[None, :]
            return jnp.stack([jnp.cos(ang), jnp.sin(ang)])

        a_id, so, po = me ^ kf, me ^ yf, me ^ 1
        xo = po ^ kf

        ids = jnp.stack([me, so // 4, (so // 2) % 2, me // 4, me % 4]
                        + [me, po, a_id, po ^ yf, so, me ^ 6, xo, me ^ 7]
                        + [me ^ m for m in range(8)]).astype(jnp.int32)
        tab = tables(jnp.stack([me, a_id]))
        g2 = g[None, :]

        xa = send(x, to_a)

        half = jax.ShapeDtypeStruct((3, 2, t, dh), BF)
        xn_shape = jax.ShapeDtypeStruct((t, d), BF)
        bd = 1024
        nd = d // bd
        flops = 2 * t * d * 12 * dh

        def partner(a):
            return send(a, lambda i: i ^ 1)

        def tile_spec(at):
            return pl.BlockSpec((bd, 1, 8, dh), lambda c, i, s: (i, c, s[at], 0))

        def tab_spec(n, b):
            return pl.BlockSpec((pl.Squeezed(), t, dh // 2), lambda *_: (n, b, 0))

        whole = pl.BlockSpec((t, d), lambda *_: (0, 0), pipeline_mode=pl.Buffered(1))
        anyspec = pl.BlockSpec(memory_space=pl.ANY)
        half2 = pl.BlockSpec((1, 2, t, dh), lambda c, *_: (c, 0, 0, 0))

        b_same, b_cross, w_b, xn_o = pl.pallas_call(
            _qkv_first,
            grid_spec=pltpu.PrefetchScalarGridSpec(
                num_scalar_prefetch=1, grid=(3, nd),
                in_specs=[whole, pl.BlockSpec((1, d), lambda *_: (0, 0)), tile_spec(B_TILE),
                          tab_spec(0, 0), tab_spec(1, 0)],
                out_specs=[half2, half2, pl.BlockSpec((1, bd, 4 * dh), lambda c, i, s: (c, i, 0)), whole],
                scratch_shapes=[pltpu.VMEM((t, 4 * dh), F32)]),
            out_shape=[half, half, jax.ShapeDtypeStruct((3, d, 4 * dh), BF), xn_shape],
            compiler_params=_params(), cost_estimate=_cost(flops * 2.5, 80e6), name="qkv_first",
        )(ids, x, g2, wqkv, tab, tab)
        rs_own, rc_own = send(b_same, to_same), send(b_cross, to_cross)
        xn_po, ptab = partner(xn_o), partner(tab)
        rb = 128
        xn_a = pl.pallas_call(
            _norm_rows, grid=(t // rb,),
            in_specs=[pl.BlockSpec((rb, d), lambda i: (i, 0)), pl.BlockSpec((1, d), lambda i: (0, 0))],
            out_specs=pl.BlockSpec((rb, d), lambda i: (i, 0)), out_shape=xn_shape,
            compiler_params=_params(), cost_estimate=_cost(2e9, 8e6), name="norm",
        )(xa, g2)
        xn_pa = partner(xn_a)
        a_same, a_cross = pl.pallas_call(
            _qkv_next,
            grid_spec=pltpu.PrefetchScalarGridSpec(
                num_scalar_prefetch=1, grid=(3, 2),
                in_specs=[whole, pl.BlockSpec((1, d, 2 * dh), lambda c, i, s: (c, 0, (i + s[ME]) % 2)),
                          tab_spec(0, 1), tab_spec(1, 1)],
                out_specs=[half2, half2],
                scratch_shapes=[pltpu.VMEM((t, 2 * dh), F32)]),
            out_shape=[half, half],
            compiler_params=_params(), cost_estimate=_cost(flops * 1.4, 35e6), name="qkv_next",
        )(ids, xn_a, w_b, tab, tab)
        rs_a, rc_a = send(a_same, to_same), send(a_cross, to_cross)
        both_tab = pl.BlockSpec((2, 2 * t, dh // 2), lambda *_: (0, 0, 0), pipeline_mode=pl.Buffered(1))
        loc = pl.pallas_call(
            _qkv_own,
            grid_spec=pltpu.PrefetchScalarGridSpec(
                num_scalar_prefetch=1, grid=(3, nd),
                in_specs=[anyspec] * 4 + [tile_spec(OWN_TILE), both_tab, both_tab],
                out_specs=pl.BlockSpec((4, 1, 2, t, dh), lambda c, i, s: (0, c, 0, 0, 0)),
                scratch_shapes=[pltpu.VMEM((4 * t, d), BF), pltpu.VMEM((4 * t, 2 * dh), F32),
                                pltpu.VMEM((bd, 2 * dh), BF), pltpu.SemaphoreType.DMA((nd, 4))]),
            out_shape=jax.ShapeDtypeStruct((4, 3, 2, t, dh), BF),
            compiler_params=_params(), cost_estimate=_cost(flops * 2.8, 60e6), name="qkv_own",
        )(ids, xn_o, xn_po, xn_a, xn_pa, wqkv, tab, ptab)
        src = [loc, rs_own, rs_a, rc_own, rc_a]

        def attend(ms):
            nq = len(ms)
            return pl.pallas_call(
                functools.partial(_attend, ms),
                grid_spec=pltpu.PrefetchScalarGridSpec(
                    num_scalar_prefetch=1, grid=(1,),
                    in_specs=[anyspec] * 5,
                    out_specs=[pl.BlockSpec((t, 2 * dh), lambda i, s: (0, 0))] * (2 * nq),
                    scratch_shapes=[pltpu.VMEM((3, 2, 8 * t, dh), BF),
                                    pltpu.VMEM((2, 2 * t, 128), F32), pltpu.VMEM((2, 2 * t, 128), F32),
                                    pltpu.VMEM((2, 2 * t, dh), F32), pltpu.SemaphoreType.DMA((2, 8))]),
                out_shape=[jax.ShapeDtypeStruct((t, 2 * dh), BF)] * (2 * nq),
                compiler_params=_params(), cost_estimate=_cost(nq * 10e9, 13e6), name="attend",
            )(ids, *src)

        got = {}
        for ms in GROUPS:
            o = attend(ms)
            for i, m in enumerate(ms):
                for e in range(2):
                    v = m ^ e
                    got[v] = send(o[2 * i + e], lambda j, v=v: j ^ v) if v else o[2 * i + e]

        wo2 = wo.reshape(hh * dh, d)
        tn = 1024
        o_spec = pl.BlockSpec((t, 2 * dh), lambda i, s: (0, 0))

        def w_spec(m):
            return pl.BlockSpec((2 * dh, tn), lambda i, s: (s[DEV + m], i))

        def project(ms, part=None):
            n = len(ms)
            col = pl.BlockSpec((t, tn), lambda i, s: (0, i))
            extra = [] if part is None else [part, x]
            return pl.pallas_call(
                _out_first if part is None else _out_last,
                grid_spec=pltpu.PrefetchScalarGridSpec(
                    num_scalar_prefetch=1, grid=(d // tn,),
                    in_specs=[o_spec] * n + [w_spec(m) for m in ms] + [col] * len(extra),
                    out_specs=col),
                out_shape=jax.ShapeDtypeStruct((t, d), F32 if part is None else BF),
                compiler_params=_params(), cost_estimate=_cost(n * 2 * t * 2 * dh * d * 1.3, n * 4.2e6 + 8e6),
                name="project",
            )(ids, *[got[m] for m in ms], *[wo2] * n, *extra)

        part = project((0, 1, 2, 3, 4, 5))
        return project((6, 7), part)

    return jax.shard_map(local, mesh=mesh,
                         in_specs=(rows, P(None), P(None, None, None, None), P(None, None, None)),
                         out_specs=rows, check_vma=False)
```

profile of v0, /device:TPU:0, one launch (start us, length us, event | category | flops | bytes accessed | tf_op | source)
XLA Modules:
  0.0 216.2 jit_solution(13761400277144491209)
XLA Ops:
  0.0 3.3 %collective-permute-start.1 = (bf16[512,4096]{1,0:T(8,128)(2,1)}, bf16[512,4096]{1,0:T(8,128)(2,1)}, u32[]{:S(2)}, u32[]{:S(2)}) collective-permute-start(bf16[512,4096]{1,0:T(8,128)(2,1)} %refs_5_.1), channel_id=1, source_target_pairs={{0,2},{1,5},{2,0},{3,7},{4,6},{5,1},{6,4},{7,3}} | collective-permute-start | bytes 12582920 | tf_op jit(solution)/shard_map/ppermute | solution.py:277
  3.3 0.1 add_multiply_fusion
  3.4 0.1 convert_bitcast_fusion
  3.5 0.6 stack.82.ids
  4.1 1.9 multiply_cosine_fusion
  6.0 1.0 pad_maximum_fusion.cos_ref.sin_ref.tab_ref
  7.1 41.2 %qkv_first.1 = (bf16[3,2,512,256]{3,2,1,0:T(8,128)(2,1)}, bf16[3,2,512,256]{3,2,1,0:T(8,128)(2,1)}, bf16[3,4096,1024]{2,1,0:T(8,128)(2,1)}, bf16[512,4096]{1,0:T(8,128)(2,1)}) custom-call(s32[21]{0:T(128)} %stack.82.ids, bf16[512,4096]{1,0:T(8,128)(2,1)} %refs_5_.1, f32[1,4096]{1,0:T(1,128)} %bitcast.29, bf16[4096,3,16,256]{3,2,1,0:T(8,128)(2,1)} %w_ref.3, ...), custom_call_target="tpu_custom_call" | custom-call | flops 1610612736 | bytes 4000000 | tf_op jit(solution)/shard_map/qkv_first/pallas_call | solution.py:325
  48.3 0.0 copy-start
  48.3 0.0 collective-permute-start
  48.3 1.8 collective-permute-done.1.x_ref
  50.1 6.1 %norm.1.x2.xn = bf16[512,4096]{1,0:T(8,128)(2,1)} custom-call(bf16[512,4096]{1,0:T(8,128)(2,1)} %collective-permute-done.1.x_ref, f32[1,4096]{1,0:T(1,128)} %bitcast.30), custom_call_target="tpu_custom_call" | custom-call | flops 100000000 | bytes 400000 | tf_op jit(solution)/shard_map/norm/pallas_call | solution.py:339
  56.2 0.0 collective-permute-start.2
  56.2 0.0 copy-done
  56.2 0.5 collective-permute-start.3
  56.7 2.1 collective-permute-start.4
  58.7 0.8 collective-permute-start.6
  59.6 20.5 %qkv_next.1 = (bf16[3,2,512,256]{3,2,1,0:T(8,128)(2,1)}, bf16[3,2,512,256]{3,2,1,0:T(8,128)(2,1)}) custom-call(s32[21]{0:T(128)} %stack.82.ids, bf16[512,4096]{1,0:T(8,128)(2,1)} %norm.1.x2.xn, bf16[3,4096,1024]{2,1,0:T(8,128)(2,1)} %get-tuple-element.21.w_ref, f32[2,1024,128]{2,1,0:T(8,128)} %pad_maximum_fusion.cos_ref.sin_ref.tab_ref, ...), custom_call_target="tpu_custom_call" | custom-call | flops 901943104 | bytes 1750000 | tf_op jit(solution)/shard_map/qkv_next/pallas_call | solution.py:346
  80.1 0.0 collective-permute-done.3.ptab_ref
  80.1 0.5 collective-permute-start.5
  80.6 0.0 collective-permute-done.x1
  80.6 0.4 collective-permute-start.7
  81.0 0.0 collective-permute-done.2.x3
  81.0 45.1 %qkv_own.1.l_ref = bf16[4,3,2,512,256]{4,3,2,1,0:T(8,128)(2,1)} custom-call(s32[21]{0:T(128)} %stack.82.ids, bf16[512,4096]{1,0:T(8,128)(2,1)} %get-tuple-element.19.x0, bf16[512,4096]{1,0:T(8,128)(2,1)} %collective-permute-done.x1, bf16[512,4096]{1,0:T(8,128)(2,1)} %norm.1.x2.xn, bf16[512,4096]{1,0:T(8,128)(2,1)} %collective-permute-done.2.x3, ...), custom_call_target="tpu_custom_call" | custom-call | flops 1803886208 | bytes 3000000 | tf_op jit(solution)/shard_map/qkv_own/pallas_call | solution.py:359
  126.2 0.0 collective-permute-done.4.rs0
  126.2 0.0 collective-permute-done.6.rc0
  126.2 0.0 collective-permute-done.5.rs1
  126.2 0.0 copy-start.1
  126.2 1.3 collective-permute-done.7.rc1
  127.5 22.7 %attend.3 = (bf16[512,512]{1,0:T(8,128)(2,1)}, bf16[512,512]{1,0:T(8,128)(2,1)}, bf16[512,512]{1,0:T(8,128)(2,1)}, bf16[512,512]{1,0:T(8,128)(2,1)}) custom-call(s32[21]{0:T(128)} %stack.82.ids, bf16[4,3,2,512,256]{4,3,2,1,0:T(8,128)(2,1)} %qkv_own.1.l_ref, bf16[3,2,512,256]{3,2,1,0:T(8,128)(2,1)} %collective-permute-done.4.rs0, ...), custom_call_target="tpu_custom_call" | custom-call | flops 1000000000 | bytes 650000 | tf_op jit(solution)/shard_map/attend/pallas_call | solution.py:374
  150.3 1.9 collective-permute-start.11
  152.2 0.0 collective-permute-start.12
  152.2 2.1 collective-permute-start.13
  154.3 0.0 collective-permute-start.14
  154.3 23.4 %attend.2 = (bf16[512,512]{1,0:T(8,128)(2,1)}, bf16[512,512]{1,0:T(8,128)(2,1)}, bf16[512,512]{1,0:T(8,128)(2,1)}, bf16[512,512]{1,0:T(8,128)(2,1)}) custom-call(s32[21]{0:T(128)} %stack.82.ids, bf16[4,3,2,512,256]{4,3,2,1,0:T(8,128)(2,1)} %qkv_own.1.l_ref, bf16[3,2,512,256]{3,2,1,0:T(8,128)(2,1)} %collective-permute-done.4.rs0, ...), custom_call_target="tpu_custom_call" | custom-call | flops 1000000000 | bytes 650000 | tf_op jit(solution)/shard_map/attend/pallas_call | solution.py:374
  177.7 0.1 collective-permute-start.10
  177.9 0.0 collective-permute-done.11.refs_2_
  177.9 2.8 %collective-permute-start.8 = (bf16[512,512]{1,0:T(8,128)(2,1)}, bf16[512,512]{1,0:T(8,128)(2,1)}, u32[]{:S(2)}, u32[]{:S(2)}) collective-permute-start(bf16[512,512]{1,0:T(8,128)(2,1)} %get-tuple-element.25), channel_id=1, source_target_pairs={{0,6},{1,7},{2,4},{3,5},{4,2},{5,3},{6,0},{7,1}} | collective-permute-start | bytes 1572872 | tf_op jit(solution)/shard_map/ppermute | solution.py:277
  180.6 0.0 collective-permute-done.12.refs_3_
  180.6 0.0 collective-permute-start.9
  180.7 0.0 collective-permute-done.13.refs_4_
  180.7 0.0 collective-permute-done.14.refs_5_
  180.7 0.0 collective-permute-done.10.refs_1_
  180.7 0.7 copy-done.3
  181.4 0.2 copy-done.4
  181.7 20.4 %project.2.refs_4_ = f32[512,4096]{1,0:T(8,128)} custom-call(s32[21]{0:T(128)} %stack.82.ids, bf16[512,512]{1,0:T(8,128)(2,1)} %get-tuple-element.27.refs_0_, bf16[512,512]{1,0:T(8,128)(2,1)} %collective-permute-done.10.refs_1_, bf16[512,512]{1,0:T(8,128)(2,1)} %copy-done.2, bf16[512,512]{1,0:T(8,128)(2,1)} %copy-done.3, bf16[512,512]{1,0:T(8,128)(2,1)} %copy-done.4, ...), custom_call_target="tpu_custom_call" | custom-call | flops 837518592 | bytes 1660000 | tf_op jit(solution)/shard_map/project/pallas_call | solution.py:406
  202.0 0.0 collective-permute-done.8.refs_0_
  202.0 2.0 collective-permute-done.9.refs_1_
  204.0 12.2 %project.3 = bf16[512,4096]{1,0:T(8,128)(2,1)} custom-call(s32[21]{0:T(128)} %stack.82.ids, bf16[512,512]{1,0:T(8,128)(2,1)} %collective-permute-done.8.refs_0_, bf16[512,512]{1,0:T(8,128)(2,1)} %collective-permute-done.9.refs_1_, bf16[4096,4096]{1,0:T(8,128)(2,1)} %bitcast.27, bf16[4096,4096]{1,0:T(8,128)(2,1)} %bitcast.28, f32[512,4096]{1,0:T(8,128)} %project.2.refs_4_, ...), custom_call_target="tpu_custom_call" | custom-call | flops 279172864 | bytes 820000 | tf_op jit(solution)/shard_map/project/pallas_call | solution.py:406
  (7 shorter events, 0.0 us)
Async XLA Ops:
  0.0 50.1 %collective-permute-start.1 = (bf16[512,4096]{1,0:T(8,128)(2,1)}, bf16[512,4096]{1,0:T(8,128)(2,1)}, u32[]{:S(2)}, u32[]{:S(2)}) collective-permute-start(bf16[512,4096]{1,0:T(8,128)(2,1)} %refs_5_.1), channel_id=1, source_target_pairs={{0,2},{1,5},{2,0},{3,7},{4,6},{5,1},{6,4},{7,3}} | collective-permute-start | bytes 12582920 | tf_op jit(solution)/shard_map/ppermute | solution.py:277
  48.3 7.9 %copy-start = (f32[2,1024,128]{2,1,0:T(8,128)S(1)}, f32[2,1024,128]{2,1,0:T(8,128)}, u32[]{:S(2)}) copy-start(f32[2,1024,128]{2,1,0:T(8,128)} %pad_maximum_fusion.cos_ref.sin_ref.tab_ref) | copy-start | bytes 3145732
  48.3 32.3 %collective-permute-start = (bf16[512,4096]{1,0:T(8,128)(2,1)}, bf16[512,4096]{1,0:T(8,128)(2,1)}, u32[]{:S(2)}, u32[]{:S(2)}) collective-permute-start(bf16[512,4096]{1,0:T(8,128)(2,1)} %get-tuple-element.19.x0), channel_id=1, source_target_pairs={{0,1},{1,0},{2,3},{3,2},{4,5},{5,4},{6,7},{7,6}} | collective-permute-start | bytes 12582920 | tf_op jit(solution)/shard_map/ppermute | solution.py:277
  56.2 24.9 %collective-permute-start.2 = (bf16[512,4096]{1,0:T(8,128)(2,1)}, bf16[512,4096]{1,0:T(8,128)(2,1)}, u32[]{:S(2)}, u32[]{:S(2)}) collective-permute-start(bf16[512,4096]{1,0:T(8,128)(2,1)} %norm.1.x2.xn), channel_id=1, source_target_pairs={{0,1},{1,0},{2,3},{3,2},{4,5},{5,4},{6,7},{7,6}} | collective-permute-start | bytes 12582920 | tf_op jit(solution)/shard_map/ppermute | solution.py:277
  56.2 23.9 %collective-permute-start.3 = (f32[2,1024,128]{2,1,0:T(8,128)S(1)}, f32[2,1024,128]{2,1,0:T(8,128)}, u32[]{:S(2)}, u32[]{:S(2)}) collective-permute-start(f32[2,1024,128]{2,1,0:T(8,128)S(1)} %copy-done), channel_id=1, source_target_pairs={{0,1},{1,0},{2,3},{3,2},{4,5},{5,4},{6,7},{7,6}} | collective-permute-start | bytes 3145736 | tf_op jit(solution)/shard_map/ppermute | solution.py:277
  56.7 69.5 %collective-permute-start.4 = (bf16[3,2,512,256]{3,2,1,0:T(8,128)(2,1)}, bf16[3,2,512,256]{3,2,1,0:T(8,128)(2,1)}, u32[]{:S(2)}, u32[]{:S(2)}) collective-permute-start(bf16[3,2,512,256]{3,2,1,0:T(8,128)(2,1)} %get-tuple-element.20), channel_id=1, source_target_pairs={{0,4},{1,3},{2,6},{3,1},{4,0},{5,7},{6,2},{7,5}} | collective-permute-start | bytes 4718600 | tf_op jit(solution)/shard_map/ppermute | solution.py:277
  58.7 67.4 %collective-permute-start.6 = (bf16[3,2,512,256]{3,2,1,0:T(8,128)(2,1)}, bf16[3,2,512,256]{3,2,1,0:T(8,128)(2,1)}, u32[]{:S(2)}, u32[]{:S(2)}) collective-permute-start(bf16[3,2,512,256]{3,2,1,0:T(8,128)(2,1)} %get-tuple-element.23), channel_id=1, source_target_pairs={{0,5},{1,2},{2,7},{3,0},{4,1},{5,6},{6,3},{7,4}} | collective-permute-start | bytes 4718600 | tf_op jit(solution)/shard_map/ppermute | solution.py:277
  80.1 46.1 %collective-permute-start.5 = (bf16[3,2,512,256]{3,2,1,0:T(8,128)(2,1)}, bf16[3,2,512,256]{3,2,1,0:T(8,128)(2,1)S(1)}, u32[]{:S(2)}, u32[]{:S(2)}) collective-permute-start(bf16[3,2,512,256]{3,2,1,0:T(8,128)(2,1)} %get-tuple-element.22), channel_id=1, source_target_pairs={{0,4},{1,3},{2,6},{3,1},{4,0},{5,7},{6,2},{7,5}} | collective-permute-start | bytes 4718600 | tf_op jit(solution)/shard_map/ppermute | solution.py:277
  80.6 46.9 %collective-permute-start.7 = (bf16[3,2,512,256]{3,2,1,0:T(8,128)(2,1)}, bf16[3,2,512,256]{3,2,1,0:T(8,128)(2,1)}, u32[]{:S(2)}, u32[]{:S(2)}) collective-permute-start(bf16[3,2,512,256]{3,2,1,0:T(8,128)(2,1)} %get-tuple-element.24), channel_id=1, source_target_pairs={{0,5},{1,2},{2,7},{3,0},{4,1},{5,6},{6,3},{7,4}} | collective-permute-start | bytes 4718600 | tf_op jit(solution)/shard_map/ppermute | solution.py:277
  126.2 1.3 copy-start.1
  150.3 27.6 %collective-permute-start.11 = (bf16[512,512]{1,0:T(8,128)(2,1)}, bf16[512,512]{1,0:T(8,128)(2,1)S(1)}, u32[]{:S(2)}, u32[]{:S(2)}) collective-permute-start(bf16[512,512]{1,0:T(8,128)(2,1)} %get-tuple-element.29), channel_id=1, source_target_pairs={{0,2},{1,3},{2,0},{3,1},{4,6},{5,7},{6,4},{7,5}} | collective-permute-start | bytes 1572872 | tf_op jit(solution)/shard_map/ppermute | solution.py:277
  152.2 28.5 %collective-permute-start.12 = (bf16[512,512]{1,0:T(8,128)(2,1)}, bf16[512,512]{1,0:T(8,128)(2,1)S(1)}, u32[]{:S(2)}, u32[]{:S(2)}) collective-permute-start(bf16[512,512]{1,0:T(8,128)(2,1)} %get-tuple-element.30), channel_id=1, source_target_pairs={{0,3},{1,2},{2,1},{3,0},{4,7},{5,6},{6,5},{7,4}} | collective-permute-start | bytes 1572872 | tf_op jit(solution)/shard_map/ppermute | solution.py:277
  152.2 28.5 %collective-permute-start.13 = (bf16[512,512]{1,0:T(8,128)(2,1)}, bf16[512,512]{1,0:T(8,128)(2,1)S(1)}, u32[]{:S(2)}, u32[]{:S(2)}) collective-permute-start(bf16[512,512]{1,0:T(8,128)(2,1)} %get-tuple-element.31), channel_id=1, source_target_pairs={{0,4},{1,5},{2,6},{3,7},{4,0},{5,1},{6,2},{7,3}} | collective-permute-start | bytes 1572872 | tf_op jit(solution)/shard_map/ppermute | solution.py:277
  154.3 26.3 %collective-permute-start.14 = (bf16[512,512]{1,0:T(8,128)(2,1)}, bf16[512,512]{1,0:T(8,128)(2,1)}, u32[]{:S(2)}, u32[]{:S(2)}) collective-permute-start(bf16[512,512]{1,0:T(8,128)(2,1)} %get-tuple-element.32), channel_id=1, source_target_pairs={{0,5},{1,4},{2,7},{3,6},{4,1},{5,0},{6,3},{7,2}} | collective-permute-start | bytes 1572872 | tf_op jit(solution)/shard_map/ppermute | solution.py:277
  177.7 2.9 %collective-permute-start.10 = (bf16[512,512]{1,0:T(8,128)(2,1)}, bf16[512,512]{1,0:T(8,128)(2,1)}, u32[]{:S(2)}, u32[]{:S(2)}) collective-permute-start(bf16[512,512]{1,0:T(8,128)(2,1)} %get-tuple-element.28), channel_id=1, source_target_pairs={{0,1},{1,0},{2,3},{3,2},{4,5},{5,4},{6,7},{7,6}} | collective-permute-start | bytes 1572872 | tf_op jit(solution)/shard_map/ppermute | solution.py:277
  177.9 2.8 %copy-start.2 = (bf16[512,512]{1,0:T(8,128)(2,1)}, bf16[512,512]{1,0:T(8,128)(2,1)S(1)}, u32[]{:S(2)}) copy-start(bf16[512,512]{1,0:T(8,128)(2,1)S(1)} %collective-permute-done.11.refs_2_) | copy-start | bytes 1572868
  177.9 24.1 %collective-permute-start.8 = (bf16[512,512]{1,0:T(8,128)(2,1)}, bf16[512,512]{1,0:T(8,128)(2,1)}, u32[]{:S(2)}, u32[]{:S(2)}) collective-permute-start(bf16[512,512]{1,0:T(8,128)(2,1)} %get-tuple-element.25), channel_id=1, source_target_pairs={{0,6},{1,7},{2,4},{3,5},{4,2},{5,3},{6,0},{7,1}} | collective-permute-start | bytes 1572872 | tf_op jit(solution)/shard_map/ppermute | solution.py:277
  180.6 0.8 copy-start.3
  180.6 23.3 %collective-permute-start.9 = (bf16[512,512]{1,0:T(8,128)(2,1)}, bf16[512,512]{1,0:T(8,128)(2,1)}, u32[]{:S(2)}, u32[]{:S(2)}) collective-permute-start(bf16[512,512]{1,0:T(8,128)(2,1)} %get-tuple-element.26), channel_id=1, source_target_pairs={{0,7},{1,6},{2,5},{3,4},{4,3},{5,2},{6,1},{7,0}} | collective-permute-start | bytes 1572872 | tf_op jit(solution)/shard_map/ppermute | solution.py:277
  180.7 1.0 copy-start.4
where the time goes:
time: 217 us; the launch traced here: 216 us
  Pallas kernels  192 us (88%)
  starting transfers between devices  14.6 us (7%)
  waiting for transfers between devices  5.08 us (2%)
  other arithmetic  3.09 us (1%)
    pallas_call x2, Pallas kernels, attend(): pl.pallas_call(functools.partial(_attend, ms), grid_spec=pltpu.PrefetchSc...  46.1 us
    pallas_call x1, Pallas kernels, local(): pl.pallas_call(_qkv_own, grid_spec=pltpu.PrefetchScalarGridSpec(num_scala...  45.1 us
    pallas_call x1, Pallas kernels, local(): pl.pallas_call(_qkv_first, grid_spec=pltpu.PrefetchScalarGridSpec(num_sca...  41.2 us
    pallas_call x2, Pallas kernels, project(): pl.pallas_call(_out_first if part is None else _out_last, grid_spec=pltpu...  32.6 us
    pallas_call x1, Pallas kernels, local(): pl.pallas_call(_qkv_next, grid_spec=pltpu.PrefetchScalarGridSpec(num_scal...  20.5 us
    ppermute x15, starting transfers between devices, send(): return lax.ppermute(a, 'seq', [(i, f(i)) for i in range(8)])  14.6 us
    pallas_call x1, Pallas kernels, local(): pl.pallas_call(_norm_rows, grid=(t // rb,), in_specs=[pl.BlockSpec((rb, d...  6.05 us
    ppermute x15, waiting for transfers between devices, send(): return lax.ppermute(a, 'seq', [(i, f(i)) for i in range(8)])  5.08 us
  transfers between devices with their start and end apart: 15, of which 3 were waited for; matrix products, arithmetic and copies ran while one was open for 2% of the time, Pallas kernels for 72%

commit v1 on v0

--- a/solution.py
+++ b/solution.py
@@ -13,7 +13,7 @@
 VMEM_LIMIT = 62 << 20
 COST = 0.05
 GROUPS = ((2, 4), (6, 0))
-ME, B_TILE, B_PART, OWN_TILE, OWN_PART, SRC, DEV = 0, 1, 2, 3, 4, 5, 13
+ME, B_HEAD, OWN_HEAD, SRC, DEV = 0, 1, 2, 3, 11
 
 
 def _norm(x_ref, g_ref, xn, base):
@@ -48,17 +48,36 @@
             o[:, 128:] = (x2 * cs + x1 * sn).astype(BF)
 
 
-def _lay(w_ref, wt, at):
-    bd, n = w_ref.shape[0], wt.shape[1]
-    for p in range(8 * 256 // n):
-        @pl.when(at == p)
-        def _():
-            wt[...] = w_ref[:, 0].reshape(bd, 8 * 256)[:, p * n:(p + 1) * n]
-
-
-def _qkv_first(ids, x_ref, g_ref, w_ref, cos_ref, sin_ref, s_ref, c_ref, wr_ref, xn, acc):
+def _stream(w_ref, buf, sem, head):
     c, d = pl.program_id(0), pl.program_id(1)
-    bd = w_ref.shape[0]
+    nc, nd = pl.num_programs(0), pl.num_programs(1)
+    _, bd, n, dh = buf.shape
+    i = c * nd + d
+
+    def copy(j):
+        rows = pl.ds(pl.multiple_of(lax.rem(j, nd) * bd, bd), bd)
+        heads = pl.ds(pl.multiple_of(head, n), n)
+        return pltpu.make_async_copy(w_ref.at[rows, j // nd, heads, :], buf.at[j % 2], sem.at[j % 2])
+
+    @pl.when(i == 0)
+    def _():
+        copy(0).start()
+
+    @pl.when(i + 1 < nc * nd)
+    def _():
+        copy(i + 1).start()
+
+    def take():
+        copy(i).wait()
+        return buf[i % 2].reshape(bd, n * dh)
+
+    return take
+
+
+def _qkv_first(ids, x_ref, g_ref, w_ref, cos_ref, sin_ref, s_ref, c_ref, wr_ref, xn, acc, buf, wsem):
+    c, d = pl.program_id(0), pl.program_id(1)
+    bd = buf.shape[1]
+    take = _stream(w_ref, buf, wsem, ids[B_HEAD])
 
     @pl.when((c == 0) & (d == 0))
     def _():
@@ -68,7 +87,7 @@
     def _():
         acc[...] = jnp.zeros_like(acc)
 
-    _lay(w_ref, wr_ref.at[0], ids[B_PART])
+    wr_ref[0] = take()
     xb = xn[:, pl.ds(pl.multiple_of(d * bd, bd), bd)]
     acc[...] += jnp.dot(xb, wr_ref[0], preferred_element_type=F32)
 
@@ -80,10 +99,11 @@
             _emit_heads(pair, cos_ref, sin_ref, c == 2, [o.at[0, h] for h in range(2)])
 
 
-def _qkv_own(ids, x0, x1, x2, x3, w_ref, tab_ref, ptab_ref, o_ref, xs, acc, wt, sem):
+def _qkv_own(ids, x0, x1, x2, x3, w_ref, tab_ref, ptab_ref, o_ref, xs, acc, wt, sem, buf, wsem):
     c, d = pl.program_id(0), pl.program_id(1)
     nd = pl.num_programs(1)
-    bd, t = w_ref.shape[0], x0.shape[0]
+    bd, t = buf.shape[1], x0.shape[0]
+    take = _stream(w_ref, buf, wsem, ids[OWN_HEAD])
 
     def copy(b, k):
         cols = pl.ds(pl.multiple_of(k * bd, bd), bd)
@@ -104,7 +124,7 @@
         for b in range(4):
             copy(b, d).wait()
 
-    _lay(w_ref, wt, ids[OWN_PART])
+    wt[...] = take()
     cols = pl.ds(pl.multiple_of(d * bd, bd), bd)
     for h in range(2):
         for m in range(2):
@@ -295,7 +315,7 @@
         a_id, so, po = me ^ kf, me ^ yf, me ^ 1
         xo = po ^ kf
 
-        ids = jnp.stack([me, so // 4, (so // 2) % 2, me // 4, me % 4]
+        ids = jnp.stack([me, so // 2 * 4, me * 2]
                         + [me, po, a_id, po ^ yf, so, me ^ 6, xo, me ^ 7]
                         + [me ^ m for m in range(8)]).astype(jnp.int32)
         tab = tables(jnp.stack([me, a_id]))
@@ -312,8 +332,8 @@
         def partner(a):
             return send(a, lambda i: i ^ 1)
 
-        def tile_spec(at):
-            return pl.BlockSpec((bd, 1, 8, dh), lambda c, i, s: (i, c, s[at], 0))
+        def tiles(n):
+            return [pltpu.VMEM((2, bd, n, dh), BF), pltpu.SemaphoreType.DMA((2,))]
 
         def tab_spec(n, b):
             return pl.BlockSpec((pl.Squeezed(), t, dh // 2), lambda *_: (n, b, 0))
@@ -326,10 +346,10 @@
             _qkv_first,
             grid_spec=pltpu.PrefetchScalarGridSpec(
                 num_scalar_prefetch=1, grid=(3, nd),
-                in_specs=[whole, pl.BlockSpec((1, d), lambda *_: (0, 0)), tile_spec(B_TILE),
+                in_specs=[whole, pl.BlockSpec((1, d), lambda *_: (0, 0)), anyspec,
                           tab_spec(0, 0), tab_spec(1, 0)],
                 out_specs=[half2, half2, pl.BlockSpec((1, bd, 4 * dh), lambda c, i, s: (c, i, 0)), whole],
-                scratch_shapes=[pltpu.VMEM((t, 4 * dh), F32)]),
+                scratch_shapes=[pltpu.VMEM((t, 4 * dh), F32)] + tiles(4)),
             out_shape=[half, half, jax.ShapeDtypeStruct((3, d, 4 * dh), BF), xn_shape],
             compiler_params=_params(), cost_estimate=_cost(flops * 2.5, 80e6), name="qkv_first",
         )(ids, x, g2, wqkv, tab, tab)
@@ -360,10 +380,11 @@
             _qkv_own,
             grid_spec=pltpu.PrefetchScalarGridSpec(
                 num_scalar_prefetch=1, grid=(3, nd),
-                in_specs=[anyspec] * 4 + [tile_spec(OWN_TILE), both_tab, both_tab],
+                in_specs=[anyspec] * 5 + [both_tab, both_tab],
                 out_specs=pl.BlockSpec((4, 1, 2, t, dh), lambda c, i, s: (0, c, 0, 0, 0)),
                 scratch_shapes=[pltpu.VMEM((4 * t, d), BF), pltpu.VMEM((4 * t, 2 * dh), F32),
-                                pltpu.VMEM((bd, 2 * dh), BF), pltpu.SemaphoreType.DMA((nd, 4))]),
+                                pltpu.VMEM((bd, 2 * dh), BF), pltpu.SemaphoreType.DMA((nd, 4))]
+                + tiles(2)),
             out_shape=jax.ShapeDtypeStruct((4, 3, 2, t, dh), BF),
             compiler_params=_params(), cost_estimate=_cost(flops * 2.8, 60e6), name="qkv_own",
         )(ids, xn_o, xn_po, xn_a, xn_pa, wqkv, tab, ptab)

time: 217 us -> 217 us (level)
  Pallas kernels: 192 us -> 177 us
  waiting for transfers between devices: 5.08 us -> 19.4 us
    ppermute x15, waiting for transfers between devices: 5.08 us -> 19.4 us  [send(): return lax.ppermute(a, 'seq', [(i, f(i)) for i in range(8)])]
    pallas_call x1, Pallas kernels: 41.2 us -> 33.6 us  [local(): pl.pallas_call(_qkv_first, grid_spec=pltpu.PrefetchScalarGridSpec(num_sca...]
    pallas_call x1, Pallas kernels: 45.1 us -> 38.5 us  [local(): pl.pallas_call(_qkv_own, grid_spec=pltpu.PrefetchScalarGridSpec(num_scala...]
  transfers between devices with their start and end apart: 15 -> 15, of which waited for: 3 -> 3; matrix products, arithmetic and copies ran while one was open for 2% -> 2% of each run, Pallas kernels for 72% -> 66%
where the time goes in v1:
time: 217 us; the launch traced here: 216 us
  Pallas kernels  177 us (82%)
  waiting for transfers between devices  19.4 us (9%)
  starting transfers between devices  14.6 us (7%)
  other arithmetic  3.09 us (1%)
    pallas_call x2, Pallas kernels, attend(): pl.pallas_call(functools.partial(_attend, ms), grid_spec=pltpu.PrefetchSc...  46.1 us
    pallas_call x1, Pallas kernels, local(): pl.pallas_call(_qkv_own, grid_spec=pltpu.PrefetchScalarGridSpec(num_scala...  38.5 us
    pallas_call x1, Pallas kernels, local(): pl.pallas_call(_qkv_first, grid_spec=pltpu.PrefetchScalarGridSpec(num_sca...  33.6 us
    pallas_call x2, Pallas kernels, project(): pl.pallas_call(_out_first if part is None else _out_last, grid_spec=pltpu...  32.6 us
    pallas_call x1, Pallas kernels, local(): pl.pallas_call(_qkv_next, grid_spec=pltpu.PrefetchScalarGridSpec(num_scal...  20.5 us
    ppermute x15, waiting for transfers between devices, send(): return lax.ppermute(a, 'seq', [(i, f(i)) for i in range(8)])  19.4 us
    ppermute x15, starting transfers between devices, send(): return lax.ppermute(a, 'seq', [(i, f(i)) for i in range(8)])  14.6 us
    pallas_call x1, Pallas kernels, local(): pl.pallas_call(_norm_rows, grid=(t // rb,), in_specs=[pl.BlockSpec((rb, d...  6.05 us
  transfers between devices with their start and end apart: 15, of which 3 were waited for; matrix products, arithmetic and copies ran while one was open for 2% of the time, Pallas kernels for 66%

profile of v1, /device:TPU:0, one launch (start us, length us, event | category | flops | bytes accessed | tf_op | source)
XLA Modules:
  0.0 216.2 jit_solution(203281271723087966)
XLA Ops:
  0.0 3.3 %collective-permute-start.1 = (bf16[512,4096]{1,0:T(8,128)(2,1)}, bf16[512,4096]{1,0:T(8,128)(2,1)}, u32[]{:S(2)}, u32[]{:S(2)}) collective-permute-start(bf16[512,4096]{1,0:T(8,128)(2,1)} %refs_5_.1), channel_id=1, source_target_pairs={{0,2},{1,5},{2,0},{3,7},{4,6},{5,1},{6,4},{7,3}} | collective-permute-start | bytes 12582920 | tf_op jit(solution)/shard_map/ppermute | solution.py:297
  3.3 0.1 add_multiply_fusion
  3.4 0.1 convert_bitcast_fusion
  3.5 0.6 stack.74.ids
  4.1 1.9 multiply_cosine_fusion
  6.0 1.0 pad_maximum_fusion.cos_ref.sin_ref.tab_ref
  7.0 33.6 %qkv_first.1 = (bf16[3,2,512,256]{3,2,1,0:T(8,128)(2,1)}, bf16[3,2,512,256]{3,2,1,0:T(8,128)(2,1)}, bf16[3,4096,1024]{2,1,0:T(8,128)(2,1)}, bf16[512,4096]{1,0:T(8,128)(2,1)}) custom-call(s32[19]{0:T(128)} %stack.74.ids, bf16[512,4096]{1,0:T(8,128)(2,1)} %refs_5_.1, f32[1,4096]{1,0:T(1,128)} %bitcast.27, bf16[4096,3,16,256]{3,2,1,0:T(8,128)(2,1)} %w_ref.3, ...), custom_call_target="tpu_custom_call" | custom-call | flops 1610612736 | bytes 4000000 | tf_op jit(solution)/shard_map/qkv_first/pallas_call | solution.py:345
  40.7 0.0 copy-start
  40.7 0.0 collective-permute-start
  40.7 9.4 %collective-permute-done.1.x_ref = bf16[512,4096]{1,0:T(8,128)(2,1)} collective-permute-done((bf16[512,4096]{1,0:T(8,128)(2,1)}, bf16[512,4096]{1,0:T(8,128)(2,1)}, u32[]{:S(2)}, u32[]{:S(2)}) %collective-permute-start.1) | collective-permute-done | bytes 4194336 | tf_op jit(solution)/shard_map/ppermute | solution.py:297
  50.1 6.1 %norm.1.x2.xn = bf16[512,4096]{1,0:T(8,128)(2,1)} custom-call(bf16[512,4096]{1,0:T(8,128)(2,1)} %collective-permute-done.1.x_ref, f32[1,4096]{1,0:T(1,128)} %bitcast.28), custom_call_target="tpu_custom_call" | custom-call | flops 100000000 | bytes 400000 | tf_op jit(solution)/shard_map/norm/pallas_call | solution.py:359
  56.2 0.0 collective-permute-start.2
  56.2 0.0 copy-done
  56.2 0.5 collective-permute-start.3
  56.7 2.1 collective-permute-start.4
  58.7 0.8 collective-permute-start.6
  59.6 20.5 %qkv_next.1 = (bf16[3,2,512,256]{3,2,1,0:T(8,128)(2,1)}, bf16[3,2,512,256]{3,2,1,0:T(8,128)(2,1)}) custom-call(s32[19]{0:T(128)} %stack.74.ids, bf16[512,4096]{1,0:T(8,128)(2,1)} %norm.1.x2.xn, bf16[3,4096,1024]{2,1,0:T(8,128)(2,1)} %get-tuple-element.21.w_ref, f32[2,1024,128]{2,1,0:T(8,128)} %pad_maximum_fusion.cos_ref.sin_ref.tab_ref, ...), custom_call_target="tpu_custom_call" | custom-call | flops 901943104 | bytes 1750000 | tf_op jit(solution)/shard_map/qkv_next/pallas_call | solution.py:366
  80.1 0.0 collective-permute-done.3.ptab_ref
  80.1 0.5 collective-permute-start.5
  80.6 0.0 collective-permute-done.x1
  80.6 0.4 collective-permute-start.7
  81.0 0.0 collective-permute-done.2.x3
  81.0 38.5 %qkv_own.1.l_ref = bf16[4,3,2,512,256]{4,3,2,1,0:T(8,128)(2,1)} custom-call(s32[19]{0:T(128)} %stack.74.ids, bf16[512,4096]{1,0:T(8,128)(2,1)} %get-tuple-element.19.x0, bf16[512,4096]{1,0:T(8,128)(2,1)} %collective-permute-done.x1, bf16[512,4096]{1,0:T(8,128)(2,1)} %norm.1.x2.xn, bf16[512,4096]{1,0:T(8,128)(2,1)} %collective-permute-done.2.x3, ...), custom_call_target="tpu_custom_call" | custom-call | flops 1803886208 | bytes 3000000 | tf_op jit(solution)/shard_map/qkv_own/pallas_call | solution.py:379
  119.5 0.0 collective-permute-done.4.rs0
  119.5 0.0 collective-permute-done.6.rc0
  119.5 0.0 collective-permute-done.5.rs1
  119.5 0.0 copy-start.1
  119.5 8.0 %collective-permute-done.7.rc1 = bf16[3,2,512,256]{3,2,1,0:T(8,128)(2,1)} collective-permute-done((bf16[3,2,512,256]{3,2,1,0:T(8,128)(2,1)}, bf16[3,2,512,256]{3,2,1,0:T(8,128)(2,1)}, u32[]{:S(2)}, u32[]{:S(2)}) %collective-permute-start.7) | collective-permute-done | bytes 1572896 | tf_op jit(solution)/shard_map/ppermute | solution.py:297
  127.5 22.7 %attend.3 = (bf16[512,512]{1,0:T(8,128)(2,1)}, bf16[512,512]{1,0:T(8,128)(2,1)}, bf16[512,512]{1,0:T(8,128)(2,1)}, bf16[512,512]{1,0:T(8,128)(2,1)}) custom-call(s32[19]{0:T(128)} %stack.74.ids, bf16[4,3,2,512,256]{4,3,2,1,0:T(8,128)(2,1)} %qkv_own.1.l_ref, bf16[3,2,512,256]{3,2,1,0:T(8,128)(2,1)} %collective-permute-done.4.rs0, ...), custom_call_target="tpu_custom_call" | custom-call | flops 1000000000 | bytes 650000 | tf_op jit(solution)/shard_map/attend/pallas_call | solution.py:395
  150.3 1.9 collective-permute-start.11
  152.2 0.0 collective-permute-start.12
  152.2 2.1 collective-permute-start.13
  154.3 0.0 collective-permute-start.14
  154.3 23.4 %attend.2 = (bf16[512,512]{1,0:T(8,128)(2,1)}, bf16[512,512]{1,0:T(8,128)(2,1)}, bf16[512,512]{1,0:T(8,128)(2,1)}, bf16[512,512]{1,0:T(8,128)(2,1)}) custom-call(s32[19]{0:T(128)} %stack.74.ids, bf16[4,3,2,512,256]{4,3,2,1,0:T(8,128)(2,1)} %qkv_own.1.l_ref, bf16[3,2,512,256]{3,2,1,0:T(8,128)(2,1)} %collective-permute-done.4.rs0, ...), custom_call_target="tpu_custom_call" | custom-call | flops 1000000000 | bytes 650000 | tf_op jit(solution)/shard_map/attend/pallas_call | solution.py:395
  177.7 0.1 collective-permute-start.10
  177.9 0.0 collective-permute-done.11.refs_2_
  177.9 2.8 %collective-permute-start.8 = (bf16[512,512]{1,0:T(8,128)(2,1)}, bf16[512,512]{1,0:T(8,128)(2,1)}, u32[]{:S(2)}, u32[]{:S(2)}) collective-permute-start(bf16[512,512]{1,0:T(8,128)(2,1)} %get-tuple-element.25), channel_id=1, source_target_pairs={{0,6},{1,7},{2,4},{3,5},{4,2},{5,3},{6,0},{7,1}} | collective-permute-start | bytes 1572872 | tf_op jit(solution)/shard_map/ppermute | solution.py:297
  180.6 0.0 collective-permute-done.12.refs_3_
  180.6 0.0 collective-permute-start.9
  180.7 0.0 collective-permute-done.13.refs_4_
  180.7 0.0 collective-permute-done.14.refs_5_
  180.7 0.0 collective-permute-done.10.refs_1_
  180.7 0.7 copy-done.3
  181.4 0.2 copy-done.4
  181.7 20.4 %project.2.refs_4_ = f32[512,4096]{1,0:T(8,128)} custom-call(s32[19]{0:T(128)} %stack.74.ids, bf16[512,512]{1,0:T(8,128)(2,1)} %get-tuple-element.27.refs_0_, bf16[512,512]{1,0:T(8,128)(2,1)} %collective-permute-done.10.refs_1_, bf16[512,512]{1,0:T(8,128)(2,1)} %copy-done.2, bf16[512,512]{1,0:T(8,128)(2,1)} %copy-done.3, bf16[512,512]{1,0:T(8,128)(2,1)} %copy-done.4, ...), custom_call_target="tpu_custom_call" | custom-call | flops 837518592 | bytes 1660000 | tf_op jit(solution)/shard_map/project/pallas_call | solution.py:427
  202.0 0.0 collective-permute-done.8.refs_0_
  202.0 2.0 collective-permute-done.9.refs_1_
  204.0 12.2 %project.3 = bf16[512,4096]{1,0:T(8,128)(2,1)} custom-call(s32[19]{0:T(128)} %stack.74.ids, bf16[512,512]{1,0:T(8,128)(2,1)} %collective-permute-done.8.refs_0_, bf16[512,512]{1,0:T(8,128)(2,1)} %collective-permute-done.9.refs_1_, bf16[4096,4096]{1,0:T(8,128)(2,1)} %bitcast.25, bf16[4096,4096]{1,0:T(8,128)(2,1)} %bitcast.26, f32[512,4096]{1,0:T(8,128)} %project.2.refs_4_, ...), custom_call_target="tpu_custom_call" | custom-call | flops 279172864 | bytes 820000 | tf_op jit(solution)/shard_map/project/pallas_call | solution.py:427
  (7 shorter events, 0.0 us)
Async XLA Ops:
  0.0 50.1 %collective-permute-start.1 = (bf16[512,4096]{1,0:T(8,128)(2,1)}, bf16[512,4096]{1,0:T(8,128)(2,1)}, u32[]{:S(2)}, u32[]{:S(2)}) collective-permute-start(bf16[512,4096]{1,0:T(8,128)(2,1)} %refs_5_.1), channel_id=1, source_target_pairs={{0,2},{1,5},{2,0},{3,7},{4,6},{5,1},{6,4},{7,3}} | collective-permute-start | bytes 12582920 | tf_op jit(solution)/shard_map/ppermute | solution.py:297
  40.7 15.5 %copy-start = (f32[2,1024,128]{2,1,0:T(8,128)S(1)}, f32[2,1024,128]{2,1,0:T(8,128)}, u32[]{:S(2)}) copy-start(f32[2,1024,128]{2,1,0:T(8,128)} %pad_maximum_fusion.cos_ref.sin_ref.tab_ref) | copy-start | bytes 3145732
  40.7 39.9 %collective-permute-start = (bf16[512,4096]{1,0:T(8,128)(2,1)}, bf16[512,4096]{1,0:T(8,128)(2,1)}, u32[]{:S(2)}, u32[]{:S(2)}) collective-permute-start(bf16[512,4096]{1,0:T(8,128)(2,1)} %get-tuple-element.19.x0), channel_id=1, source_target_pairs={{0,1},{1,0},{2,3},{3,2},{4,5},{5,4},{6,7},{7,6}} | collective-permute-start | bytes 12582920 | tf_op jit(solution)/shard_map/ppermute | solution.py:297
  56.2 24.9 %collective-permute-start.2 = (bf16[512,4096]{1,0:T(8,128)(2,1)}, bf16[512,4096]{1,0:T(8,128)(2,1)}, u32[]{:S(2)}, u32[]{:S(2)}) collective-permute-start(bf16[512,4096]{1,0:T(8,128)(2,1)} %norm.1.x2.xn), channel_id=1, source_target_pairs={{0,1},{1,0},{2,3},{3,2},{4,5},{5,4},{6,7},{7,6}} | collective-permute-start | bytes 12582920 | tf_op jit(solution)/shard_map/ppermute | solution.py:297
  56.2 23.9 %collective-permute-start.3 = (f32[2,1024,128]{2,1,0:T(8,128)S(1)}, f32[2,1024,128]{2,1,0:T(8,128)}, u32[]{:S(2)}, u32[]{:S(2)}) collective-permute-start(f32[2,1024,128]{2,1,0:T(8,128)S(1)} %copy-done), channel_id=1, source_target_pairs={{0,1},{1,0},{2,3},{3,2},{4,5},{5,4},{6,7},{7,6}} | collective-permute-start | bytes 3145736 | tf_op jit(solution)/shard_map/ppermute | solution.py:297
  56.7 62.8 %collective-permute-start.4 = (bf16[3,2,512,256]{3,2,1,0:T(8,128)(2,1)}, bf16[3,2,512,256]{3,2,1,0:T(8,128)(2,1)}, u32[]{:S(2)}, u32[]{:S(2)}) collective-permute-start(bf16[3,2,512,256]{3,2,1,0:T(8,128)(2,1)} %get-tuple-element.20), channel_id=1, source_target_pairs={{0,4},{1,3},{2,6},{3,1},{4,0},{5,7},{6,2},{7,5}} | collective-permute-start | bytes 4718600 | tf_op jit(solution)/shard_map/ppermute | solution.py:297
  58.7 60.8 %collective-permute-start.6 = (bf16[3,2,512,256]{3,2,1,0:T(8,128)(2,1)}, bf16[3,2,512,256]{3,2,1,0:T(8,128)(2,1)}, u32[]{:S(2)}, u32[]{:S(2)}) collective-permute-start(bf16[3,2,512,256]{3,2,1,0:T(8,128)(2,1)} %get-tuple-element.23), channel_id=1, source_target_pairs={{0,5},{1,2},{2,7},{3,0},{4,1},{5,6},{6,3},{7,4}} | collective-permute-start | bytes 4718600 | tf_op jit(solution)/shard_map/ppermute | solution.py:297
  80.1 39.4 %collective-permute-start.5 = (bf16[3,2,512,256]{3,2,1,0:T(8,128)(2,1)}, bf16[3,2,512,256]{3,2,1,0:T(8,128)(2,1)S(1)}, u32[]{:S(2)}, u32[]{:S(2)}) collective-permute-start(bf16[3,2,512,256]{3,2,1,0:T(8,128)(2,1)} %get-tuple-element.22), channel_id=1, source_target_pairs={{0,4},{1,3},{2,6},{3,1},{4,0},{5,7},{6,2},{7,5}} | collective-permute-start | bytes 4718600 | tf_op jit(solution)/shard_map/ppermute | solution.py:297
  80.6 46.9 %collective-permute-start.7 = (bf16[3,2,512,256]{3,2,1,0:T(8,128)(2,1)}, bf16[3,2,512,256]{3,2,1,0:T(8,128)(2,1)}, u32[]{:S(2)}, u32[]{:S(2)}) collective-permute-start(bf16[3,2,512,256]{3,2,1,0:T(8,128)(2,1)} %get-tuple-element.24), channel_id=1, source_target_pairs={{0,5},{1,2},{2,7},{3,0},{4,1},{5,6},{6,3},{7,4}} | collective-permute-start | bytes 4718600 | tf_op jit(solution)/shard_map/ppermute | solution.py:297
  119.5 8.0 %copy-start.1 = (bf16[3,2,512,256]{3,2,1,0:T(8,128)(2,1)}, bf16[3,2,512,256]{3,2,1,0:T(8,128)(2,1)S(1)}, u32[]{:S(2)}) copy-start(bf16[3,2,512,256]{3,2,1,0:T(8,128)(2,1)S(1)} %collective-permute-done.5.rs1) | copy-start | bytes 4718596
  150.3 27.6 %collective-permute-start.11 = (bf16[512,512]{1,0:T(8,128)(2,1)}, bf16[512,512]{1,0:T(8,128)(2,1)S(1)}, u32[]{:S(2)}, u32[]{:S(2)}) collective-permute-start(bf16[512,512]{1,0:T(8,128)(2,1)} %get-tuple-element.29), channel_id=1, source_target_pairs={{0,2},{1,3},{2,0},{3,1},{4,6},{5,7},{6,4},{7,5}} | collective-permute-start | bytes 1572872 | tf_op jit(solution)/shard_map/ppermute | solution.py:297
  152.2 28.5 %collective-permute-start.12 = (bf16[512,512]{1,0:T(8,128)(2,1)}, bf16[512,512]{1,0:T(8,128)(2,1)S(1)}, u32[]{:S(2)}, u32[]{:S(2)}) collective-permute-start(bf16[512,512]{1,0:T(8,128)(2,1)} %get-tuple-element.30), channel_id=1, source_target_pairs={{0,3},{1,2},{2,1},{3,0},{4,7},{5,6},{6,5},{7,4}} | collective-permute-start | bytes 1572872 | tf_op jit(solution)/shard_map/ppermute | solution.py:297
  152.2 28.5 %collective-permute-start.13 = (bf16[512,512]{1,0:T(8,128)(2,1)}, bf16[512,512]{1,0:T(8,128)(2,1)S(1)}, u32[]{:S(2)}, u32[]{:S(2)}) collective-permute-start(bf16[512,512]{1,0:T(8,128)(2,1)} %get-tuple-element.31), channel_id=1, source_target_pairs={{0,4},{1,5},{2,6},{3,7},{4,0},{5,1},{6,2},{7,3}} | collective-permute-start | bytes 1572872 | tf_op jit(solution)/shard_map/ppermute | solution.py:297
  154.3 26.3 %collective-permute-start.14 = (bf16[512,512]{1,0:T(8,128)(2,1)}, bf16[512,512]{1,0:T(8,128)(2,1)}, u32[]{:S(2)}, u32[]{:S(2)}) collective-permute-start(bf16[512,512]{1,0:T(8,128)(2,1)} %get-tuple-element.32), channel_id=1, source_target_pairs={{0,5},{1,4},{2,7},{3,6},{4,1},{5,0},{6,3},{7,2}} | collective-permute-start | bytes 1572872 | tf_op jit(solution)/shard_map/ppermute | solution.py:297
  177.7 2.9 %collective-permute-start.10 = (bf16[512,512]{1,0:T(8,128)(2,1)}, bf16[512,512]{1,0:T(8,128)(2,1)}, u32[]{:S(2)}, u32[]{:S(2)}) collective-permute-start(bf16[512,512]{1,0:T(8,128)(2,1)} %get-tuple-element.28), channel_id=1, source_target_pairs={{0,1},{1,0},{2,3},{3,2},{4,5},{5,4},{6,7},{7,6}} | collective-permute-start | bytes 1572872 | tf_op jit(solution)/shard_map/ppermute | solution.py:297
  177.9 2.8 %copy-start.2 = (bf16[512,512]{1,0:T(8,128)(2,1)}, bf16[512,512]{1,0:T(8,128)(2,1)S(1)}, u32[]{:S(2)}) copy-start(bf16[512,512]{1,0:T(8,128)(2,1)S(1)} %collective-permute-done.11.refs_2_) | copy-start | bytes 1572868
  177.9 24.1 %collective-permute-start.8 = (bf16[512,512]{1,0:T(8,128)(2,1)}, bf16[512,512]{1,0:T(8,128)(2,1)}, u32[]{:S(2)}, u32[]{:S(2)}) collective-permute-start(bf16[512,512]{1,0:T(8,128)(2,1)} %get-tuple-element.25), channel_id=1, source_target_pairs={{0,6},{1,7},{2,4},{3,5},{4,2},{5,3},{6,0},{7,1}} | collective-permute-start | bytes 1572872 | tf_op jit(solution)/shard_map/ppermute | solution.py:297
  180.6 0.8 copy-start.3
  180.6 23.3 %collective-permute-start.9 = (bf16[512,512]{1,0:T(8,128)(2,1)}, bf16[512,512]{1,0:T(8,128)(2,1)}, u32[]{:S(2)}, u32[]{:S(2)}) collective-permute-start(bf16[512,512]{1,0:T(8,128)(2,1)} %get-tuple-element.26), channel_id=1, source_target_pairs={{0,7},{1,6},{2,5},{3,4},{4,3},{5,2},{6,1},{7,0}} | collective-permute-start | bytes 1572872 | tf_op jit(solution)/shard_map/ppermute | solution.py:297
  180.7 1.0 copy-start.4

commit v2 on v1

--- a/solution.py
+++ b/solution.py
@@ -11,7 +11,9 @@
 BF = jnp.bfloat16
 F32 = jnp.float32
 VMEM_LIMIT = 62 << 20
+PROJ_VMEM = 40 << 20
 COST = 0.05
+TN0, TN1 = 1024, 1024
 GROUPS = ((2, 4), (6, 0))
 ME, B_HEAD, OWN_HEAD, SRC, DEV = 0, 1, 2, 3, 11
 
@@ -169,17 +171,26 @@
         rows = pl.ds(pl.multiple_of(b * t, t), t)
         return pltpu.make_async_copy(src[n].at[0], qkv.at[0, :, rows, :], sem.at[1, b])
 
-    for n in range(8):
-        b = ids[SRC + n]
-        want = functools.reduce(jnp.logical_or, [b // 2 == cc for cc in chips])
-
-        @pl.when(want)
+    def issue(want_chip, queries):
+        for n in range(8):
+            b = ids[SRC + n]
+
+            @pl.when(b // 2 == want_chip)
+            def _():
+                if queries:
+                    q_copy(n, b).start()
+                else:
+                    kv_copy(n, b).start()
+
+    issue(chips[0], True)
+    for j in range(4):
+        @pl.when(j <= last)
         def _():
-            q_copy(n, b).start()
-
-        @pl.when(b // 2 <= last)
-        def _():
-            kv_copy(n, b).start()
+            issue(j, False)
+
+        if j == 0:
+            for cc in chips[1:]:
+                issue(cc, True)
 
     k2 = (dh ** -0.5) * 1.4426950408889634
 
@@ -259,24 +270,21 @@
     lax.fori_loop(0, nq, chip_rows, 0)
 
 
-def _out_first(ids, *refs):
-    n = (len(refs) - 1) // 2
+def _project(n, ids, *refs):
     o = jnp.concatenate([r[...] for r in refs[:n]], axis=1)
     w = jnp.concatenate([r[...] for r in refs[n:2 * n]], axis=0)
-    refs[-1][...] = jnp.dot(o, w, preferred_element_type=F32)
-
-
-def _out_last(ids, *refs):
-    n = (len(refs) - 3) // 2
-    o = jnp.concatenate([r[...] for r in refs[:n]], axis=1)
-    w = jnp.concatenate([r[...] for r in refs[n:2 * n]], axis=0)
-    part, x, out = refs[2 * n], refs[2 * n + 1], refs[-1]
-    a = part[...] + jnp.dot(o, w, preferred_element_type=F32)
-    out[...] = (x[...].astype(F32) + a).astype(BF)
-
-
-def _params(**kw):
-    return pltpu.CompilerParams(vmem_limit_bytes=VMEM_LIMIT, **kw)
+    base, out = refs[2 * n], refs[2 * n + 1]
+    tn = w.shape[1]
+    cols = pl.ds(pl.multiple_of(pl.program_id(0) * tn, tn), tn)
+    a = jnp.dot(o, w, preferred_element_type=F32)
+    if out.shape[1] == tn:
+        out[...] = (base[:, cols] + a).astype(BF)
+    else:
+        out[:, cols] = base[...].astype(F32) + a
+
+
+def _params(limit=VMEM_LIMIT):
+    return pltpu.CompilerParams(vmem_limit_bytes=limit)
 
 
 def _cost(flops, nbytes):
@@ -414,29 +422,29 @@
                     got[v] = send(o[2 * i + e], lambda j, v=v: j ^ v) if v else o[2 * i + e]
 
         wo2 = wo.reshape(hh * dh, d)
-        tn = 1024
         o_spec = pl.BlockSpec((t, 2 * dh), lambda i, s: (0, 0))
 
-        def w_spec(m):
-            return pl.BlockSpec((2 * dh, tn), lambda i, s: (s[DEV + m], i))
-
-        def project(ms, part=None):
+        def project(tn, ms, part=None):
             n = len(ms)
+
+            def w_spec(m):
+                return pl.BlockSpec((2 * dh, tn), lambda i, s: (s[DEV + m], i))
+
             col = pl.BlockSpec((t, tn), lambda i, s: (0, i))
-            extra = [] if part is None else [part, x]
+            kept = pl.BlockSpec(memory_space=pltpu.VMEM)
             return pl.pallas_call(
-                _out_first if part is None else _out_last,
+                functools.partial(_project, n),
                 grid_spec=pltpu.PrefetchScalarGridSpec(
                     num_scalar_prefetch=1, grid=(d // tn,),
-                    in_specs=[o_spec] * n + [w_spec(m) for m in ms] + [col] * len(extra),
-                    out_specs=col),
-                out_shape=jax.ShapeDtypeStruct((t, d), F32 if part is None else BF),
-                compiler_params=_params(), cost_estimate=_cost(n * 2 * t * 2 * dh * d * 1.3, n * 4.2e6 + 8e6),
+                    in_specs=[o_spec] * n + [w_spec(m) for m in ms] + [col if part is None else kept],
+                    out_specs=kept if part is None else col),
+                out_shape=pltpu.VMEM((t, d), F32) if part is None else jax.ShapeDtypeStruct((t, d), BF),
+                compiler_params=_params(PROJ_VMEM), cost_estimate=_cost(n * 2 * t * 2 * dh * d * 1.3, n * 4.2e6 + 8e6),
                 name="project",
-            )(ids, *[got[m] for m in ms], *[wo2] * n, *extra)
-
-        part = project((0, 1, 2, 3, 4, 5))
-        return project((6, 7), part)
+            )(ids, *[got[m] for m in ms], *[wo2] * n, x if part is None else part)
+
+        part = project(TN0, (0, 1, 2, 3, 4, 5))
+        return project(TN1, (6, 7), part)
 
     return jax.shard_map(local, mesh=mesh,
                          in_specs=(rows, P(None), P(None, None, None, None), P(None, None, None)),

time: 217 us -> 209 us (0.963)
  Pallas kernels: 177 us -> 169 us
    pallas_call x2, Pallas kernels: 32.6 us -> 27.8 us  [project(): pl.pallas_call(functools.partial(_project, n), grid_spec=pltpu.PrefetchSc...]
    pallas_call x2, Pallas kernels: 46.1 us -> 42.5 us  [attend(): pl.pallas_call(functools.partial(_attend, ms), grid_spec=pltpu.PrefetchSc...]
  transfers between devices with their start and end apart: 15 -> 15, of which waited for: 3 -> 3; matrix products, arithmetic and copies ran while one was open for 2% -> 2% of each run, Pallas kernels for 66% -> 67%
where the time goes in v2:
time: 209 us
  Pallas kernels  169 us (81%)
  waiting for transfers between devices  20.2 us (10%)
  starting transfers between devices  14.7 us (7%)
  other arithmetic  3.09 us (1%)
    pallas_call x2, Pallas kernels, attend(): pl.pallas_call(functools.partial(_attend, ms), grid_spec=pltpu.PrefetchSc...  42.5 us
    pallas_call x1, Pallas kernels, local(): pl.pallas_call(_qkv_own, grid_spec=pltpu.PrefetchScalarGridSpec(num_scala...  38.5 us
    pallas_call x1, Pallas kernels, local(): pl.pallas_call(_qkv_first, grid_spec=pltpu.PrefetchScalarGridSpec(num_sca...  33.6 us
    pallas_call x2, Pallas kernels, project(): pl.pallas_call(functools.partial(_project, n), grid_spec=pltpu.PrefetchSc...  27.8 us
    pallas_call x1, Pallas kernels, local(): pl.pallas_call(_qkv_next, grid_spec=pltpu.PrefetchScalarGridSpec(num_scal...  20.5 us
    ppermute x15, waiting for transfers between devices, send(): return lax.ppermute(a, 'seq', [(i, f(i)) for i in range(8)])  20.2 us
    ppermute x15, starting transfers between devices, send(): return lax.ppermute(a, 'seq', [(i, f(i)) for i in range(8)])  14.7 us
    pallas_call x1, Pallas kernels, local(): pl.pallas_call(_norm_rows, grid=(t // rb,), in_specs=[pl.BlockSpec((rb, d...  6.06 us
  transfers between devices with their start and end apart: 15, of which 3 were waited for; matrix products, arithmetic and copies ran while one was open for 2% of the time, Pallas kernels for 67%

profile of v2, /device:TPU:0, one launch (start us, length us, event | category | flops | bytes accessed | tf_op | source)
XLA Modules:
  0.0 208.7 jit_solution(3427568887368753901)
XLA Ops:
  0.0 3.3 %collective-permute-start.1 = (bf16[512,4096]{1,0:T(8,128)(2,1)}, bf16[512,4096]{1,0:T(8,128)(2,1)}, u32[]{:S(2)}, u32[]{:S(2)}) collective-permute-start(bf16[512,4096]{1,0:T(8,128)(2,1)} %refs_12_.1), channel_id=1, source_target_pairs={{0,2},{1,5},{2,0},{3,7},{4,6},{5,1},{6,4},{7,3}} | collective-permute-start | bytes 12582920 | tf_op jit(solution)/shard_map/ppermute | solution.py:305
  3.3 0.1 add_multiply_fusion
  3.4 0.1 convert_bitcast_fusion
  3.5 0.6 stack.74.ids
  4.1 1.9 multiply_cosine_fusion
  6.0 1.0 pad_maximum_fusion.cos_ref.sin_ref.tab_ref
  7.0 33.6 %qkv_first.1 = (bf16[3,2,512,256]{3,2,1,0:T(8,128)(2,1)}, bf16[3,2,512,256]{3,2,1,0:T(8,128)(2,1)}, bf16[3,4096,1024]{2,1,0:T(8,128)(2,1)}, bf16[512,4096]{1,0:T(8,128)(2,1)}) custom-call(s32[19]{0:T(128)} %stack.74.ids, bf16[512,4096]{1,0:T(8,128)(2,1)} %refs_12_.1, f32[1,4096]{1,0:T(1,128)} %bitcast.27, bf16[4096,3,16,256]{3,2,1,0:T(8,128)(2,1)} %w_ref.3, ...), custom_call_target="tpu_custom_call" | custom-call | flops 1610612736 | bytes 4000000 | tf_op jit(solution)/shard_map/qkv_first/pallas_call | solution.py:353
  40.6 0.0 copy-start.2
  40.7 0.0 collective-permute-start
  40.7 9.4 %collective-permute-done.1.x_ref = bf16[512,4096]{1,0:T(8,128)(2,1)} collective-permute-done((bf16[512,4096]{1,0:T(8,128)(2,1)}, bf16[512,4096]{1,0:T(8,128)(2,1)}, u32[]{:S(2)}, u32[]{:S(2)}) %collective-permute-start.1) | collective-permute-done | bytes 4194336 | tf_op jit(solution)/shard_map/ppermute | solution.py:305
  50.1 6.1 %norm.1.x2.xn = bf16[512,4096]{1,0:T(8,128)(2,1)} custom-call(bf16[512,4096]{1,0:T(8,128)(2,1)} %collective-permute-done.1.x_ref, f32[1,4096]{1,0:T(1,128)} %bitcast.28), custom_call_target="tpu_custom_call" | custom-call | flops 100000000 | bytes 400000 | tf_op jit(solution)/shard_map/norm/pallas_call | solution.py:367
  56.2 0.0 collective-permute-start.2
  56.2 0.0 copy-done.2
  56.2 0.5 collective-permute-start.3
  56.7 2.1 collective-permute-start.4
  58.7 0.8 collective-permute-start.6
  59.6 20.5 %qkv_next.1 = (bf16[3,2,512,256]{3,2,1,0:T(8,128)(2,1)}, bf16[3,2,512,256]{3,2,1,0:T(8,128)(2,1)}) custom-call(s32[19]{0:T(128)} %stack.74.ids, bf16[512,4096]{1,0:T(8,128)(2,1)} %norm.1.x2.xn, bf16[3,4096,1024]{2,1,0:T(8,128)(2,1)} %get-tuple-element.21.w_ref, f32[2,1024,128]{2,1,0:T(8,128)} %pad_maximum_fusion.cos_ref.sin_ref.tab_ref, ...), custom_call_target="tpu_custom_call" | custom-call | flops 901943104 | bytes 1750000 | tf_op jit(solution)/shard_map/qkv_next/pallas_call | solution.py:374
  80.1 0.0 collective-permute-done.3.ptab_ref
  80.1 0.5 collective-permute-start.5
  80.6 0.0 collective-permute-done.x1
  80.6 0.4 collective-permute-start.7
  81.0 0.0 collective-permute-done.2.x3
  81.0 38.5 %qkv_own.1.l_ref = bf16[4,3,2,512,256]{4,3,2,1,0:T(8,128)(2,1)} custom-call(s32[19]{0:T(128)} %stack.74.ids, bf16[512,4096]{1,0:T(8,128)(2,1)} %get-tuple-element.19.x0, bf16[512,4096]{1,0:T(8,128)(2,1)} %collective-permute-done.x1, bf16[512,4096]{1,0:T(8,128)(2,1)} %norm.1.x2.xn, bf16[512,4096]{1,0:T(8,128)(2,1)} %collective-permute-done.2.x3, ...), custom_call_target="tpu_custom_call" | custom-call | flops 1803886208 | bytes 3000000 | tf_op jit(solution)/shard_map/qkv_own/pallas_call | solution.py:387
  119.5 0.0 collective-permute-done.4.rs0
  119.5 0.0 collective-permute-done.6.rc0
  119.6 0.0 collective-permute-done.5.rs1
  119.6 0.0 copy-start.3
  119.6 8.0 %collective-permute-done.7.rc1 = bf16[3,2,512,256]{3,2,1,0:T(8,128)(2,1)} collective-permute-done((bf16[3,2,512,256]{3,2,1,0:T(8,128)(2,1)}, bf16[3,2,512,256]{3,2,1,0:T(8,128)(2,1)}, u32[]{:S(2)}, u32[]{:S(2)}) %collective-permute-start.7) | collective-permute-done | bytes 1572896 | tf_op jit(solution)/shard_map/ppermute | solution.py:305
  127.5 0.0 copy-done.3
  127.5 21.2 %attend.3 = (bf16[512,512]{1,0:T(8,128)(2,1)}, bf16[512,512]{1,0:T(8,128)(2,1)}, bf16[512,512]{1,0:T(8,128)(2,1)}, bf16[512,512]{1,0:T(8,128)(2,1)}) custom-call(s32[19]{0:T(128)} %stack.74.ids, bf16[4,3,2,512,256]{4,3,2,1,0:T(8,128)(2,1)} %qkv_own.1.l_ref, bf16[3,2,512,256]{3,2,1,0:T(8,128)(2,1)} %collective-permute-done.4.rs0, ...), custom_call_target="tpu_custom_call" | custom-call | flops 1000000000 | bytes 650000 | tf_op jit(solution)/shard_map/attend/pallas_call | solution.py:403
  148.8 1.5 collective-permute-start.11
  150.3 0.4 collective-permute-start.12
  150.7 1.7 collective-permute-start.13
  152.5 0.0 collective-permute-start.14
  152.5 21.3 %attend.2 = (bf16[512,512]{1,0:T(8,128)(2,1)}, bf16[512,512]{1,0:T(8,128)(2,1)}, bf16[512,512]{1,0:T(8,128)(2,1)}, bf16[512,512]{1,0:T(8,128)(2,1)}) custom-call(s32[19]{0:T(128)} %stack.74.ids, bf16[4,3,2,512,256]{4,3,2,1,0:T(8,128)(2,1)} %qkv_own.1.l_ref, bf16[3,2,512,256]{3,2,1,0:T(8,128)(2,1)} %collective-permute-done.4.rs0, ...), custom_call_target="tpu_custom_call" | custom-call | flops 1000000000 | bytes 650000 | tf_op jit(solution)/shard_map/attend/pallas_call | solution.py:403
  173.8 0.4 collective-permute-start.10
  174.1 0.0 collective-permute-done.11.refs_2_
  174.1 2.7 %collective-permute-start.8 = (bf16[512,512]{1,0:T(8,128)(2,1)}, bf16[512,512]{1,0:T(8,128)(2,1)S(1)}, u32[]{:S(2)}, u32[]{:S(2)}) collective-permute-start(bf16[512,512]{1,0:T(8,128)(2,1)} %get-tuple-element.25), channel_id=1, source_target_pairs={{0,6},{1,7},{2,4},{3,5},{4,2},{5,3},{6,0},{7,1}} | collective-permute-start | bytes 1572872 | tf_op jit(solution)/shard_map/ppermute | solution.py:305
  176.8 0.0 collective-permute-done.12.refs_3_
  176.8 0.3 collective-permute-start.9
  177.1 0.0 collective-permute-done.13.refs_4_
  177.1 0.0 collective-permute-done.14.refs_5_
  177.1 0.0 collective-permute-done.10.refs_1_
  177.2 1.0 copy-done
  178.2 18.8 %project.2.refs_4_ = f32[512,4096]{1,0:T(8,128)S(1)} custom-call(s32[19]{0:T(128)S(1)} %copy-done.1, bf16[512,512]{1,0:T(8,128)(2,1)S(1)} %copy-done, bf16[512,512]{1,0:T(8,128)(2,1)S(1)} %collective-permute-done.10.refs_1_, bf16[512,512]{1,0:T(8,128)(2,1)S(1)} %collective-permute-done.11.refs_2_, bf16[512,512]{1,0:T(8,128)(2,1)S(1)} %collective-permute-done.12.refs_3_, ...), custom_call_target="tpu_custom_call" | custom-call | flops 837518592 | bytes 1660000 | tf_op jit(solution)/shard_map/project/pallas_call | solution.py:435
  197.0 0.0 collective-permute-done.8.refs_0_
  197.0 2.8 %collective-permute-done.9.refs_1_ = bf16[512,512]{1,0:T(8,128)(2,1)S(1)} collective-permute-done((bf16[512,512]{1,0:T(8,128)(2,1)}, bf16[512,512]{1,0:T(8,128)(2,1)S(1)}, u32[]{:S(2)}, u32[]{:S(2)}) %collective-permute-start.9) | collective-permute-done | bytes 524320 | tf_op jit(solution)/shard_map/ppermute | solution.py:305
  199.8 9.0 %project.3 = bf16[512,4096]{1,0:T(8,128)(2,1)} custom-call(s32[19]{0:T(128)S(1)} %copy-done.1, bf16[512,512]{1,0:T(8,128)(2,1)S(1)} %collective-permute-done.8.refs_0_, bf16[512,512]{1,0:T(8,128)(2,1)S(1)} %collective-permute-done.9.refs_1_, bf16[4096,4096]{1,0:T(8,128)(2,1)} %bitcast.25, bf16[4096,4096]{1,0:T(8,128)(2,1)} %bitcast.26, ...), custom_call_target="tpu_custom_call" | custom-call | flops 279172864 | bytes 820000 | tf_op jit(solution)/shard_map/project/pallas_call | solution.py:435
  (5 shorter events, 0.0 us)
Async XLA Ops:
  0.0 50.1 %collective-permute-start.1 = (bf16[512,4096]{1,0:T(8,128)(2,1)}, bf16[512,4096]{1,0:T(8,128)(2,1)}, u32[]{:S(2)}, u32[]{:S(2)}) collective-permute-start(bf16[512,4096]{1,0:T(8,128)(2,1)} %refs_12_.1), channel_id=1, source_target_pairs={{0,2},{1,5},{2,0},{3,7},{4,6},{5,1},{6,4},{7,3}} | collective-permute-start | bytes 12582920 | tf_op jit(solution)/shard_map/ppermute | solution.py:305
  40.6 15.5 %copy-start.2 = (f32[2,1024,128]{2,1,0:T(8,128)S(1)}, f32[2,1024,128]{2,1,0:T(8,128)}, u32[]{:S(2)}) copy-start(f32[2,1024,128]{2,1,0:T(8,128)} %pad_maximum_fusion.cos_ref.sin_ref.tab_ref) | copy-start | bytes 3145732
  40.7 39.9 %collective-permute-start = (bf16[512,4096]{1,0:T(8,128)(2,1)}, bf16[512,4096]{1,0:T(8,128)(2,1)}, u32[]{:S(2)}, u32[]{:S(2)}) collective-permute-start(bf16[512,4096]{1,0:T(8,128)(2,1)} %get-tuple-element.19.x0), channel_id=1, source_target_pairs={{0,1},{1,0},{2,3},{3,2},{4,5},{5,4},{6,7},{7,6}} | collective-permute-start | bytes 12582920 | tf_op jit(solution)/shard_map/ppermute | solution.py:305
  56.2 24.9 %collective-permute-start.2 = (bf16[512,4096]{1,0:T(8,128)(2,1)}, bf16[512,4096]{1,0:T(8,128)(2,1)}, u32[]{:S(2)}, u32[]{:S(2)}) collective-permute-start(bf16[512,4096]{1,0:T(8,128)(2,1)} %norm.1.x2.xn), channel_id=1, source_target_pairs={{0,1},{1,0},{2,3},{3,2},{4,5},{5,4},{6,7},{7,6}} | collective-permute-start | bytes 12582920 | tf_op jit(solution)/shard_map/ppermute | solution.py:305
  56.2 23.9 %collective-permute-start.3 = (f32[2,1024,128]{2,1,0:T(8,128)S(1)}, f32[2,1024,128]{2,1,0:T(8,128)}, u32[]{:S(2)}, u32[]{:S(2)}) collective-permute-start(f32[2,1024,128]{2,1,0:T(8,128)S(1)} %copy-done.2), channel_id=1, source_target_pairs={{0,1},{1,0},{2,3},{3,2},{4,5},{5,4},{6,7},{7,6}} | collective-permute-start | bytes 3145736 | tf_op jit(solution)/shard_map/ppermute | solution.py:305
  56.7 62.9 %collective-permute-start.4 = (bf16[3,2,512,256]{3,2,1,0:T(8,128)(2,1)}, bf16[3,2,512,256]{3,2,1,0:T(8,128)(2,1)}, u32[]{:S(2)}, u32[]{:S(2)}) collective-permute-start(bf16[3,2,512,256]{3,2,1,0:T(8,128)(2,1)} %get-tuple-element.20), channel_id=1, source_target_pairs={{0,4},{1,3},{2,6},{3,1},{4,0},{5,7},{6,2},{7,5}} | collective-permute-start | bytes 4718600 | tf_op jit(solution)/shard_map/ppermute | solution.py:305
  58.7 60.8 %collective-permute-start.6 = (bf16[3,2,512,256]{3,2,1,0:T(8,128)(2,1)}, bf16[3,2,512,256]{3,2,1,0:T(8,128)(2,1)}, u32[]{:S(2)}, u32[]{:S(2)}) collective-permute-start(bf16[3,2,512,256]{3,2,1,0:T(8,128)(2,1)} %get-tuple-element.23), channel_id=1, source_target_pairs={{0,5},{1,2},{2,7},{3,0},{4,1},{5,6},{6,3},{7,4}} | collective-permute-start | bytes 4718600 | tf_op jit(solution)/shard_map/ppermute | solution.py:305
  80.1 39.5 %collective-permute-start.5 = (bf16[3,2,512,256]{3,2,1,0:T(8,128)(2,1)}, bf16[3,2,512,256]{3,2,1,0:T(8,128)(2,1)S(1)}, u32[]{:S(2)}, u32[]{:S(2)}) collective-permute-start(bf16[3,2,512,256]{3,2,1,0:T(8,128)(2,1)} %get-tuple-element.22), channel_id=1, source_target_pairs={{0,4},{1,3},{2,6},{3,1},{4,0},{5,7},{6,2},{7,5}} | collective-permute-start | bytes 4718600 | tf_op jit(solution)/shard_map/ppermute | solution.py:305
  80.6 46.9 %collective-permute-start.7 = (bf16[3,2,512,256]{3,2,1,0:T(8,128)(2,1)}, bf16[3,2,512,256]{3,2,1,0:T(8,128)(2,1)}, u32[]{:S(2)}, u32[]{:S(2)}) collective-permute-start(bf16[3,2,512,256]{3,2,1,0:T(8,128)(2,1)} %get-tuple-element.24), channel_id=1, source_target_pairs={{0,5},{1,2},{2,7},{3,0},{4,1},{5,6},{6,3},{7,4}} | collective-permute-start | bytes 4718600 | tf_op jit(solution)/shard_map/ppermute | solution.py:305
  119.6 8.0 %copy-start.3 = (bf16[3,2,512,256]{3,2,1,0:T(8,128)(2,1)}, bf16[3,2,512,256]{3,2,1,0:T(8,128)(2,1)S(1)}, u32[]{:S(2)}) copy-start(bf16[3,2,512,256]{3,2,1,0:T(8,128)(2,1)S(1)} %collective-permute-done.5.rs1) | copy-start | bytes 4718596
  148.8 25.4 %collective-permute-start.11 = (bf16[512,512]{1,0:T(8,128)(2,1)}, bf16[512,512]{1,0:T(8,128)(2,1)S(1)}, u32[]{:S(2)}, u32[]{:S(2)}) collective-permute-start(bf16[512,512]{1,0:T(8,128)(2,1)} %get-tuple-element.29), channel_id=1, source_target_pairs={{0,2},{1,3},{2,0},{3,1},{4,6},{5,7},{6,4},{7,5}} | collective-permute-start | bytes 1572872 | tf_op jit(solution)/shard_map/ppermute | solution.py:305
  150.3 26.5 %collective-permute-start.12 = (bf16[512,512]{1,0:T(8,128)(2,1)}, bf16[512,512]{1,0:T(8,128)(2,1)S(1)}, u32[]{:S(2)}, u32[]{:S(2)}) collective-permute-start(bf16[512,512]{1,0:T(8,128)(2,1)} %get-tuple-element.30), channel_id=1, source_target_pairs={{0,3},{1,2},{2,1},{3,0},{4,7},{5,6},{6,5},{7,4}} | collective-permute-start | bytes 1572872 | tf_op jit(solution)/shard_map/ppermute | solution.py:305
  150.7 26.4 %collective-permute-start.13 = (bf16[512,512]{1,0:T(8,128)(2,1)}, bf16[512,512]{1,0:T(8,128)(2,1)S(1)}, u32[]{:S(2)}, u32[]{:S(2)}) collective-permute-start(bf16[512,512]{1,0:T(8,128)(2,1)} %get-tuple-element.31), channel_id=1, source_target_pairs={{0,4},{1,5},{2,6},{3,7},{4,0},{5,1},{6,2},{7,3}} | collective-permute-start | bytes 1572872 | tf_op jit(solution)/shard_map/ppermute | solution.py:305
  152.5 24.7 %copy-start.1 = (s32[19]{0:T(128)S(1)}, s32[19]{0:T(128)}, u32[]{:S(2)}) copy-start(s32[19]{0:T(128)} %stack.74.ids) | copy-start | bytes 232
  152.5 24.7 %collective-permute-start.14 = (bf16[512,512]{1,0:T(8,128)(2,1)}, bf16[512,512]{1,0:T(8,128)(2,1)}, u32[]{:S(2)}, u32[]{:S(2)}) collective-permute-start(bf16[512,512]{1,0:T(8,128)(2,1)} %get-tuple-element.32), channel_id=1, source_target_pairs={{0,5},{1,4},{2,7},{3,6},{4,1},{5,0},{6,3},{7,2}} | collective-permute-start | bytes 1572872 | tf_op jit(solution)/shard_map/ppermute | solution.py:305
  173.8 3.3 %collective-permute-start.10 = (bf16[512,512]{1,0:T(8,128)(2,1)}, bf16[512,512]{1,0:T(8,128)(2,1)S(1)}, u32[]{:S(2)}, u32[]{:S(2)}) collective-permute-start(bf16[512,512]{1,0:T(8,128)(2,1)} %get-tuple-element.28), channel_id=1, source_target_pairs={{0,1},{1,0},{2,3},{3,2},{4,5},{5,4},{6,7},{7,6}} | collective-permute-start | bytes 1572872 | tf_op jit(solution)/shard_map/ppermute | solution.py:305
  174.1 22.8 %collective-permute-start.8 = (bf16[512,512]{1,0:T(8,128)(2,1)}, bf16[512,512]{1,0:T(8,128)(2,1)S(1)}, u32[]{:S(2)}, u32[]{:S(2)}) collective-permute-start(bf16[512,512]{1,0:T(8,128)(2,1)} %get-tuple-element.25), channel_id=1, source_target_pairs={{0,6},{1,7},{2,4},{3,5},{4,2},{5,3},{6,0},{7,1}} | collective-permute-start | bytes 1572872 | tf_op jit(solution)/shard_map/ppermute | solution.py:305
  176.8 22.9 %collective-permute-start.9 = (bf16[512,512]{1,0:T(8,128)(2,1)}, bf16[512,512]{1,0:T(8,128)(2,1)S(1)}, u32[]{:S(2)}, u32[]{:S(2)}) collective-permute-start(bf16[512,512]{1,0:T(8,128)(2,1)} %get-tuple-element.26), channel_id=1, source_target_pairs={{0,7},{1,6},{2,5},{3,4},{4,3},{5,2},{6,1},{7,0}} | collective-permute-start | bytes 1572872 | tf_op jit(solution)/shard_map/ppermute | solution.py:305
  177.1 1.0 copy-start

commit v3 on v2

--- a/solution.py
+++ b/solution.py
@@ -76,10 +76,12 @@
     return take
 
 
-def _qkv_first(ids, x_ref, g_ref, w_ref, cos_ref, sin_ref, s_ref, c_ref, wr_ref, xn, acc, buf, wsem):
+def _qkv_first(ids, x_ref, g_ref, w_ref, cos_ref, sin_ref, s_ref, c_ref, o_ref, wr_ref, xn, acc, acc2, wt,
+               buf, wsem, buf2, wsem2):
     c, d = pl.program_id(0), pl.program_id(1)
     bd = buf.shape[1]
     take = _stream(w_ref, buf, wsem, ids[B_HEAD])
+    take2 = _stream(w_ref, buf2, wsem2, ids[OWN_HEAD])
 
     @pl.when((c == 0) & (d == 0))
     def _():
@@ -88,10 +90,13 @@
     @pl.when(d == 0)
     def _():
         acc[...] = jnp.zeros_like(acc)
+        acc2[...] = jnp.zeros_like(acc2)
 
     wr_ref[0] = take()
     xb = xn[:, pl.ds(pl.multiple_of(d * bd, bd), bd)]
     acc[...] += jnp.dot(xb, wr_ref[0], preferred_element_type=F32)
+    wt[...] = take2()
+    acc2[...] += jnp.dot(xb, wt[...], preferred_element_type=F32)
 
     @pl.when(d == pl.num_programs(1) - 1)
     def _():
@@ -99,22 +104,26 @@
         for o, kk in ((s_ref, k), (c_ref, 1 - k)):
             pair = acc.at[:, pl.ds(pl.multiple_of(kk * 512, 512), 512)]
             _emit_heads(pair, cos_ref, sin_ref, c == 2, [o.at[0, h] for h in range(2)])
-
-
-def _qkv_own(ids, x0, x1, x2, x3, w_ref, tab_ref, ptab_ref, o_ref, xs, acc, wt, sem, buf, wsem):
+        _emit_heads(acc2, cos_ref, sin_ref, c == 2, [o_ref.at[0, h] for h in range(2)])
+
+
+def _qkv_own(halves, ids, *refs):
+    nb = len(halves)
+    xr = refs[:nb]
+    w_ref, tab_ref, ptab_ref, o_ref, xs, acc, wt, sem, buf, wsem = refs[nb:]
     c, d = pl.program_id(0), pl.program_id(1)
     nd = pl.num_programs(1)
-    bd, t = buf.shape[1], x0.shape[0]
+    bd, t = buf.shape[1], xr[0].shape[0]
     take = _stream(w_ref, buf, wsem, ids[OWN_HEAD])
 
     def copy(b, k):
         cols = pl.ds(pl.multiple_of(k * bd, bd), bd)
-        return pltpu.make_async_copy((x0, x1, x2, x3)[b].at[:, cols], xs.at[pl.ds(b * t, t), cols], sem.at[k, b])
+        return pltpu.make_async_copy(xr[b].at[:, cols], xs.at[pl.ds(b * t, t), cols], sem.at[k, b])
 
     @pl.when((c == 0) & (d == 0))
     def _():
-        for k in range(x0.shape[1] // bd):
-            for b in range(4):
+        for k in range(xr[0].shape[1] // bd):
+            for b in range(nb):
                 copy(b, k).start()
 
     @pl.when(d == 0)
@@ -123,41 +132,41 @@
 
     @pl.when(c == 0)
     def _():
-        for b in range(4):
+        for b in range(nb):
             copy(b, d).wait()
 
     wt[...] = take()
     cols = pl.ds(pl.multiple_of(d * bd, bd), bd)
-    for h in range(2):
-        for m in range(2):
-            r = slice(m * 2 * t, (m + 1) * 2 * t)
-            acc[r, h * 256:(h + 1) * 256] += jnp.dot(xs[r, cols], wt[:, h * 256:(h + 1) * 256],
-                                                     preferred_element_type=F32)
+    acc[...] += jnp.dot(xs[:, cols], wt[...], preferred_element_type=F32)
 
     @pl.when(d == nd - 1)
     def _():
-        for b in range(4):
-            r = pl.ds(b * t, t)
-            tb = (tab_ref, ptab_ref)[b % 2]
-            tr = pl.ds((b // 2) * t, t)
+        for b, (n, half) in enumerate(halves):
+            tb = (tab_ref, ptab_ref)[n]
+            r, tr = pl.ds(b * t, t), pl.ds(half * t, t)
             _emit_heads(acc.at[r], tb.at[0, tr], tb.at[1, tr], c == 2, [o_ref.at[b, 0, h] for h in range(2)])
 
 
-def _qkv_next(ids, xn, w_ref, cos_ref, sin_ref, s_ref, c_ref, acc):
+def _qkv_next(ids, xn, w_ref, cos_ref, sin_ref, qs_ref, qc_ref, s_ref, c_ref, acc):
     c, j = pl.program_id(0), pl.program_id(1)
-
     acc[...] = jnp.dot(xn[...], w_ref[0], preferred_element_type=F32)
-    for n, o_ref in enumerate((s_ref, c_ref)):
-        @pl.when(j == n)
+    for n, (q_ref, o_ref) in enumerate(((qs_ref, s_ref), (qc_ref, c_ref))):
+        @pl.when((j == n) & (c == 0))
+        def _():
+            _emit_heads(acc, cos_ref, sin_ref, c == 2, [q_ref.at[0, h] for h in range(2)])
+
+        @pl.when((j == n) & (c > 0))
         def _():
             _emit_heads(acc, cos_ref, sin_ref, c == 2, [o_ref.at[0, h] for h in range(2)])
 
 
-def _attend(masks, ids, l_ref, rs0, rs1, rc0, rc1, *refs):
+def _attend(masks, ids, lo, lr, rs0, rs1, rc0, rc1, qs1, qc1, *refs):
     nq = len(masks)
     outs = refs[:2 * nq]
     qkv, m_s, l_s, acc, sem = refs[2 * nq:]
-    src = [l_ref.at[b] for b in range(4)] + [rs0, rs1, rc0, rc1]
+    kv = pl.ds(1, 2)
+    q_src = [lo.at[0]] + [lr.at[b, 0] for b in range(3)] + [rs0.at[0], qs1.at[0], rc0.at[0], qc1.at[0]]
+    kv_src = [lo.at[kv]] + [lr.at[b, kv] for b in range(3)] + [rs0.at[kv], rs1, rc0.at[kv], rc1]
     t, dh = rs0.shape[2:]
     me = ids[ME]
     chips = [(me ^ m) // 2 for m in masks]
@@ -165,11 +174,11 @@
 
     def kv_copy(n, b):
         rows = pl.ds(pl.multiple_of(b * t, t), t)
-        return pltpu.make_async_copy(src[n].at[pl.ds(1, 2)], qkv.at[pl.ds(1, 2), :, rows, :], sem.at[0, b])
+        return pltpu.make_async_copy(kv_src[n], qkv.at[kv, :, rows, :], sem.at[0, b])
 
     def q_copy(n, b):
         rows = pl.ds(pl.multiple_of(b * t, t), t)
-        return pltpu.make_async_copy(src[n].at[0], qkv.at[0, :, rows, :], sem.at[1, b])
+        return pltpu.make_async_copy(q_src[n], qkv.at[0, :, rows, :], sem.at[1, b])
 
     def issue(want_chip, queries):
         for n in range(8):
@@ -350,17 +359,35 @@
         anyspec = pl.BlockSpec(memory_space=pl.ANY)
         half2 = pl.BlockSpec((1, 2, t, dh), lambda c, *_: (c, 0, 0, 0))
 
-        b_same, b_cross, w_b, xn_o = pl.pallas_call(
+        b_same, b_cross, loc_o, w_b, xn_o = pl.pallas_call(
             _qkv_first,
             grid_spec=pltpu.PrefetchScalarGridSpec(
                 num_scalar_prefetch=1, grid=(3, nd),
                 in_specs=[whole, pl.BlockSpec((1, d), lambda *_: (0, 0)), anyspec,
                           tab_spec(0, 0), tab_spec(1, 0)],
-                out_specs=[half2, half2, pl.BlockSpec((1, bd, 4 * dh), lambda c, i, s: (c, i, 0)), whole],
-                scratch_shapes=[pltpu.VMEM((t, 4 * dh), F32)] + tiles(4)),
-            out_shape=[half, half, jax.ShapeDtypeStruct((3, d, 4 * dh), BF), xn_shape],
+                out_specs=[half2, half2, half2, pl.BlockSpec((1, bd, 4 * dh), lambda c, i, s: (c, i, 0)), whole],
+                scratch_shapes=[pltpu.VMEM((t, 4 * dh), F32), pltpu.VMEM((t, 2 * dh), F32),
+                                pltpu.VMEM((bd, 2 * dh), BF)] + tiles(4) + tiles(2)),
+            out_shape=[half, half, half, jax.ShapeDtypeStruct((3, d, 4 * dh), BF), xn_shape],
             compiler_params=_params(), cost_estimate=_cost(flops * 2.5, 80e6), name="qkv_first",
         )(ids, x, g2, wqkv, tab, tab)
+        both_tab = pl.BlockSpec((2, 2 * t, dh // 2), lambda *_: (0, 0, 0), pipeline_mode=pl.Buffered(1))
+
+        def own(xs, halves, ptab):
+            n = len(xs)
+            return pl.pallas_call(
+                functools.partial(_qkv_own, halves),
+                grid_spec=pltpu.PrefetchScalarGridSpec(
+                    num_scalar_prefetch=1, grid=(3, nd),
+                    in_specs=[anyspec] * (n + 1) + [both_tab, both_tab],
+                    out_specs=pl.BlockSpec((n, 1, 2, t, dh), lambda c, i, s: (0, c, 0, 0, 0)),
+                    scratch_shapes=[pltpu.VMEM((n * t, d), BF), pltpu.VMEM((n * t, 2 * dh), F32),
+                                    pltpu.VMEM((bd, 2 * dh), BF), pltpu.SemaphoreType.DMA((nd, n))]
+                    + tiles(2)),
+                out_shape=jax.ShapeDtypeStruct((n, 3, 2, t, dh), BF),
+                compiler_params=_params(), cost_estimate=_cost(flops * 0.7 * n, 15e6 + n * 6e6), name="qkv_own",
+            )(ids, *xs, wqkv, tab, ptab)
+
         rs_own, rc_own = send(b_same, to_same), send(b_cross, to_cross)
         xn_po, ptab = partner(xn_o), partner(tab)
         rb = 128
@@ -371,32 +398,21 @@
             compiler_params=_params(), cost_estimate=_cost(2e9, 8e6), name="norm",
         )(xa, g2)
         xn_pa = partner(xn_a)
-        a_same, a_cross = pl.pallas_call(
+        q_same, q_cross, a_same, a_cross = pl.pallas_call(
             _qkv_next,
             grid_spec=pltpu.PrefetchScalarGridSpec(
                 num_scalar_prefetch=1, grid=(3, 2),
                 in_specs=[whole, pl.BlockSpec((1, d, 2 * dh), lambda c, i, s: (c, 0, (i + s[ME]) % 2)),
                           tab_spec(0, 1), tab_spec(1, 1)],
-                out_specs=[half2, half2],
+                out_specs=[pl.BlockSpec((1, 2, t, dh), lambda *_: (0, 0, 0, 0))] * 2
+                + [pl.BlockSpec((1, 2, t, dh), lambda c, *_: (jnp.maximum(c - 1, 0), 0, 0, 0))] * 2,
                 scratch_shapes=[pltpu.VMEM((t, 2 * dh), F32)]),
-            out_shape=[half, half],
+            out_shape=[jax.ShapeDtypeStruct((n, 2, t, dh), BF) for n in (1, 1, 2, 2)],
             compiler_params=_params(), cost_estimate=_cost(flops * 1.4, 35e6), name="qkv_next",
         )(ids, xn_a, w_b, tab, tab)
         rs_a, rc_a = send(a_same, to_same), send(a_cross, to_cross)
-        both_tab = pl.BlockSpec((2, 2 * t, dh // 2), lambda *_: (0, 0, 0), pipeline_mode=pl.Buffered(1))
-        loc = pl.pallas_call(
-            _qkv_own,
-            grid_spec=pltpu.PrefetchScalarGridSpec(
-                num_scalar_prefetch=1, grid=(3, nd),
-                in_specs=[anyspec] * 5 + [both_tab, both_tab],
-                out_specs=pl.BlockSpec((4, 1, 2, t, dh), lambda c, i, s: (0, c, 0, 0, 0)),
-                scratch_shapes=[pltpu.VMEM((4 * t, d), BF), pltpu.VMEM((4 * t, 2 * dh), F32),
-                                pltpu.VMEM((bd, 2 * dh), BF), pltpu.SemaphoreType.DMA((nd, 4))]
-                + tiles(2)),
-            out_shape=jax.ShapeDtypeStruct((4, 3, 2, t, dh), BF),
-            compiler_params=_params(), cost_estimate=_cost(flops * 2.8, 60e6), name="qkv_own",
-        )(ids, xn_o, xn_po, xn_a, xn_pa, wqkv, tab, ptab)
-        src = [loc, rs_own, rs_a, rc_own, rc_a]
+        rs_q, rc_q = send(q_same, to_same), send(q_cross, to_cross)
+        loc_r = own((xn_po, xn_a, xn_pa), ((1, 0), (0, 1), (1, 1)), ptab)
 
         def attend(ms):
             nq = len(ms)
@@ -404,14 +420,14 @@
                 functools.partial(_attend, ms),
                 grid_spec=pltpu.PrefetchScalarGridSpec(
                     num_scalar_prefetch=1, grid=(1,),
-                    in_specs=[anyspec] * 5,
+                    in_specs=[anyspec] * 8,
                     out_specs=[pl.BlockSpec((t, 2 * dh), lambda i, s: (0, 0))] * (2 * nq),
                     scratch_shapes=[pltpu.VMEM((3, 2, 8 * t, dh), BF),
                                     pltpu.VMEM((2, 2 * t, 128), F32), pltpu.VMEM((2, 2 * t, 128), F32),
                                     pltpu.VMEM((2, 2 * t, dh), F32), pltpu.SemaphoreType.DMA((2, 8))]),
                 out_shape=[jax.ShapeDtypeStruct((t, 2 * dh), BF)] * (2 * nq),
                 compiler_params=_params(), cost_estimate=_cost(nq * 10e9, 13e6), name="attend",
-            )(ids, *src)
+            )(ids, loc_o, loc_r, rs_own, rs_a, rc_own, rc_a, *((rs_q, rc_q) if 6 in ms else (rs_a, rc_a)))
 
         got = {}
         for ms in GROUPS:

time: 209 us -> 248 us (1.19)
  waiting for transfers between devices: 20.2 us -> 55.2 us
  starting transfers between devices: 14.7 us -> 17.9 us
    ppermute x15 -> x17, waiting for transfers between devices: 20.2 us -> 55.2 us  [send(): return lax.ppermute(a, 'seq', [(i, f(i)) for i in range(8)])]
    pallas_call x1, Pallas kernels: 33.6 us -> 40.9 us  [local(): pl.pallas_call(_qkv_first, grid_spec=pltpu.PrefetchScalarGridSpec(num_sca...]
    pallas_call x1, Pallas kernels: 38.5 us -> 32 us  [own(): pl.pallas_call(functools.partial(_qkv_own, halves), grid_spec=pltpu.Prefe...]
    ppermute x15 -> x17, starting transfers between devices: 14.7 us -> 17.9 us  [send(): return lax.ppermute(a, 'seq', [(i, f(i)) for i in range(8)])]
  transfers between devices with their start and end apart: 15 -> 17, of which waited for: 3 -> 6; matrix products, arithmetic and copies ran while one was open for 2% -> 2% of each run, Pallas kernels for 67% -> 56%
where the time goes in v3:
time: 248 us; the launch traced here: 247 us
  Pallas kernels  169 us (68%)
  waiting for transfers between devices  55.2 us (22%)
  starting transfers between devices  17.9 us (7%)
  other arithmetic  3.1 us (1%)
    ppermute x17, waiting for transfers between devices, send(): return lax.ppermute(a, 'seq', [(i, f(i)) for i in range(8)])  55.2 us
    pallas_call x2, Pallas kernels, attend(): pl.pallas_call(functools.partial(_attend, ms), grid_spec=pltpu.PrefetchSc...  42.7 us
    pallas_call x1, Pallas kernels, local(): pl.pallas_call(_qkv_first, grid_spec=pltpu.PrefetchScalarGridSpec(num_sca...  40.9 us
    pallas_call x1, Pallas kernels, own(): pl.pallas_call(functools.partial(_qkv_own, halves), grid_spec=pltpu.Prefe...  32 us
    pallas_call x2, Pallas kernels, project(): pl.pallas_call(functools.partial(_project, n), grid_spec=pltpu.PrefetchSc...  26.8 us
    pallas_call x1, Pallas kernels, local(): pl.pallas_call(_qkv_next, grid_spec=pltpu.PrefetchScalarGridSpec(num_scal...  21 us
    ppermute x17, starting transfers between devices, send(): return lax.ppermute(a, 'seq', [(i, f(i)) for i in range(8)])  17.9 us
    pallas_call x1, Pallas kernels, local(): pl.pallas_call(_norm_rows, grid=(t // rb,), in_specs=[pl.BlockSpec((rb, d...  6.06 us
  transfers between devices with their start and end apart: 17, of which 6 were waited for; matrix products, arithmetic and copies ran while one was open for 2% of the time, Pallas kernels for 56%

profile of v3, /device:TPU:0, one launch (start us, length us, event | category | flops | bytes accessed | tf_op | source)
XLA Modules:
  0.0 247.3 jit_solution(853064087294753942)
XLA Ops:
  0.0 3.3 %collective-permute-start.1 = (bf16[512,4096]{1,0:T(8,128)(2,1)}, bf16[512,4096]{1,0:T(8,128)(2,1)}, u32[]{:S(2)}, u32[]{:S(2)}) collective-permute-start(bf16[512,4096]{1,0:T(8,128)(2,1)} %refs_12_.1), channel_id=1, source_target_pairs={{0,2},{1,5},{2,0},{3,7},{4,6},{5,1},{6,4},{7,3}} | collective-permute-start | bytes 12582920 | tf_op jit(solution)/shard_map/ppermute | solution.py:314
  3.3 0.1 add_multiply_fusion
  3.4 0.1 convert_bitcast_fusion
  3.5 0.6 stack.74.ids
  4.1 1.9 multiply_cosine_fusion
  6.0 1.1 pad_maximum_fusion.cos_ref.sin_ref.refs_4_
  7.0 40.9 %qkv_first.1 = (bf16[3,2,512,256]{3,2,1,0:T(8,128)(2,1)}, bf16[3,2,512,256]{3,2,1,0:T(8,128)(2,1)}, bf16[3,2,512,256]{3,2,1,0:T(8,128)(2,1)}, bf16[3,4096,1024]{2,1,0:T(8,128)(2,1)}, bf16[512,4096]{1,0:T(8,128)(2,1)}) custom-call(s32[19]{0:T(128)} %stack.74.ids, bf16[512,4096]{1,0:T(8,128)(2,1)} %refs_12_.1, f32[1,4096]{1,0:T(1,128)} %bitcast.27, ...), custom_call_target="tpu_custom_call" | custom-call | flops 1610612736 | bytes 4000000 | tf_op jit(solution)/shard_map/qkv_first/pallas_call | solution.py:362
  48.0 0.0 collective-permute-start
  48.0 2.1 collective-permute-done.1.x_ref
  50.1 6.1 %norm.1.refs_1_.xn = bf16[512,4096]{1,0:T(8,128)(2,1)} custom-call(bf16[512,4096]{1,0:T(8,128)(2,1)} %collective-permute-done.1.x_ref, f32[1,4096]{1,0:T(1,128)} %bitcast.28), custom_call_target="tpu_custom_call" | custom-call | flops 100000000 | bytes 400000 | tf_op jit(solution)/shard_map/norm/pallas_call | solution.py:394
  56.2 0.0 collective-permute-start.2
  56.2 2.1 collective-permute-start.4
  58.2 0.2 collective-permute-start.3
  58.4 1.1 collective-permute-start.6
  59.5 21.0 %qkv_next.1 = (bf16[1,2,512,256]{3,2,1,0:T(8,128)(2,1)}, bf16[1,2,512,256]{3,2,1,0:T(8,128)(2,1)}, bf16[2,2,512,256]{3,2,1,0:T(8,128)(2,1)}, bf16[2,2,512,256]{3,2,1,0:T(8,128)(2,1)}) custom-call(s32[19]{0:T(128)} %stack.74.ids, bf16[512,4096]{1,0:T(8,128)(2,1)} %norm.1.refs_1_.xn, bf16[3,4096,1024]{2,1,0:T(8,128)(2,1)} %get-tuple-element.25.w_ref, ...), custom_call_target="tpu_custom_call" | custom-call | flops 901943104 | bytes 1750000 | tf_op jit(solution)/shard_map/qkv_next/pallas_call | solution.py:401
  80.5 0.0 collective-permute-done.3.refs_5_
  80.5 0.8 collective-permute-start.5
  81.3 0.0 collective-permute-done.4.rs0
  81.3 1.0 collective-permute-start.7
  82.4 0.0 collective-permute-done.refs_0_
  82.4 0.5 collective-permute-start.8
  82.9 0.0 collective-permute-done.2.refs_2_
  82.9 1.1 collective-permute-start.9
  84.0 32.0 %qkv_own.1.lr = bf16[3,3,2,512,256]{4,3,2,1,0:T(8,128)(2,1)} custom-call(s32[19]{0:T(128)} %stack.74.ids, bf16[512,4096]{1,0:T(8,128)(2,1)} %collective-permute-done.refs_0_, bf16[512,4096]{1,0:T(8,128)(2,1)} %norm.1.refs_1_.xn, bf16[512,4096]{1,0:T(8,128)(2,1)} %collective-permute-done.2.refs_2_, bf16[4096,3,16,256]{3,2,1,0:T(8,128)(2,1)} %refs_3_.1, ...), custom_call_target="tpu_custom_call" | custom-call | flops 1352914688 | bytes 1650000 | tf_op jit(solution)/shard_map/qkv_own/pallas_call | solution.py:378
  116.0 0.0 collective-permute-done.6.rc0
  116.0 5.7 %collective-permute-done.8.qs1 = bf16[1,2,512,256]{3,2,1,0:T(8,128)(2,1)S(1)} collective-permute-done((bf16[1,2,512,256]{3,2,1,0:T(8,128)(2,1)}, bf16[1,2,512,256]{3,2,1,0:T(8,128)(2,1)S(1)}, u32[]{:S(2)}, u32[]{:S(2)}) %collective-permute-start.8) | collective-permute-done | bytes 524320 | tf_op jit(solution)/shard_map/ppermute | solution.py:314
  121.8 5.5 %collective-permute-done.9.qc1 = bf16[1,2,512,256]{3,2,1,0:T(8,128)(2,1)} collective-permute-done((bf16[1,2,512,256]{3,2,1,0:T(8,128)(2,1)}, bf16[1,2,512,256]{3,2,1,0:T(8,128)(2,1)}, u32[]{:S(2)}, u32[]{:S(2)}) %collective-permute-start.9) | collective-permute-done | bytes 524320 | tf_op jit(solution)/shard_map/ppermute | solution.py:314
  127.3 0.0 collective-permute-done.5.rs1.qs1
  127.3 0.0 collective-permute-done.7.rc1.qc1
  127.3 1.0 copy-done.3
  128.2 21.3 %attend.2 = (bf16[512,512]{1,0:T(8,128)(2,1)}, bf16[512,512]{1,0:T(8,128)(2,1)}, bf16[512,512]{1,0:T(8,128)(2,1)}, bf16[512,512]{1,0:T(8,128)(2,1)}) custom-call(s32[19]{0:T(128)} %stack.74.ids, bf16[3,2,512,256]{3,2,1,0:T(8,128)(2,1)} %get-tuple-element.22.lo, bf16[3,3,2,512,256]{4,3,2,1,0:T(8,128)(2,1)} %qkv_own.1.lr, ...), custom_call_target="tpu_custom_call" | custom-call | flops 1000000000 | bytes 650000 | tf_op jit(solution)/shard_map/attend/pallas_call | solution.py:419
  149.6 0.1 collective-permute-start.12
  149.7 21.4 %attend.3 = (bf16[512,512]{1,0:T(8,128)(2,1)}, bf16[512,512]{1,0:T(8,128)(2,1)}, bf16[512,512]{1,0:T(8,128)(2,1)}, bf16[512,512]{1,0:T(8,128)(2,1)}) custom-call(s32[19]{0:T(128)} %stack.74.ids, bf16[3,2,512,256]{3,2,1,0:T(8,128)(2,1)} %get-tuple-element.22.lo, bf16[3,3,2,512,256]{4,3,2,1,0:T(8,128)(2,1)} %qkv_own.1.lr, ...), custom_call_target="tpu_custom_call" | custom-call | flops 1000000000 | bytes 650000 | tf_op jit(solution)/shard_map/attend/pallas_call | solution.py:419
  171.1 1.8 collective-permute-start.13
  173.0 0.0 collective-permute-start.14
  173.0 1.7 collective-permute-start.15
  174.7 0.0 collective-permute-start.16
  174.7 0.0 collective-permute-done.12.refs_1_
  174.7 2.7 %collective-permute-start.10 = (bf16[512,512]{1,0:T(8,128)(2,1)}, bf16[512,512]{1,0:T(8,128)(2,1)S(1)}, u32[]{:S(2)}, u32[]{:S(2)}) collective-permute-start(bf16[512,512]{1,0:T(8,128)(2,1)} %get-tuple-element.31), channel_id=1, source_target_pairs={{0,6},{1,7},{2,4},{3,5},{4,2},{5,3},{6,0},{7,1}} | collective-permute-start | bytes 1572872 | tf_op jit(solution)/shard_map/ppermute | solution.py:314
  177.4 8.7 %collective-permute-done.13.refs_2_ = bf16[512,512]{1,0:T(8,128)(2,1)S(1)} collective-permute-done((bf16[512,512]{1,0:T(8,128)(2,1)}, bf16[512,512]{1,0:T(8,128)(2,1)S(1)}, u32[]{:S(2)}, u32[]{:S(2)}) %collective-permute-start.13) | collective-permute-done | bytes 524320 | tf_op jit(solution)/shard_map/ppermute | solution.py:314
  186.2 1.3 collective-permute-start.11
  187.5 9.4 %collective-permute-done.14.refs_3_ = bf16[512,512]{1,0:T(8,128)(2,1)S(1)} collective-permute-done((bf16[512,512]{1,0:T(8,128)(2,1)}, bf16[512,512]{1,0:T(8,128)(2,1)S(1)}, u32[]{:S(2)}, u32[]{:S(2)}) %collective-permute-start.14) | collective-permute-done | bytes 524320 | tf_op jit(solution)/shard_map/ppermute | solution.py:314
  196.8 0.0 collective-permute-done.15.refs_4_
  196.8 23.7 %collective-permute-done.16.refs_5_ = bf16[512,512]{1,0:T(8,128)(2,1)S(1)} collective-permute-done((bf16[512,512]{1,0:T(8,128)(2,1)}, bf16[512,512]{1,0:T(8,128)(2,1)S(1)}, u32[]{:S(2)}, u32[]{:S(2)}) %collective-permute-start.16) | collective-permute-done | bytes 524320 | tf_op jit(solution)/shard_map/ppermute | solution.py:314
  220.5 17.8 %project.2.refs_4_ = f32[512,4096]{1,0:T(8,128)S(1)} custom-call(s32[19]{0:T(128)S(1)} %copy-done.1, bf16[512,512]{1,0:T(8,128)(2,1)S(1)} %copy-done, bf16[512,512]{1,0:T(8,128)(2,1)S(1)} %collective-permute-done.12.refs_1_, bf16[512,512]{1,0:T(8,128)(2,1)S(1)} %collective-permute-done.13.refs_2_, bf16[512,512]{1,0:T(8,128)(2,1)S(1)} %collective-permute-done.14.refs_3_, ...), custom_call_target="tpu_custom_call" | custom-call | flops 837518592 | bytes 1660000 | tf_op jit(solution)/shard_map/project/pallas_call | solution.py:451
  238.3 0.0 collective-permute-done.10.refs_0_
  238.4 0.0 collective-permute-done.11.refs_1_
  238.4 9.0 %project.3 = bf16[512,4096]{1,0:T(8,128)(2,1)} custom-call(s32[19]{0:T(128)S(1)} %copy-done.1, bf16[512,512]{1,0:T(8,128)(2,1)S(1)} %collective-permute-done.10.refs_0_, bf16[512,512]{1,0:T(8,128)(2,1)S(1)} %collective-permute-done.11.refs_1_, bf16[4096,4096]{1,0:T(8,128)(2,1)} %bitcast.25, bf16[4096,4096]{1,0:T(8,128)(2,1)} %bitcast.26, ...), custom_call_target="tpu_custom_call" | custom-call | flops 279172864 | bytes 820000 | tf_op jit(solution)/shard_map/project/pallas_call | solution.py:451
  (13 shorter events, 0.0 us)
Async XLA Ops:
  0.0 50.1 %collective-permute-start.1 = (bf16[512,4096]{1,0:T(8,128)(2,1)}, bf16[512,4096]{1,0:T(8,128)(2,1)}, u32[]{:S(2)}, u32[]{:S(2)}) collective-permute-start(bf16[512,4096]{1,0:T(8,128)(2,1)} %refs_12_.1), channel_id=1, source_target_pairs={{0,2},{1,5},{2,0},{3,7},{4,6},{5,1},{6,4},{7,3}} | collective-permute-start | bytes 12582920 | tf_op jit(solution)/shard_map/ppermute | solution.py:314
  47.9 10.3 %copy-start.2 = (f32[2,1024,128]{2,1,0:T(8,128)S(1)}, f32[2,1024,128]{2,1,0:T(8,128)}, u32[]{:S(2)}) copy-start(f32[2,1024,128]{2,1,0:T(8,128)} %pad_maximum_fusion.cos_ref.sin_ref.refs_4_) | copy-start | bytes 3145732
  48.0 34.4 %collective-permute-start = (bf16[512,4096]{1,0:T(8,128)(2,1)}, bf16[512,4096]{1,0:T(8,128)(2,1)}, u32[]{:S(2)}, u32[]{:S(2)}) collective-permute-start(bf16[512,4096]{1,0:T(8,128)(2,1)} %get-tuple-element.23), channel_id=1, source_target_pairs={{0,1},{1,0},{2,3},{3,2},{4,5},{5,4},{6,7},{7,6}} | collective-permute-start | bytes 12582920 | tf_op jit(solution)/shard_map/ppermute | solution.py:314
  56.2 26.7 %collective-permute-start.2 = (bf16[512,4096]{1,0:T(8,128)(2,1)}, bf16[512,4096]{1,0:T(8,128)(2,1)}, u32[]{:S(2)}, u32[]{:S(2)}) collective-permute-start(bf16[512,4096]{1,0:T(8,128)(2,1)} %norm.1.refs_1_.xn), channel_id=1, source_target_pairs={{0,1},{1,0},{2,3},{3,2},{4,5},{5,4},{6,7},{7,6}} | collective-permute-start | bytes 12582920 | tf_op jit(solution)/shard_map/ppermute | solution.py:314
  56.2 25.2 %collective-permute-start.4 = (bf16[3,2,512,256]{3,2,1,0:T(8,128)(2,1)}, bf16[3,2,512,256]{3,2,1,0:T(8,128)(2,1)}, u32[]{:S(2)}, u32[]{:S(2)}) collective-permute-start(bf16[3,2,512,256]{3,2,1,0:T(8,128)(2,1)} %get-tuple-element.24), channel_id=1, source_target_pairs={{0,4},{1,3},{2,6},{3,1},{4,0},{5,7},{6,2},{7,5}} | collective-permute-start | bytes 4718600 | tf_op jit(solution)/shard_map/ppermute | solution.py:314
  58.2 22.3 %collective-permute-start.3 = (f32[2,1024,128]{2,1,0:T(8,128)S(1)}, f32[2,1024,128]{2,1,0:T(8,128)}, u32[]{:S(2)}, u32[]{:S(2)}) collective-permute-start(f32[2,1024,128]{2,1,0:T(8,128)S(1)} %copy-done.2), channel_id=1, source_target_pairs={{0,1},{1,0},{2,3},{3,2},{4,5},{5,4},{6,7},{7,6}} | collective-permute-start | bytes 3145736 | tf_op jit(solution)/shard_map/ppermute | solution.py:314
  58.4 57.6 %collective-permute-start.6 = (bf16[3,2,512,256]{3,2,1,0:T(8,128)(2,1)}, bf16[3,2,512,256]{3,2,1,0:T(8,128)(2,1)}, u32[]{:S(2)}, u32[]{:S(2)}) collective-permute-start(bf16[3,2,512,256]{3,2,1,0:T(8,128)(2,1)} %get-tuple-element.27), channel_id=1, source_target_pairs={{0,5},{1,2},{2,7},{3,0},{4,1},{5,6},{6,3},{7,4}} | collective-permute-start | bytes 4718600 | tf_op jit(solution)/shard_map/ppermute | solution.py:314
  80.5 46.8 %collective-permute-start.5 = (bf16[2,2,512,256]{3,2,1,0:T(8,128)(2,1)}, bf16[2,2,512,256]{3,2,1,0:T(8,128)(2,1)S(1)}, u32[]{:S(2)}, u32[]{:S(2)}) collective-permute-start(bf16[2,2,512,256]{3,2,1,0:T(8,128)(2,1)} %get-tuple-element.26), channel_id=1, source_target_pairs={{0,4},{1,3},{2,6},{3,1},{4,0},{5,7},{6,2},{7,5}} | collective-permute-start | bytes 3145736 | tf_op jit(solution)/shard_map/ppermute | solution.py:314
  81.3 45.9 %collective-permute-start.7 = (bf16[2,2,512,256]{3,2,1,0:T(8,128)(2,1)}, bf16[2,2,512,256]{3,2,1,0:T(8,128)(2,1)}, u32[]{:S(2)}, u32[]{:S(2)}) collective-permute-start(bf16[2,2,512,256]{3,2,1,0:T(8,128)(2,1)} %get-tuple-element.28), channel_id=1, source_target_pairs={{0,5},{1,2},{2,7},{3,0},{4,1},{5,6},{6,3},{7,4}} | collective-permute-start | bytes 3145736 | tf_op jit(solution)/shard_map/ppermute | solution.py:314
  82.4 39.4 %collective-permute-start.8 = (bf16[1,2,512,256]{3,2,1,0:T(8,128)(2,1)}, bf16[1,2,512,256]{3,2,1,0:T(8,128)(2,1)S(1)}, u32[]{:S(2)}, u32[]{:S(2)}) collective-permute-start(bf16[1,2,512,256]{3,2,1,0:T(8,128)(2,1)} %get-tuple-element.29), channel_id=1, source_target_pairs={{0,4},{1,3},{2,6},{3,1},{4,0},{5,7},{6,2},{7,5}} | collective-permute-start | bytes 1572872 | tf_op jit(solution)/shard_map/ppermute | solution.py:314
  82.9 44.4 %collective-permute-start.9 = (bf16[1,2,512,256]{3,2,1,0:T(8,128)(2,1)}, bf16[1,2,512,256]{3,2,1,0:T(8,128)(2,1)}, u32[]{:S(2)}, u32[]{:S(2)}) collective-permute-start(bf16[1,2,512,256]{3,2,1,0:T(8,128)(2,1)} %get-tuple-element.30), channel_id=1, source_target_pairs={{0,5},{1,2},{2,7},{3,0},{4,1},{5,6},{6,3},{7,4}} | collective-permute-start | bytes 1572872 | tf_op jit(solution)/shard_map/ppermute | solution.py:314
  121.8 5.5 %copy-start.4 = (bf16[1,2,512,256]{3,2,1,0:T(8,128)(2,1)}, bf16[1,2,512,256]{3,2,1,0:T(8,128)(2,1)S(1)}, u32[]{:S(2)}) copy-start(bf16[1,2,512,256]{3,2,1,0:T(8,128)(2,1)S(1)} %collective-permute-done.8.qs1) | copy-start | bytes 1572868
  127.3 1.0 copy-start.3
  149.5 36.6 %copy-start.5 = (bf16[512,512]{1,0:T(8,128)(2,1)S(1)}, bf16[512,512]{1,0:T(8,128)(2,1)}, u32[]{:S(2)}) copy-start(bf16[512,512]{1,0:T(8,128)(2,1)} %get-tuple-element.32) | copy-start | bytes 1572868
  149.5 71.0 %copy-start = (bf16[512,512]{1,0:T(8,128)(2,1)S(1)}, bf16[512,512]{1,0:T(8,128)(2,1)}, u32[]{:S(2)}) copy-start(bf16[512,512]{1,0:T(8,128)(2,1)} %get-tuple-element.33.refs_0_) | copy-start | bytes 1572868
  149.5 71.0 %copy-start.1 = (s32[19]{0:T(128)S(1)}, s32[19]{0:T(128)}, u32[]{:S(2)}) copy-start(s32[19]{0:T(128)} %stack.74.ids) | copy-start | bytes 232
  149.6 25.2 %collective-permute-start.12 = (bf16[512,512]{1,0:T(8,128)(2,1)}, bf16[512,512]{1,0:T(8,128)(2,1)S(1)}, u32[]{:S(2)}, u32[]{:S(2)}) collective-permute-start(bf16[512,512]{1,0:T(8,128)(2,1)} %get-tuple-element.34), channel_id=1, source_target_pairs={{0,1},{1,0},{2,3},{3,2},{4,5},{5,4},{6,7},{7,6}} | collective-permute-start | bytes 1572872 | tf_op jit(solution)/shard_map/ppermute | solution.py:314
  171.1 15.0 %collective-permute-start.13 = (bf16[512,512]{1,0:T(8,128)(2,1)}, bf16[512,512]{1,0:T(8,128)(2,1)S(1)}, u32[]{:S(2)}, u32[]{:S(2)}) collective-permute-start(bf16[512,512]{1,0:T(8,128)(2,1)} %get-tuple-element.35), channel_id=1, source_target_pairs={{0,2},{1,3},{2,0},{3,1},{4,6},{5,7},{6,4},{7,5}} | collective-permute-start | bytes 1572872 | tf_op jit(solution)/shard_map/ppermute | solution.py:314
  173.0 23.9 %collective-permute-start.14 = (bf16[512,512]{1,0:T(8,128)(2,1)}, bf16[512,512]{1,0:T(8,128)(2,1)S(1)}, u32[]{:S(2)}, u32[]{:S(2)}) collective-permute-start(bf16[512,512]{1,0:T(8,128)(2,1)} %get-tuple-element.36), channel_id=1, source_target_pairs={{0,3},{1,2},{2,1},{3,0},{4,7},{5,6},{6,5},{7,4}} | collective-permute-start | bytes 1572872 | tf_op jit(solution)/shard_map/ppermute | solution.py:314
  173.0 23.9 %collective-permute-start.15 = (bf16[512,512]{1,0:T(8,128)(2,1)}, bf16[512,512]{1,0:T(8,128)(2,1)S(1)}, u32[]{:S(2)}, u32[]{:S(2)}) collective-permute-start(bf16[512,512]{1,0:T(8,128)(2,1)} %get-tuple-element.37), channel_id=1, source_target_pairs={{0,4},{1,5},{2,6},{3,7},{4,0},{5,1},{6,2},{7,3}} | collective-permute-start | bytes 1572872 | tf_op jit(solution)/shard_map/ppermute | solution.py:314
  174.7 45.8 %collective-permute-start.16 = (bf16[512,512]{1,0:T(8,128)(2,1)}, bf16[512,512]{1,0:T(8,128)(2,1)S(1)}, u32[]{:S(2)}, u32[]{:S(2)}) collective-permute-start(bf16[512,512]{1,0:T(8,128)(2,1)} %get-tuple-element.38), channel_id=1, source_target_pairs={{0,5},{1,4},{2,7},{3,6},{4,1},{5,0},{6,3},{7,2}} | collective-permute-start | bytes 1572872 | tf_op jit(solution)/shard_map/ppermute | solution.py:314
  174.7 63.6 %collective-permute-start.10 = (bf16[512,512]{1,0:T(8,128)(2,1)}, bf16[512,512]{1,0:T(8,128)(2,1)S(1)}, u32[]{:S(2)}, u32[]{:S(2)}) collective-permute-start(bf16[512,512]{1,0:T(8,128)(2,1)} %get-tuple-element.31), channel_id=1, source_target_pairs={{0,6},{1,7},{2,4},{3,5},{4,2},{5,3},{6,0},{7,1}} | collective-permute-start | bytes 1572872 | tf_op jit(solution)/shard_map/ppermute | solution.py:314
  186.2 52.2 %collective-permute-start.11 = (bf16[512,512]{1,0:T(8,128)(2,1)S(1)}, bf16[512,512]{1,0:T(8,128)(2,1)S(1)}, u32[]{:S(2)}, u32[]{:S(2)}) collective-permute-start(bf16[512,512]{1,0:T(8,128)(2,1)S(1)} %copy-done.5), channel_id=1, source_target_pairs={{0,7},{1,6},{2,5},{3,4},{4,3},{5,2},{6,1},{7,0}} | collective-permute-start | bytes 1572872 | tf_op jit(solution)/shard_map/ppermute | solution.py:314

commit v4 on v3

--- a/solution.py
+++ b/solution.py
@@ -18,21 +18,27 @@
 ME, B_HEAD, OWN_HEAD, SRC, DEV = 0, 1, 2, 3, 11
 
 
-def _norm(x_ref, g_ref, xn, base):
-    rb = 16
-
-    def body(i, c):
+def _norm(x_ref, g_ref, xn):
+    rb, d = 16, x_ref.shape[1]
+    cols = [slice(j * 128, (j + 1) * 128) for j in range(d // 128)]
+
+    def body(i, carry):
         r = pl.ds(pl.multiple_of(i * rb, rb), rb)
-        xf = x_ref[r, :].astype(F32)
-        ms = jnp.mean(xf * xf, axis=-1, keepdims=True)
-        xn[pl.ds(pl.multiple_of(base + i * rb, rb), rb), :] = (xf * lax.rsqrt(ms + 1e-5) * g_ref[...]).astype(BF)
-        return c
-
-    lax.fori_loop(0, x_ref.shape[0] // rb, body, 0, unroll=2)
+        parts = [jnp.zeros((rb, 128), F32)] * 4
+        for j, c in enumerate(cols):
+            v = x_ref[r, c].astype(F32)
+            parts[j % 4] = parts[j % 4] + v * v
+        ss = jnp.sum((parts[0] + parts[1]) + (parts[2] + parts[3]), axis=-1, keepdims=True)
+        inv = jnp.broadcast_to(lax.rsqrt(ss * (1.0 / d) + 1e-5), (rb, 128))
+        for c in cols:
+            xn[r, c] = (x_ref[r, c].astype(F32) * inv * g_ref[:, c]).astype(BF)
+        return carry
+
+    lax.fori_loop(0, x_ref.shape[0] // rb, body, 0, unroll=8)
 
 
 def _norm_rows(x_ref, g_ref, o_ref):
-    _norm(x_ref, g_ref, o_ref, 0)
+    _norm(x_ref, g_ref, o_ref)
 
 
 def _emit_heads(acc, cos, sin, is_v, outs):
@@ -85,7 +91,7 @@
 
     @pl.when((c == 0) & (d == 0))
     def _():
-        _norm(x_ref, g_ref, xn, 0)
+        _norm(x_ref, g_ref, xn)
 
     @pl.when(d == 0)
     def _():
@@ -378,19 +384,19 @@
             return pl.pallas_call(
                 functools.partial(_qkv_own, halves),
                 grid_spec=pltpu.PrefetchScalarGridSpec(
-                    num_scalar_prefetch=1, grid=(3, nd),
+                    num_scalar_prefetch=1, grid=(3, 2),
                     in_specs=[anyspec] * (n + 1) + [both_tab, both_tab],
                     out_specs=pl.BlockSpec((n, 1, 2, t, dh), lambda c, i, s: (0, c, 0, 0, 0)),
                     scratch_shapes=[pltpu.VMEM((n * t, d), BF), pltpu.VMEM((n * t, 2 * dh), F32),
-                                    pltpu.VMEM((bd, 2 * dh), BF), pltpu.SemaphoreType.DMA((nd, n))]
-                    + tiles(2)),
+                                    pltpu.VMEM((2048, 2 * dh), BF), pltpu.SemaphoreType.DMA((2, n))]
+                    + [pltpu.VMEM((2, 2048, 2, dh), BF), pltpu.SemaphoreType.DMA((2,))]),
                 out_shape=jax.ShapeDtypeStruct((n, 3, 2, t, dh), BF),
                 compiler_params=_params(), cost_estimate=_cost(flops * 0.7 * n, 15e6 + n * 6e6), name="qkv_own",
             )(ids, *xs, wqkv, tab, ptab)
 
         rs_own, rc_own = send(b_same, to_same), send(b_cross, to_cross)
         xn_po, ptab = partner(xn_o), partner(tab)
-        rb = 128
+        rb = 256
         xn_a = pl.pallas_call(
             _norm_rows, grid=(t // rb,),
             in_specs=[pl.BlockSpec((rb, d), lambda i: (i, 0)), pl.BlockSpec((1, d), lambda i: (0, 0))],

time: 248 us -> 247 us (level)
  transfers between devices with their start and end apart: 17 -> 17, of which waited for: 6 -> 6; matrix products, arithmetic and copies ran while one was open for 2% -> 2% of each run, Pallas kernels for 56% -> 55%
where the time goes in v4:
time: 247 us; the launch traced here: 246 us
  Pallas kernels  167 us (68%)
  waiting for transfers between devices  56.9 us (23%)
  starting transfers between devices  17.9 us (7%)
  other arithmetic  3.1 us (1%)
    ppermute x17, waiting for transfers between devices, send(): return lax.ppermute(a, 'seq', [(i, f(i)) for i in range(8)])  56.9 us
    pallas_call x2, Pallas kernels, attend(): pl.pallas_call(functools.partial(_attend, ms), grid_spec=pltpu.PrefetchSc...  42.7 us
    pallas_call x1, Pallas kernels, local(): pl.pallas_call(_qkv_first, grid_spec=pltpu.PrefetchScalarGridSpec(num_sca...  40.1 us
    pallas_call x1, Pallas kernels, own(): pl.pallas_call(functools.partial(_qkv_own, halves), grid_spec=pltpu.Prefe...  31.1 us
    pallas_call x2, Pallas kernels, project(): pl.pallas_call(functools.partial(_project, n), grid_spec=pltpu.PrefetchSc...  26.8 us
    pallas_call x1, Pallas kernels, local(): pl.pallas_call(_qkv_next, grid_spec=pltpu.PrefetchScalarGridSpec(num_scal...  21 us
    ppermute x17, starting transfers between devices, send(): return lax.ppermute(a, 'seq', [(i, f(i)) for i in range(8)])  17.9 us
    pallas_call x1, Pallas kernels, local(): pl.pallas_call(_norm_rows, grid=(t // rb,), in_specs=[pl.BlockSpec((rb, d...  5.01 us
  transfers between devices with their start and end apart: 17, of which 6 were waited for; matrix products, arithmetic and copies ran while one was open for 2% of the time, Pallas kernels for 55%

profile of v4, /device:TPU:0, one launch (start us, length us, event | category | flops | bytes accessed | tf_op | source)
XLA Modules:
  0.0 246.3 jit_solution(3376489820246376580)
XLA Ops:
  0.0 3.3 %collective-permute-start.1 = (bf16[512,4096]{1,0:T(8,128)(2,1)}, bf16[512,4096]{1,0:T(8,128)(2,1)}, u32[]{:S(2)}, u32[]{:S(2)}) collective-permute-start(bf16[512,4096]{1,0:T(8,128)(2,1)} %refs_12_.1), channel_id=1, source_target_pairs={{0,2},{1,5},{2,0},{3,7},{4,6},{5,1},{6,4},{7,3}} | collective-permute-start | bytes 12582920 | tf_op jit(solution)/shard_map/ppermute | solution.py:320
  3.3 0.1 add_multiply_fusion
  3.4 0.1 convert_bitcast_fusion
  3.5 0.6 stack.74.ids
  4.1 1.9 multiply_cosine_fusion
  6.0 1.1 pad_maximum_fusion.cos_ref.sin_ref.refs_4_
  7.0 40.1 %qkv_first.1 = (bf16[3,2,512,256]{3,2,1,0:T(8,128)(2,1)}, bf16[3,2,512,256]{3,2,1,0:T(8,128)(2,1)}, bf16[3,2,512,256]{3,2,1,0:T(8,128)(2,1)}, bf16[3,4096,1024]{2,1,0:T(8,128)(2,1)}, bf16[512,4096]{1,0:T(8,128)(2,1)}) custom-call(s32[19]{0:T(128)} %stack.74.ids, bf16[512,4096]{1,0:T(8,128)(2,1)} %refs_12_.1, f32[1,4096]{1,0:T(1,128)} %bitcast.27, ...), custom_call_target="tpu_custom_call" | custom-call | flops 1610612736 | bytes 4000000 | tf_op jit(solution)/shard_map/qkv_first/pallas_call | solution.py:368
  47.1 0.0 collective-permute-start
  47.2 2.9 %collective-permute-done.1.x_ref = bf16[512,4096]{1,0:T(8,128)(2,1)} collective-permute-done((bf16[512,4096]{1,0:T(8,128)(2,1)}, bf16[512,4096]{1,0:T(8,128)(2,1)}, u32[]{:S(2)}, u32[]{:S(2)}) %collective-permute-start.1) | collective-permute-done | bytes 4194336 | tf_op jit(solution)/shard_map/ppermute | solution.py:320
  50.1 5.0 %norm.1.refs_1_.xn = bf16[512,4096]{1,0:T(8,128)(2,1)} custom-call(bf16[512,4096]{1,0:T(8,128)(2,1)} %collective-permute-done.1.x_ref, f32[1,4096]{1,0:T(1,128)} %bitcast.28), custom_call_target="tpu_custom_call" | custom-call | flops 100000000 | bytes 400000 | tf_op jit(solution)/shard_map/norm/pallas_call | solution.py:400
  55.1 0.0 collective-permute-start.2
  55.1 2.1 collective-permute-start.4
  57.2 0.2 collective-permute-start.3
  57.4 1.1 collective-permute-start.6
  58.5 21.0 %qkv_next.1 = (bf16[1,2,512,256]{3,2,1,0:T(8,128)(2,1)}, bf16[1,2,512,256]{3,2,1,0:T(8,128)(2,1)}, bf16[2,2,512,256]{3,2,1,0:T(8,128)(2,1)}, bf16[2,2,512,256]{3,2,1,0:T(8,128)(2,1)}) custom-call(s32[19]{0:T(128)} %stack.74.ids, bf16[512,4096]{1,0:T(8,128)(2,1)} %norm.1.refs_1_.xn, bf16[3,4096,1024]{2,1,0:T(8,128)(2,1)} %get-tuple-element.25.w_ref, ...), custom_call_target="tpu_custom_call" | custom-call | flops 901943104 | bytes 1750000 | tf_op jit(solution)/shard_map/qkv_next/pallas_call | solution.py:407
  79.5 0.0 collective-permute-done.3.refs_5_
  79.5 0.8 collective-permute-start.5
  80.3 0.0 collective-permute-done.4.rs0
  80.3 1.0 collective-permute-start.7
  81.3 0.0 collective-permute-done.refs_0_
  81.3 0.5 collective-permute-start.8
  81.9 0.0 collective-permute-done.2.refs_2_
  81.9 1.1 collective-permute-start.9
  83.0 31.1 %qkv_own.1.lr = bf16[3,3,2,512,256]{4,3,2,1,0:T(8,128)(2,1)} custom-call(s32[19]{0:T(128)} %stack.74.ids, bf16[512,4096]{1,0:T(8,128)(2,1)} %collective-permute-done.refs_0_, bf16[512,4096]{1,0:T(8,128)(2,1)} %norm.1.refs_1_.xn, bf16[512,4096]{1,0:T(8,128)(2,1)} %collective-permute-done.2.refs_2_, bf16[4096,3,16,256]{3,2,1,0:T(8,128)(2,1)} %refs_3_.1, ...), custom_call_target="tpu_custom_call" | custom-call | flops 1352914688 | bytes 1650000 | tf_op jit(solution)/shard_map/qkv_own/pallas_call | solution.py:384
  114.1 0.0 collective-permute-done.6.rc0
  114.1 6.6 %collective-permute-done.8.qs1 = bf16[1,2,512,256]{3,2,1,0:T(8,128)(2,1)S(1)} collective-permute-done((bf16[1,2,512,256]{3,2,1,0:T(8,128)(2,1)}, bf16[1,2,512,256]{3,2,1,0:T(8,128)(2,1)S(1)}, u32[]{:S(2)}, u32[]{:S(2)}) %collective-permute-start.8) | collective-permute-done | bytes 524320 | tf_op jit(solution)/shard_map/ppermute | solution.py:320
  120.7 5.5 %collective-permute-done.9.qc1 = bf16[1,2,512,256]{3,2,1,0:T(8,128)(2,1)} collective-permute-done((bf16[1,2,512,256]{3,2,1,0:T(8,128)(2,1)}, bf16[1,2,512,256]{3,2,1,0:T(8,128)(2,1)}, u32[]{:S(2)}, u32[]{:S(2)}) %collective-permute-start.9) | collective-permute-done | bytes 524320 | tf_op jit(solution)/shard_map/ppermute | solution.py:320
  126.2 0.0 collective-permute-done.5.rs1.qs1
  126.2 0.0 collective-permute-done.7.rc1.qc1
  126.3 1.0 copy-done.3
  127.2 21.3 %attend.2 = (bf16[512,512]{1,0:T(8,128)(2,1)}, bf16[512,512]{1,0:T(8,128)(2,1)}, bf16[512,512]{1,0:T(8,128)(2,1)}, bf16[512,512]{1,0:T(8,128)(2,1)}) custom-call(s32[19]{0:T(128)} %stack.74.ids, bf16[3,2,512,256]{3,2,1,0:T(8,128)(2,1)} %get-tuple-element.22.lo, bf16[3,3,2,512,256]{4,3,2,1,0:T(8,128)(2,1)} %qkv_own.1.lr, ...), custom_call_target="tpu_custom_call" | custom-call | flops 1000000000 | bytes 650000 | tf_op jit(solution)/shard_map/attend/pallas_call | solution.py:425
  148.5 0.1 collective-permute-start.12
  148.7 21.4 %attend.3 = (bf16[512,512]{1,0:T(8,128)(2,1)}, bf16[512,512]{1,0:T(8,128)(2,1)}, bf16[512,512]{1,0:T(8,128)(2,1)}, bf16[512,512]{1,0:T(8,128)(2,1)}) custom-call(s32[19]{0:T(128)} %stack.74.ids, bf16[3,2,512,256]{3,2,1,0:T(8,128)(2,1)} %get-tuple-element.22.lo, bf16[3,3,2,512,256]{4,3,2,1,0:T(8,128)(2,1)} %qkv_own.1.lr, ...), custom_call_target="tpu_custom_call" | custom-call | flops 1000000000 | bytes 650000 | tf_op jit(solution)/shard_map/attend/pallas_call | solution.py:425
  170.1 1.8 collective-permute-start.13
  171.9 0.0 collective-permute-start.14
  171.9 1.7 collective-permute-start.15
  173.7 0.0 collective-permute-start.16
  173.7 0.0 collective-permute-done.12.refs_1_
  173.7 2.7 %collective-permute-start.10 = (bf16[512,512]{1,0:T(8,128)(2,1)}, bf16[512,512]{1,0:T(8,128)(2,1)S(1)}, u32[]{:S(2)}, u32[]{:S(2)}) collective-permute-start(bf16[512,512]{1,0:T(8,128)(2,1)} %get-tuple-element.31), channel_id=1, source_target_pairs={{0,6},{1,7},{2,4},{3,5},{4,2},{5,3},{6,0},{7,1}} | collective-permute-start | bytes 1572872 | tf_op jit(solution)/shard_map/ppermute | solution.py:320
  176.4 8.7 %collective-permute-done.13.refs_2_ = bf16[512,512]{1,0:T(8,128)(2,1)S(1)} collective-permute-done((bf16[512,512]{1,0:T(8,128)(2,1)}, bf16[512,512]{1,0:T(8,128)(2,1)S(1)}, u32[]{:S(2)}, u32[]{:S(2)}) %collective-permute-start.13) | collective-permute-done | bytes 524320 | tf_op jit(solution)/shard_map/ppermute | solution.py:320
  185.1 1.3 collective-permute-start.11
  186.4 9.4 %collective-permute-done.14.refs_3_ = bf16[512,512]{1,0:T(8,128)(2,1)S(1)} collective-permute-done((bf16[512,512]{1,0:T(8,128)(2,1)}, bf16[512,512]{1,0:T(8,128)(2,1)S(1)}, u32[]{:S(2)}, u32[]{:S(2)}) %collective-permute-start.14) | collective-permute-done | bytes 524320 | tf_op jit(solution)/shard_map/ppermute | solution.py:320
  195.8 0.0 collective-permute-done.15.refs_4_
  195.8 23.7 %collective-permute-done.16.refs_5_ = bf16[512,512]{1,0:T(8,128)(2,1)S(1)} collective-permute-done((bf16[512,512]{1,0:T(8,128)(2,1)}, bf16[512,512]{1,0:T(8,128)(2,1)S(1)}, u32[]{:S(2)}, u32[]{:S(2)}) %collective-permute-start.16) | collective-permute-done | bytes 524320 | tf_op jit(solution)/shard_map/ppermute | solution.py:320
  219.5 17.8 %project.2.refs_4_ = f32[512,4096]{1,0:T(8,128)S(1)} custom-call(s32[19]{0:T(128)S(1)} %copy-done.1, bf16[512,512]{1,0:T(8,128)(2,1)S(1)} %copy-done, bf16[512,512]{1,0:T(8,128)(2,1)S(1)} %collective-permute-done.12.refs_1_, bf16[512,512]{1,0:T(8,128)(2,1)S(1)} %collective-permute-done.13.refs_2_, bf16[512,512]{1,0:T(8,128)(2,1)S(1)} %collective-permute-done.14.refs_3_, ...), custom_call_target="tpu_custom_call" | custom-call | flops 837518592 | bytes 1660000 | tf_op jit(solution)/shard_map/project/pallas_call | solution.py:457
  237.3 0.0 collective-permute-done.10.refs_0_
  237.3 0.0 collective-permute-done.11.refs_1_
  237.3 9.0 %project.3 = bf16[512,4096]{1,0:T(8,128)(2,1)} custom-call(s32[19]{0:T(128)S(1)} %copy-done.1, bf16[512,512]{1,0:T(8,128)(2,1)S(1)} %collective-permute-done.10.refs_0_, bf16[512,512]{1,0:T(8,128)(2,1)S(1)} %collective-permute-done.11.refs_1_, bf16[4096,4096]{1,0:T(8,128)(2,1)} %bitcast.25, bf16[4096,4096]{1,0:T(8,128)(2,1)} %bitcast.26, ...), custom_call_target="tpu_custom_call" | custom-call | flops 279172864 | bytes 820000 | tf_op jit(solution)/shard_map/project/pallas_call | solution.py:457
  (13 shorter events, 0.0 us)
Async XLA Ops:
  0.0 50.1 %collective-permute-start.1 = (bf16[512,4096]{1,0:T(8,128)(2,1)}, bf16[512,4096]{1,0:T(8,128)(2,1)}, u32[]{:S(2)}, u32[]{:S(2)}) collective-permute-start(bf16[512,4096]{1,0:T(8,128)(2,1)} %refs_12_.1), channel_id=1, source_target_pairs={{0,2},{1,5},{2,0},{3,7},{4,6},{5,1},{6,4},{7,3}} | collective-permute-start | bytes 12582920 | tf_op jit(solution)/shard_map/ppermute | solution.py:320
  47.1 10.0 %copy-start.2 = (f32[2,1024,128]{2,1,0:T(8,128)S(1)}, f32[2,1024,128]{2,1,0:T(8,128)}, u32[]{:S(2)}) copy-start(f32[2,1024,128]{2,1,0:T(8,128)} %pad_maximum_fusion.cos_ref.sin_ref.refs_4_) | copy-start | bytes 3145732
  47.1 34.2 %collective-permute-start = (bf16[512,4096]{1,0:T(8,128)(2,1)}, bf16[512,4096]{1,0:T(8,128)(2,1)}, u32[]{:S(2)}, u32[]{:S(2)}) collective-permute-start(bf16[512,4096]{1,0:T(8,128)(2,1)} %get-tuple-element.23), channel_id=1, source_target_pairs={{0,1},{1,0},{2,3},{3,2},{4,5},{5,4},{6,7},{7,6}} | collective-permute-start | bytes 12582920 | tf_op jit(solution)/shard_map/ppermute | solution.py:320
  55.1 26.7 %collective-permute-start.2 = (bf16[512,4096]{1,0:T(8,128)(2,1)}, bf16[512,4096]{1,0:T(8,128)(2,1)}, u32[]{:S(2)}, u32[]{:S(2)}) collective-permute-start(bf16[512,4096]{1,0:T(8,128)(2,1)} %norm.1.refs_1_.xn), channel_id=1, source_target_pairs={{0,1},{1,0},{2,3},{3,2},{4,5},{5,4},{6,7},{7,6}} | collective-permute-start | bytes 12582920 | tf_op jit(solution)/shard_map/ppermute | solution.py:320
  55.1 25.2 %collective-permute-start.4 = (bf16[3,2,512,256]{3,2,1,0:T(8,128)(2,1)}, bf16[3,2,512,256]{3,2,1,0:T(8,128)(2,1)}, u32[]{:S(2)}, u32[]{:S(2)}) collective-permute-start(bf16[3,2,512,256]{3,2,1,0:T(8,128)(2,1)} %get-tuple-element.24), channel_id=1, source_target_pairs={{0,4},{1,3},{2,6},{3,1},{4,0},{5,7},{6,2},{7,5}} | collective-permute-start | bytes 4718600 | tf_op jit(solution)/shard_map/ppermute | solution.py:320
  57.2 22.3 %collective-permute-start.3 = (f32[2,1024,128]{2,1,0:T(8,128)S(1)}, f32[2,1024,128]{2,1,0:T(8,128)}, u32[]{:S(2)}, u32[]{:S(2)}) collective-permute-start(f32[2,1024,128]{2,1,0:T(8,128)S(1)} %copy-done.2), channel_id=1, source_target_pairs={{0,1},{1,0},{2,3},{3,2},{4,5},{5,4},{6,7},{7,6}} | collective-permute-start | bytes 3145736 | tf_op jit(solution)/shard_map/ppermute | solution.py:320
  57.4 56.7 %collective-permute-start.6 = (bf16[3,2,512,256]{3,2,1,0:T(8,128)(2,1)}, bf16[3,2,512,256]{3,2,1,0:T(8,128)(2,1)}, u32[]{:S(2)}, u32[]{:S(2)}) collective-permute-start(bf16[3,2,512,256]{3,2,1,0:T(8,128)(2,1)} %get-tuple-element.27), channel_id=1, source_target_pairs={{0,5},{1,2},{2,7},{3,0},{4,1},{5,6},{6,3},{7,4}} | collective-permute-start | bytes 4718600 | tf_op jit(solution)/shard_map/ppermute | solution.py:320
  79.5 46.8 %collective-permute-start.5 = (bf16[2,2,512,256]{3,2,1,0:T(8,128)(2,1)}, bf16[2,2,512,256]{3,2,1,0:T(8,128)(2,1)S(1)}, u32[]{:S(2)}, u32[]{:S(2)}) collective-permute-start(bf16[2,2,512,256]{3,2,1,0:T(8,128)(2,1)} %get-tuple-element.26), channel_id=1, source_target_pairs={{0,4},{1,3},{2,6},{3,1},{4,0},{5,7},{6,2},{7,5}} | collective-permute-start | bytes 3145736 | tf_op jit(solution)/shard_map/ppermute | solution.py:320
  80.3 45.9 %collective-permute-start.7 = (bf16[2,2,512,256]{3,2,1,0:T(8,128)(2,1)}, bf16[2,2,512,256]{3,2,1,0:T(8,128)(2,1)}, u32[]{:S(2)}, u32[]{:S(2)}) collective-permute-start(bf16[2,2,512,256]{3,2,1,0:T(8,128)(2,1)} %get-tuple-element.28), channel_id=1, source_target_pairs={{0,5},{1,2},{2,7},{3,0},{4,1},{5,6},{6,3},{7,4}} | collective-permute-start | bytes 3145736 | tf_op jit(solution)/shard_map/ppermute | solution.py:320
  81.3 39.4 %collective-permute-start.8 = (bf16[1,2,512,256]{3,2,1,0:T(8,128)(2,1)}, bf16[1,2,512,256]{3,2,1,0:T(8,128)(2,1)S(1)}, u32[]{:S(2)}, u32[]{:S(2)}) collective-permute-start(bf16[1,2,512,256]{3,2,1,0:T(8,128)(2,1)} %get-tuple-element.29), channel_id=1, source_target_pairs={{0,4},{1,3},{2,6},{3,1},{4,0},{5,7},{6,2},{7,5}} | collective-permute-start | bytes 1572872 | tf_op jit(solution)/shard_map/ppermute | solution.py:320
  81.9 44.4 %collective-permute-start.9 = (bf16[1,2,512,256]{3,2,1,0:T(8,128)(2,1)}, bf16[1,2,512,256]{3,2,1,0:T(8,128)(2,1)}, u32[]{:S(2)}, u32[]{:S(2)}) collective-permute-start(bf16[1,2,512,256]{3,2,1,0:T(8,128)(2,1)} %get-tuple-element.30), channel_id=1, source_target_pairs={{0,5},{1,2},{2,7},{3,0},{4,1},{5,6},{6,3},{7,4}} | collective-permute-start | bytes 1572872 | tf_op jit(solution)/shard_map/ppermute | solution.py:320
  120.7 5.5 %copy-start.4 = (bf16[1,2,512,256]{3,2,1,0:T(8,128)(2,1)}, bf16[1,2,512,256]{3,2,1,0:T(8,128)(2,1)S(1)}, u32[]{:S(2)}) copy-start(bf16[1,2,512,256]{3,2,1,0:T(8,128)(2,1)S(1)} %collective-permute-done.8.qs1) | copy-start | bytes 1572868
  126.2 1.0 copy-start.3
  148.5 36.7 %copy-start.5 = (bf16[512,512]{1,0:T(8,128)(2,1)S(1)}, bf16[512,512]{1,0:T(8,128)(2,1)}, u32[]{:S(2)}) copy-start(bf16[512,512]{1,0:T(8,128)(2,1)} %get-tuple-element.32) | copy-start | bytes 1572868
  148.5 71.0 %copy-start = (bf16[512,512]{1,0:T(8,128)(2,1)S(1)}, bf16[512,512]{1,0:T(8,128)(2,1)}, u32[]{:S(2)}) copy-start(bf16[512,512]{1,0:T(8,128)(2,1)} %get-tuple-element.33.refs_0_) | copy-start | bytes 1572868
  148.5 71.0 %copy-start.1 = (s32[19]{0:T(128)S(1)}, s32[19]{0:T(128)}, u32[]{:S(2)}) copy-start(s32[19]{0:T(128)} %stack.74.ids) | copy-start | bytes 232
  148.5 25.2 %collective-permute-start.12 = (bf16[512,512]{1,0:T(8,128)(2,1)}, bf16[512,512]{1,0:T(8,128)(2,1)S(1)}, u32[]{:S(2)}, u32[]{:S(2)}) collective-permute-start(bf16[512,512]{1,0:T(8,128)(2,1)} %get-tuple-element.34), channel_id=1, source_target_pairs={{0,1},{1,0},{2,3},{3,2},{4,5},{5,4},{6,7},{7,6}} | collective-permute-start | bytes 1572872 | tf_op jit(solution)/shard_map/ppermute | solution.py:320
  170.1 15.0 %collective-permute-start.13 = (bf16[512,512]{1,0:T(8,128)(2,1)}, bf16[512,512]{1,0:T(8,128)(2,1)S(1)}, u32[]{:S(2)}, u32[]{:S(2)}) collective-permute-start(bf16[512,512]{1,0:T(8,128)(2,1)} %get-tuple-element.35), channel_id=1, source_target_pairs={{0,2},{1,3},{2,0},{3,1},{4,6},{5,7},{6,4},{7,5}} | collective-permute-start | bytes 1572872 | tf_op jit(solution)/shard_map/ppermute | solution.py:320
  171.9 23.9 %collective-permute-start.14 = (bf16[512,512]{1,0:T(8,128)(2,1)}, bf16[512,512]{1,0:T(8,128)(2,1)S(1)}, u32[]{:S(2)}, u32[]{:S(2)}) collective-permute-start(bf16[512,512]{1,0:T(8,128)(2,1)} %get-tuple-element.36), channel_id=1, source_target_pairs={{0,3},{1,2},{2,1},{3,0},{4,7},{5,6},{6,5},{7,4}} | collective-permute-start | bytes 1572872 | tf_op jit(solution)/shard_map/ppermute | solution.py:320
  171.9 23.9 %collective-permute-start.15 = (bf16[512,512]{1,0:T(8,128)(2,1)}, bf16[512,512]{1,0:T(8,128)(2,1)S(1)}, u32[]{:S(2)}, u32[]{:S(2)}) collective-permute-start(bf16[512,512]{1,0:T(8,128)(2,1)} %get-tuple-element.37), channel_id=1, source_target_pairs={{0,4},{1,5},{2,6},{3,7},{4,0},{5,1},{6,2},{7,3}} | collective-permute-start | bytes 1572872 | tf_op jit(solution)/shard_map/ppermute | solution.py:320
  173.7 45.8 %collective-permute-start.16 = (bf16[512,512]{1,0:T(8,128)(2,1)}, bf16[512,512]{1,0:T(8,128)(2,1)S(1)}, u32[]{:S(2)}, u32[]{:S(2)}) collective-permute-start(bf16[512,512]{1,0:T(8,128)(2,1)} %get-tuple-element.38), channel_id=1, source_target_pairs={{0,5},{1,4},{2,7},{3,6},{4,1},{5,0},{6,3},{7,2}} | collective-permute-start | bytes 1572872 | tf_op jit(solution)/shard_map/ppermute | solution.py:320
  173.7 63.6 %collective-permute-start.10 = (bf16[512,512]{1,0:T(8,128)(2,1)}, bf16[512,512]{1,0:T(8,128)(2,1)S(1)}, u32[]{:S(2)}, u32[]{:S(2)}) collective-permute-start(bf16[512,512]{1,0:T(8,128)(2,1)} %get-tuple-element.31), channel_id=1, source_target_pairs={{0,6},{1,7},{2,4},{3,5},{4,2},{5,3},{6,0},{7,1}} | collective-permute-start | bytes 1572872 | tf_op jit(solution)/shard_map/ppermute | solution.py:320
  185.1 52.2 %collective-permute-start.11 = (bf16[512,512]{1,0:T(8,128)(2,1)S(1)}, bf16[512,512]{1,0:T(8,128)(2,1)S(1)}, u32[]{:S(2)}, u32[]{:S(2)}) collective-permute-start(bf16[512,512]{1,0:T(8,128)(2,1)S(1)} %copy-done.5), channel_id=1, source_target_pairs={{0,7},{1,6},{2,5},{3,4},{4,3},{5,2},{6,1},{7,0}} | collective-permute-start | bytes 1572872 | tf_op jit(solution)/shard_map/ppermute | solution.py:320

commit v5 on v4

--- a/solution.py
+++ b/solution.py
@@ -11,7 +11,9 @@
 BF = jnp.bfloat16
 F32 = jnp.float32
 VMEM_LIMIT = 62 << 20
-PROJ_VMEM = 40 << 20
+PROJ_VMEM = KEEP_VMEM = 40 << 20
+ATT_VMEM = 50 << 20
+OWN_VMEM = 48 << 20
 COST = 0.05
 TN0, TN1 = 1024, 1024
 GROUPS = ((2, 4), (6, 0))
@@ -37,8 +39,10 @@
     lax.fori_loop(0, x_ref.shape[0] // rb, body, 0, unroll=8)
 
 
-def _norm_rows(x_ref, g_ref, o_ref):
+def _norm_rows(x_ref, g_ref, o_ref, keep):
+    rb = x_ref.shape[0]
     _norm(x_ref, g_ref, o_ref)
+    keep[pl.ds(pl.multiple_of(pl.program_id(0) * rb, rb), rb), :] = o_ref[...]
 
 
 def _emit_heads(acc, cos, sin, is_v, outs):
@@ -391,31 +395,33 @@
                                     pltpu.VMEM((2048, 2 * dh), BF), pltpu.SemaphoreType.DMA((2, n))]
                     + [pltpu.VMEM((2, 2048, 2, dh), BF), pltpu.SemaphoreType.DMA((2,))]),
                 out_shape=jax.ShapeDtypeStruct((n, 3, 2, t, dh), BF),
-                compiler_params=_params(), cost_estimate=_cost(flops * 0.7 * n, 15e6 + n * 6e6), name="qkv_own",
+                compiler_params=_params(OWN_VMEM), cost_estimate=_cost(flops * 0.7 * n, 15e6 + n * 6e6), name="qkv_own",
             )(ids, *xs, wqkv, tab, ptab)
 
         rs_own, rc_own = send(b_same, to_same), send(b_cross, to_cross)
         xn_po, ptab = partner(xn_o), partner(tab)
         rb = 256
-        xn_a = pl.pallas_call(
+        kept = pl.BlockSpec(memory_space=pltpu.VMEM)
+        xn_a, xn_k = pl.pallas_call(
             _norm_rows, grid=(t // rb,),
             in_specs=[pl.BlockSpec((rb, d), lambda i: (i, 0)), pl.BlockSpec((1, d), lambda i: (0, 0))],
-            out_specs=pl.BlockSpec((rb, d), lambda i: (i, 0)), out_shape=xn_shape,
-            compiler_params=_params(), cost_estimate=_cost(2e9, 8e6), name="norm",
+            out_specs=[pl.BlockSpec((rb, d), lambda i: (i, 0)), kept],
+            out_shape=[xn_shape, pltpu.VMEM((t, d), BF)],
+            compiler_params=_params(KEEP_VMEM), cost_estimate=_cost(2e9, 8e6), name="norm",
         )(xa, g2)
         xn_pa = partner(xn_a)
         q_same, q_cross, a_same, a_cross = pl.pallas_call(
             _qkv_next,
             grid_spec=pltpu.PrefetchScalarGridSpec(
                 num_scalar_prefetch=1, grid=(3, 2),
-                in_specs=[whole, pl.BlockSpec((1, d, 2 * dh), lambda c, i, s: (c, 0, (i + s[ME]) % 2)),
+                in_specs=[kept, pl.BlockSpec((1, d, 2 * dh), lambda c, i, s: (c, 0, (i + s[ME]) % 2)),
                           tab_spec(0, 1), tab_spec(1, 1)],
                 out_specs=[pl.BlockSpec((1, 2, t, dh), lambda *_: (0, 0, 0, 0))] * 2
                 + [pl.BlockSpec((1, 2, t, dh), lambda c, *_: (jnp.maximum(c - 1, 0), 0, 0, 0))] * 2,
                 scratch_shapes=[pltpu.VMEM((t, 2 * dh), F32)]),
             out_shape=[jax.ShapeDtypeStruct((n, 2, t, dh), BF) for n in (1, 1, 2, 2)],
-            compiler_params=_params(), cost_estimate=_cost(flops * 1.4, 35e6), name="qkv_next",
-        )(ids, xn_a, w_b, tab, tab)
+            compiler_params=_params(KEEP_VMEM), cost_estimate=_cost(flops * 1.4, 35e6), name="qkv_next",
+        )(ids, xn_k, w_b, tab, tab)
         rs_a, rc_a = send(a_same, to_same), send(a_cross, to_cross)
         rs_q, rc_q = send(q_same, to_same), send(q_cross, to_cross)
         loc_r = own((xn_po, xn_a, xn_pa), ((1, 0), (0, 1), (1, 1)), ptab)
@@ -427,12 +433,14 @@
                 grid_spec=pltpu.PrefetchScalarGridSpec(
                     num_scalar_prefetch=1, grid=(1,),
                     in_specs=[anyspec] * 8,
-                    out_specs=[pl.BlockSpec((t, 2 * dh), lambda i, s: (0, 0))] * (2 * nq),
+                    out_specs=[kept if m == 0 and e == 0 else pl.BlockSpec((t, 2 * dh), lambda i, s: (0, 0))
+                               for m in ms for e in range(2)],
                     scratch_shapes=[pltpu.VMEM((3, 2, 8 * t, dh), BF),
                                     pltpu.VMEM((2, 2 * t, 128), F32), pltpu.VMEM((2, 2 * t, 128), F32),
                                     pltpu.VMEM((2, 2 * t, dh), F32), pltpu.SemaphoreType.DMA((2, 8))]),
-                out_shape=[jax.ShapeDtypeStruct((t, 2 * dh), BF)] * (2 * nq),
-                compiler_params=_params(), cost_estimate=_cost(nq * 10e9, 13e6), name="attend",
+                out_shape=[(pltpu.VMEM if m == 0 and e == 0 else jax.ShapeDtypeStruct)((t, 2 * dh), BF)
+                           for m in ms for e in range(2)],
+                compiler_params=_params(ATT_VMEM), cost_estimate=_cost(nq * 10e9, 13e6), name="attend",
             )(ids, loc_o, loc_r, rs_own, rs_a, rc_own, rc_a, *((rs_q, rc_q) if 6 in ms else (rs_a, rc_a)))
 
         got = {}
@@ -453,12 +461,11 @@
                 return pl.BlockSpec((2 * dh, tn), lambda i, s: (s[DEV + m], i))
 
             col = pl.BlockSpec((t, tn), lambda i, s: (0, i))
-            kept = pl.BlockSpec(memory_space=pltpu.VMEM)
             return pl.pallas_call(
                 functools.partial(_project, n),
                 grid_spec=pltpu.PrefetchScalarGridSpec(
                     num_scalar_prefetch=1, grid=(d // tn,),
-                    in_specs=[o_spec] * n + [w_spec(m) for m in ms] + [col if part is None else kept],
+                    in_specs=[o_spec if m else kept for m in ms] + [w_spec(m) for m in ms] + [col if part is None else kept],
                     out_specs=kept if part is None else col),
                 out_shape=pltpu.VMEM((t, d), F32) if part is None else jax.ShapeDtypeStruct((t, d), BF),
                 compiler_params=_params(PROJ_VMEM), cost_estimate=_cost(n * 2 * t * 2 * dh * d * 1.3, n * 4.2e6 + 8e6),

time: 247 us -> 243 us (0.984)
  Pallas kernels: 167 us -> 158 us
  local copies, waits for them, and re-layouts: 1.59 us -> 5.24 us
  waiting for transfers between devices: 56.9 us -> 59.4 us
    unnamed x13 -> x23, local copies, waits for them, and re-layouts: 0.98 us -> 4.56 us
    pallas_call x2, Pallas kernels: 42.7 us -> 39.4 us  [attend(): pl.pallas_call(functools.partial(_attend, ms), grid_spec=pltpu.PrefetchSc...]
    pallas_call x1, Pallas kernels: 21 us -> 18 us  [local(): pl.pallas_call(_qkv_next, grid_spec=pltpu.PrefetchScalarGridSpec(num_scal...]
    ppermute x17, waiting for transfers between devices: 56.9 us -> 59.4 us  [send(): return lax.ppermute(a, 'seq', [(i, f(i)) for i in range(8)])]
  transfers between devices with their start and end apart: 17 -> 17, of which waited for: 6 -> 6; matrix products, arithmetic and copies ran while one was open for 2% -> 2% of each run, Pallas kernels for 55% -> 53%
where the time goes in v5:
time: 243 us
  Pallas kernels  158 us (65%)
  waiting for transfers between devices  59.4 us (24%)
  starting transfers between devices  17.4 us (7%)
  local copies, waits for them, and re-layouts  5.24 us (2%)
  other arithmetic  3.08 us (1%)
    ppermute x17, waiting for transfers between devices, send(): return lax.ppermute(a, 'seq', [(i, f(i)) for i in range(8)])  59.4 us
    pallas_call x1, Pallas kernels, local(): pl.pallas_call(_qkv_first, grid_spec=pltpu.PrefetchScalarGridSpec(num_sca...  40.2 us
    pallas_call x2, Pallas kernels, attend(): pl.pallas_call(functools.partial(_attend, ms), grid_spec=pltpu.PrefetchSc...  39.4 us
    pallas_call x1, Pallas kernels, own(): pl.pallas_call(functools.partial(_qkv_own, halves), grid_spec=pltpu.Prefe...  29.4 us
    pallas_call x2, Pallas kernels, project(): pl.pallas_call(functools.partial(_project, n), grid_spec=pltpu.PrefetchSc...  26.8 us
    pallas_call x1, Pallas kernels, local(): pl.pallas_call(_qkv_next, grid_spec=pltpu.PrefetchScalarGridSpec(num_scal...  18 us
    ppermute x17, starting transfers between devices, send(): return lax.ppermute(a, 'seq', [(i, f(i)) for i in range(8)])  17.4 us
  transfers between devices with their start and end apart: 17, of which 6 were waited for; matrix products, arithmetic and copies ran while one was open for 2% of the time, Pallas kernels for 53%

profile of v5, /device:TPU:0, one launch (start us, length us, event | category | flops | bytes accessed | tf_op | source)
XLA Modules:
  0.0 243.2 jit_solution(3378124430868941303)
XLA Ops:
  0.0 3.3 %collective-permute-start.1 = (bf16[512,4096]{1,0:T(8,128)(2,1)}, bf16[512,4096]{1,0:T(8,128)(2,1)}, u32[]{:S(2)}, u32[]{:S(2)}) collective-permute-start(bf16[512,4096]{1,0:T(8,128)(2,1)} %refs_12_.1), channel_id=1, source_target_pairs={{0,2},{1,5},{2,0},{3,7},{4,6},{5,1},{6,4},{7,3}} | collective-permute-start | bytes 12582920 | tf_op jit(solution)/shard_map/ppermute | solution.py:324
  3.3 0.1 add_multiply_fusion
  3.4 0.1 convert_bitcast_fusion
  3.5 0.7 stack.74.ids
  4.2 1.9 multiply_cosine_fusion
  6.1 1.0 pad_maximum_fusion.cos_ref.sin_ref.refs_4_
  7.1 40.2 %qkv_first.1 = (bf16[3,2,512,256]{3,2,1,0:T(8,128)(2,1)}, bf16[3,2,512,256]{3,2,1,0:T(8,128)(2,1)}, bf16[3,2,512,256]{3,2,1,0:T(8,128)(2,1)}, bf16[3,4096,1024]{2,1,0:T(8,128)(2,1)}, bf16[512,4096]{1,0:T(8,128)(2,1)}) custom-call(s32[19]{0:T(128)} %stack.74.ids, bf16[512,4096]{1,0:T(8,128)(2,1)} %refs_12_.1, f32[1,4096]{1,0:T(1,128)} %bitcast.19, ...), custom_call_target="tpu_custom_call" | custom-call | flops 1610612736 | bytes 4000000 | tf_op jit(solution)/shard_map/qkv_first/pallas_call | solution.py:372
  47.4 0.0 collective-permute-start
  47.4 2.7 %collective-permute-done.1.x_ref = bf16[512,4096]{1,0:T(8,128)(2,1)} collective-permute-done((bf16[512,4096]{1,0:T(8,128)(2,1)}, bf16[512,4096]{1,0:T(8,128)(2,1)}, u32[]{:S(2)}, u32[]{:S(2)}) %collective-permute-start.1) | collective-permute-done | bytes 4194336 | tf_op jit(solution)/shard_map/ppermute | solution.py:324
  50.1 3.9 %norm.1 = (bf16[512,4096]{1,0:T(8,128)(2,1)S(1)}, bf16[512,4096]{1,0:T(8,128)(2,1)S(1)}) custom-call(bf16[512,4096]{1,0:T(8,128)(2,1)} %collective-permute-done.1.x_ref, f32[1,4096]{1,0:T(1,128)S(1)} %bitcast.20), custom_call_target="tpu_custom_call" | custom-call | flops 100000000 | bytes 400000 | tf_op jit(solution)/shard_map/norm/pallas_call | solution.py:405
  54.0 0.0 collective-permute-start.2
  54.1 2.1 collective-permute-start.4
  56.2 0.2 collective-permute-start.3
  56.3 1.2 collective-permute-start.6
  57.5 18.0 %qkv_next.1 = (bf16[1,2,512,256]{3,2,1,0:T(8,128)(2,1)S(1)}, bf16[1,2,512,256]{3,2,1,0:T(8,128)(2,1)S(1)}, bf16[2,2,512,256]{3,2,1,0:T(8,128)(2,1)S(1)}, bf16[2,2,512,256]{3,2,1,0:T(8,128)(2,1)S(1)}) custom-call(s32[19]{0:T(128)S(1)} %copy-done.5, bf16[512,4096]{1,0:T(8,128)(2,1)S(1)} %get-tuple-element.28.xn, ...), custom_call_target="tpu_custom_call" | custom-call | flops 901943104 | bytes 1750000 | tf_op jit(solution)/shard_map/qkv_next/pallas_call | solution.py:413
  75.5 0.0 collective-permute-done.3.refs_5_
  75.5 0.8 collective-permute-start.5
  76.4 0.0 collective-permute-done.4.rs0
  76.4 1.0 collective-permute-start.7
  77.4 0.0 collective-permute-done.refs_0_
  77.4 0.5 collective-permute-start.8
  77.9 0.0 collective-permute-done.2.refs_2_
  77.9 2.0 copy-done.8
  79.9 1.2 collective-permute-start.9
  81.1 29.4 %qkv_own.1.lr = bf16[3,3,2,512,256]{4,3,2,1,0:T(8,128)(2,1)} custom-call(s32[19]{0:T(128)S(1)} %copy-done.5, bf16[512,4096]{1,0:T(8,128)(2,1)} %collective-permute-done.refs_0_, bf16[512,4096]{1,0:T(8,128)(2,1)} %copy-done.3, bf16[512,4096]{1,0:T(8,128)(2,1)} %copy-done.8, bf16[4096,3,16,256]{3,2,1,0:T(8,128)(2,1)} %refs_3_.1, f32[2,1024,128]{2,1,0:T(8,128)S(1)} %copy-done, ...), custom_call_target="tpu_custom_call" | custom-call | flops 1352914688 | bytes 1650000 | tf_op jit(solution)/shard_map/qkv_own/pallas_call | solution.py:388
  110.5 0.0 collective-permute-done.6.rc0
  110.5 9.0 %collective-permute-done.8.qs1 = bf16[1,2,512,256]{3,2,1,0:T(8,128)(2,1)S(1)} collective-permute-done((bf16[1,2,512,256]{3,2,1,0:T(8,128)(2,1)S(1)}, bf16[1,2,512,256]{3,2,1,0:T(8,128)(2,1)S(1)}, u32[]{:S(2)}, u32[]{:S(2)}) %collective-permute-start.8) | collective-permute-done | bytes 524320 | tf_op jit(solution)/shard_map/ppermute | solution.py:324
  119.5 5.4 %collective-permute-done.9.qc1 = bf16[1,2,512,256]{3,2,1,0:T(8,128)(2,1)S(1)} collective-permute-done((bf16[1,2,512,256]{3,2,1,0:T(8,128)(2,1)S(1)}, bf16[1,2,512,256]{3,2,1,0:T(8,128)(2,1)S(1)}, u32[]{:S(2)}, u32[]{:S(2)}) %collective-permute-start.9) | collective-permute-done | bytes 524320 | tf_op jit(solution)/shard_map/ppermute | solution.py:324
  124.9 0.0 collective-permute-done.5.rs1.qs1
  124.9 1.0 copy-done.1
  125.8 0.3 copy-done.6
  126.2 19.6 %attend.2 = (bf16[512,512]{1,0:T(8,128)(2,1)S(1)}, bf16[512,512]{1,0:T(8,128)(2,1)S(1)}, bf16[512,512]{1,0:T(8,128)(2,1)S(1)}, bf16[512,512]{1,0:T(8,128)(2,1)S(1)}) custom-call(s32[19]{0:T(128)S(1)} %copy-done.5, bf16[3,2,512,256]{3,2,1,0:T(8,128)(2,1)} %get-tuple-element.24.lo, bf16[3,3,2,512,256]{4,3,2,1,0:T(8,128)(2,1)} %qkv_own.1.lr, ...), custom_call_target="tpu_custom_call" | custom-call | flops 1000000000 | bytes 650000 | tf_op jit(solution)/shard_map/attend/pallas_call | solution.py:431
  145.8 0.1 collective-permute-start.12
  145.9 1.2 copy-done.2
  147.1 19.8 %attend.3 = (bf16[512,512]{1,0:T(8,128)(2,1)S(1)}, bf16[512,512]{1,0:T(8,128)(2,1)S(1)}, bf16[512,512]{1,0:T(8,128)(2,1)S(1)}, bf16[512,512]{1,0:T(8,128)(2,1)S(1)}) custom-call(s32[19]{0:T(128)S(1)} %copy-done.5, bf16[3,2,512,256]{3,2,1,0:T(8,128)(2,1)} %get-tuple-element.24.lo, bf16[3,3,2,512,256]{4,3,2,1,0:T(8,128)(2,1)} %qkv_own.1.lr, ...), custom_call_target="tpu_custom_call" | custom-call | flops 1000000000 | bytes 650000 | tf_op jit(solution)/shard_map/attend/pallas_call | solution.py:431
  166.9 2.0 collective-permute-start.13
  169.0 0.0 collective-permute-start.14
  169.0 1.6 collective-permute-start.15
  170.5 0.2 collective-permute-start.16
  170.7 0.0 collective-permute-done.12.refs_1_
  170.7 2.4 collective-permute-start.10
  173.1 8.6 %collective-permute-done.13.refs_2_ = bf16[512,512]{1,0:T(8,128)(2,1)S(1)} collective-permute-done((bf16[512,512]{1,0:T(8,128)(2,1)S(1)}, bf16[512,512]{1,0:T(8,128)(2,1)S(1)}, u32[]{:S(2)}, u32[]{:S(2)}) %collective-permute-start.13) | collective-permute-done | bytes 524320 | tf_op jit(solution)/shard_map/ppermute | solution.py:324
  181.8 0.8 collective-permute-start.11
  182.6 9.9 %collective-permute-done.14.refs_3_ = bf16[512,512]{1,0:T(8,128)(2,1)S(1)} collective-permute-done((bf16[512,512]{1,0:T(8,128)(2,1)S(1)}, bf16[512,512]{1,0:T(8,128)(2,1)S(1)}, u32[]{:S(2)}, u32[]{:S(2)}) %collective-permute-start.14) | collective-permute-done | bytes 524320 | tf_op jit(solution)/shard_map/ppermute | solution.py:324
  192.5 23.8 %collective-permute-done.16.refs_5_ = bf16[512,512]{1,0:T(8,128)(2,1)S(1)} collective-permute-done((bf16[512,512]{1,0:T(8,128)(2,1)S(1)}, bf16[512,512]{1,0:T(8,128)(2,1)S(1)}, u32[]{:S(2)}, u32[]{:S(2)}) %collective-permute-start.16) | collective-permute-done | bytes 524320 | tf_op jit(solution)/shard_map/ppermute | solution.py:324
  216.3 17.8 %project.2.refs_4_ = f32[512,4096]{1,0:T(8,128)S(1)} custom-call(s32[19]{0:T(128)S(1)} %copy-done.5, bf16[512,512]{1,0:T(8,128)(2,1)S(1)} %get-tuple-element.37.refs_0_, bf16[512,512]{1,0:T(8,128)(2,1)S(1)} %collective-permute-done.12.refs_1_, bf16[512,512]{1,0:T(8,128)(2,1)S(1)} %collective-permute-done.13.refs_2_, ...), custom_call_target="tpu_custom_call" | custom-call | flops 837518592 | bytes 1660000 | tf_op jit(solution)/shard_map/project/pallas_call | solution.py:464
  234.2 0.0 collective-permute-done.11.refs_1_
  234.2 9.0 %project.3 = bf16[512,4096]{1,0:T(8,128)(2,1)} custom-call(s32[19]{0:T(128)S(1)} %copy-done.5, bf16[512,512]{1,0:T(8,128)(2,1)S(1)} %collective-permute-done.10.refs_0_, bf16[512,512]{1,0:T(8,128)(2,1)S(1)} %collective-permute-done.11.refs_1_, bf16[4096,4096]{1,0:T(8,128)(2,1)} %bitcast.27, bf16[4096,4096]{1,0:T(8,128)(2,1)} %bitcast.28, ...), custom_call_target="tpu_custom_call" | custom-call | flops 279172864 | bytes 820000 | tf_op jit(solution)/shard_map/project/pallas_call | solution.py:464
  (23 shorter events, 0.1 us)
Async XLA Ops:
  0.0 50.1 %collective-permute-start.1 = (bf16[512,4096]{1,0:T(8,128)(2,1)}, bf16[512,4096]{1,0:T(8,128)(2,1)}, u32[]{:S(2)}, u32[]{:S(2)}) collective-permute-start(bf16[512,4096]{1,0:T(8,128)(2,1)} %refs_12_.1), channel_id=1, source_target_pairs={{0,2},{1,5},{2,0},{3,7},{4,6},{5,1},{6,4},{7,3}} | collective-permute-start | bytes 12582920 | tf_op jit(solution)/shard_map/ppermute | solution.py:324
  7.1 43.0 %copy-start.4 = (f32[4096]{0:T(1024)S(1)}, f32[4096]{0:T(1024)}, u32[]{:S(2)}) copy-start(f32[4096]{0:T(1024)} %param.5) | copy-start | bytes 49156
  47.3 6.8 %copy-start.10 = (bf16[3,2,512,256]{3,2,1,0:T(8,128)(2,1)S(1)}, bf16[3,2,512,256]{3,2,1,0:T(8,128)(2,1)}, u32[]{:S(2)}) copy-start(bf16[3,2,512,256]{3,2,1,0:T(8,128)(2,1)} %get-tuple-element.27) | copy-start | bytes 4718596
  47.3 8.8 %copy-start = (f32[2,1024,128]{2,1,0:T(8,128)S(1)}, f32[2,1024,128]{2,1,0:T(8,128)}, u32[]{:S(2)}) copy-start(f32[2,1024,128]{2,1,0:T(8,128)} %pad_maximum_fusion.cos_ref.sin_ref.refs_4_) | copy-start | bytes 3145732
  47.3 9.0 %copy-start.9 = (bf16[3,2,512,256]{3,2,1,0:T(8,128)(2,1)S(1)}, bf16[3,2,512,256]{3,2,1,0:T(8,128)(2,1)}, u32[]{:S(2)}) copy-start(bf16[3,2,512,256]{3,2,1,0:T(8,128)(2,1)} %get-tuple-element.31) | copy-start | bytes 4718596
  47.4 10.1 %copy-start.5 = (s32[19]{0:T(128)S(1)}, s32[19]{0:T(128)}, u32[]{:S(2)}) copy-start(s32[19]{0:T(128)} %stack.74.ids) | copy-start | bytes 232
  47.4 30.0 %collective-permute-start = (bf16[512,4096]{1,0:T(8,128)(2,1)}, bf16[512,4096]{1,0:T(8,128)(2,1)}, u32[]{:S(2)}, u32[]{:S(2)}) collective-permute-start(bf16[512,4096]{1,0:T(8,128)(2,1)} %get-tuple-element.25), channel_id=1, source_target_pairs={{0,1},{1,0},{2,3},{3,2},{4,5},{5,4},{6,7},{7,6}} | collective-permute-start | bytes 12582920 | tf_op jit(solution)/shard_map/ppermute | solution.py:324
  54.0 21.5 %copy-start.3 = (bf16[512,4096]{1,0:T(8,128)(2,1)}, bf16[512,4096]{1,0:T(8,128)(2,1)S(1)}, u32[]{:S(2)}) copy-start(bf16[512,4096]{1,0:T(8,128)(2,1)S(1)} %get-tuple-element.26.refs_1_) | copy-start | bytes 12582916
  54.0 23.8 %collective-permute-start.2 = (bf16[512,4096]{1,0:T(8,128)(2,1)S(1)}, bf16[512,4096]{1,0:T(8,128)(2,1)S(1)}, u32[]{:S(2)}, u32[]{:S(2)}) collective-permute-start(bf16[512,4096]{1,0:T(8,128)(2,1)S(1)} %get-tuple-element.26.refs_1_), channel_id=1, source_target_pairs={{0,1},{1,0},{2,3},{3,2},{4,5},{5,4},{6,7},{7,6}} | collective-permute-start | bytes 12582920 | tf_op jit(solution)/shard_map/ppermute | solution.py:324
  54.1 22.3 %collective-permute-start.4 = (bf16[3,2,512,256]{3,2,1,0:T(8,128)(2,1)S(1)}, bf16[3,2,512,256]{3,2,1,0:T(8,128)(2,1)S(1)}, u32[]{:S(2)}, u32[]{:S(2)}) collective-permute-start(bf16[3,2,512,256]{3,2,1,0:T(8,128)(2,1)S(1)} %copy-done.10), channel_id=1, source_target_pairs={{0,4},{1,3},{2,6},{3,1},{4,0},{5,7},{6,2},{7,5}} | collective-permute-start | bytes 4718600 | tf_op jit(solution)/shard_map/ppermute | solution.py:324
  56.2 19.3 %collective-permute-start.3 = (f32[2,1024,128]{2,1,0:T(8,128)S(1)}, f32[2,1024,128]{2,1,0:T(8,128)S(1)}, u32[]{:S(2)}, u32[]{:S(2)}) collective-permute-start(f32[2,1024,128]{2,1,0:T(8,128)S(1)} %copy-done), channel_id=1, source_target_pairs={{0,1},{1,0},{2,3},{3,2},{4,5},{5,4},{6,7},{7,6}} | collective-permute-start | bytes 3145736 | tf_op jit(solution)/shard_map/ppermute | solution.py:324
  56.3 54.2 %collective-permute-start.6 = (bf16[3,2,512,256]{3,2,1,0:T(8,128)(2,1)S(1)}, bf16[3,2,512,256]{3,2,1,0:T(8,128)(2,1)}, u32[]{:S(2)}, u32[]{:S(2)}) collective-permute-start(bf16[3,2,512,256]{3,2,1,0:T(8,128)(2,1)S(1)} %copy-done.9), channel_id=1, source_target_pairs={{0,5},{1,2},{2,7},{3,0},{4,1},{5,6},{6,3},{7,4}} | collective-permute-start | bytes 4718600 | tf_op jit(solution)/shard_map/ppermute | solution.py:324
  75.5 49.4 %collective-permute-start.5 = (bf16[2,2,512,256]{3,2,1,0:T(8,128)(2,1)S(1)}, bf16[2,2,512,256]{3,2,1,0:T(8,128)(2,1)S(1)}, u32[]{:S(2)}, u32[]{:S(2)}) collective-permute-start(bf16[2,2,512,256]{3,2,1,0:T(8,128)(2,1)S(1)} %get-tuple-element.30), channel_id=1, source_target_pairs={{0,4},{1,3},{2,6},{3,1},{4,0},{5,7},{6,2},{7,5}} | collective-permute-start | bytes 3145736 | tf_op jit(solution)/shard_map/ppermute | solution.py:324
  76.4 1.5 copy-start.7
  76.4 48.5 %collective-permute-start.7 = (bf16[2,2,512,256]{3,2,1,0:T(8,128)(2,1)S(1)}, bf16[2,2,512,256]{3,2,1,0:T(8,128)(2,1)S(1)}, u32[]{:S(2)}, u32[]{:S(2)}) collective-permute-start(bf16[2,2,512,256]{3,2,1,0:T(8,128)(2,1)S(1)} %get-tuple-element.32), channel_id=1, source_target_pairs={{0,5},{1,2},{2,7},{3,0},{4,1},{5,6},{6,3},{7,4}} | collective-permute-start | bytes 3145736 | tf_op jit(solution)/shard_map/ppermute | solution.py:324
  77.4 42.1 %collective-permute-start.8 = (bf16[1,2,512,256]{3,2,1,0:T(8,128)(2,1)S(1)}, bf16[1,2,512,256]{3,2,1,0:T(8,128)(2,1)S(1)}, u32[]{:S(2)}, u32[]{:S(2)}) collective-permute-start(bf16[1,2,512,256]{3,2,1,0:T(8,128)(2,1)S(1)} %get-tuple-element.33), channel_id=1, source_target_pairs={{0,4},{1,3},{2,6},{3,1},{4,0},{5,7},{6,2},{7,5}} | collective-permute-start | bytes 1572872 | tf_op jit(solution)/shard_map/ppermute | solution.py:324
  77.9 2.0 copy-start.8
  79.9 45.0 %collective-permute-start.9 = (bf16[1,2,512,256]{3,2,1,0:T(8,128)(2,1)S(1)}, bf16[1,2,512,256]{3,2,1,0:T(8,128)(2,1)S(1)}, u32[]{:S(2)}, u32[]{:S(2)}) collective-permute-start(bf16[1,2,512,256]{3,2,1,0:T(8,128)(2,1)S(1)} %get-tuple-element.34), channel_id=1, source_target_pairs={{0,5},{1,2},{2,7},{3,0},{4,1},{5,6},{6,3},{7,4}} | collective-permute-start | bytes 1572872 | tf_op jit(solution)/shard_map/ppermute | solution.py:324
  124.9 1.0 copy-start.1
  124.9 1.3 copy-start.6
  145.8 24.9 %collective-permute-start.12 = (bf16[512,512]{1,0:T(8,128)(2,1)S(1)}, bf16[512,512]{1,0:T(8,128)(2,1)S(1)}, u32[]{:S(2)}, u32[]{:S(2)}) collective-permute-start(bf16[512,512]{1,0:T(8,128)(2,1)S(1)} %get-tuple-element.38), channel_id=1, source_target_pairs={{0,1},{1,0},{2,3},{3,2},{4,5},{5,4},{6,7},{7,6}} | collective-permute-start | bytes 1572872 | tf_op jit(solution)/shard_map/ppermute | solution.py:324
  145.9 1.2 copy-start.2
  166.9 14.8 %collective-permute-start.13 = (bf16[512,512]{1,0:T(8,128)(2,1)S(1)}, bf16[512,512]{1,0:T(8,128)(2,1)S(1)}, u32[]{:S(2)}, u32[]{:S(2)}) collective-permute-start(bf16[512,512]{1,0:T(8,128)(2,1)S(1)} %get-tuple-element.39), channel_id=1, source_target_pairs={{0,2},{1,3},{2,0},{3,1},{4,6},{5,7},{6,4},{7,5}} | collective-permute-start | bytes 1572872 | tf_op jit(solution)/shard_map/ppermute | solution.py:324
  169.0 23.6 %collective-permute-start.14 = (bf16[512,512]{1,0:T(8,128)(2,1)S(1)}, bf16[512,512]{1,0:T(8,128)(2,1)S(1)}, u32[]{:S(2)}, u32[]{:S(2)}) collective-permute-start(bf16[512,512]{1,0:T(8,128)(2,1)S(1)} %get-tuple-element.40), channel_id=1, source_target_pairs={{0,3},{1,2},{2,1},{3,0},{4,7},{5,6},{6,5},{7,4}} | collective-permute-start | bytes 1572872 | tf_op jit(solution)/shard_map/ppermute | solution.py:324
  169.0 23.6 %collective-permute-start.15 = (bf16[512,512]{1,0:T(8,128)(2,1)S(1)}, bf16[512,512]{1,0:T(8,128)(2,1)S(1)}, u32[]{:S(2)}, u32[]{:S(2)}) collective-permute-start(bf16[512,512]{1,0:T(8,128)(2,1)S(1)} %get-tuple-element.41), channel_id=1, source_target_pairs={{0,4},{1,5},{2,6},{3,7},{4,0},{5,1},{6,2},{7,3}} | collective-permute-start | bytes 1572872 | tf_op jit(solution)/shard_map/ppermute | solution.py:324
  170.5 45.8 %collective-permute-start.16 = (bf16[512,512]{1,0:T(8,128)(2,1)S(1)}, bf16[512,512]{1,0:T(8,128)(2,1)S(1)}, u32[]{:S(2)}, u32[]{:S(2)}) collective-permute-start(bf16[512,512]{1,0:T(8,128)(2,1)S(1)} %get-tuple-element.42), channel_id=1, source_target_pairs={{0,5},{1,4},{2,7},{3,6},{4,1},{5,0},{6,3},{7,2}} | collective-permute-start | bytes 1572872 | tf_op jit(solution)/shard_map/ppermute | solution.py:324
  170.7 63.5 %collective-permute-start.10 = (bf16[512,512]{1,0:T(8,128)(2,1)S(1)}, bf16[512,512]{1,0:T(8,128)(2,1)S(1)}, u32[]{:S(2)}, u32[]{:S(2)}) collective-permute-start(bf16[512,512]{1,0:T(8,128)(2,1)S(1)} %get-tuple-element.35), channel_id=1, source_target_pairs={{0,6},{1,7},{2,4},{3,5},{4,2},{5,3},{6,0},{7,1}} | collective-permute-start | bytes 1572872 | tf_op jit(solution)/shard_map/ppermute | solution.py:324
  181.8 52.4 %collective-permute-start.11 = (bf16[512,512]{1,0:T(8,128)(2,1)S(1)}, bf16[512,512]{1,0:T(8,128)(2,1)S(1)}, u32[]{:S(2)}, u32[]{:S(2)}) collective-permute-start(bf16[512,512]{1,0:T(8,128)(2,1)S(1)} %get-tuple-element.36), channel_id=1, source_target_pairs={{0,7},{1,6},{2,5},{3,4},{4,3},{5,2},{6,1},{7,0}} | collective-permute-start | bytes 1572872 | tf_op jit(solution)/shard_map/ppermute | solution.py:324
